TPU v7x, 32 devices: a whole 2x2x4 slice. The times are simulated.
32 devices in a mesh: seq: 4 (over y, x), sample: 2 (over core), head: 4 (over z).
Axes of the slice: x: 2, y: 2, z: 4, core: 2. Of those that a mesh axis runs over, the one named last changes fastest.
Arguments:
- block_in: bfloat16 [4, 2048, 1024], P('sample', 'seq'), may hold values from -6 to 6
- out_cotangent: bfloat16 [4, 2048, 1024], P('sample', 'seq'), may hold values from -6 to 6
- norm_gain: float32 [1024], replicated, may hold values from 0.25 to 1.75
- gate_proj: bfloat16 [1024, 2048], P(None, 'head'), may hold values from -0.296875 to 0.296875
- value_proj: bfloat16 [1024, 2048], P(None, 'head'), may hold values from -0.1875 to 0.1875
- state_proj: bfloat16 [2, 1024, 128], P(None, None, 'head'), may hold values from -0.1875 to 0.1875
- step_proj: bfloat16 [1024, 32], P(None, 'head'), may hold values from -0.1875 to 0.1875
- conv_value: float32 [4, 2048], P(None, 'head'), may hold values from -0.6 to 0.6
- conv_state: float32 [4, 2, 128], P(None, None, 'head'), may hold values from -0.6 to 0.6
- conv_value_bias: float32 [2048], P('head'), may hold values from -0.5 to 0.5
- conv_state_bias: float32 [2, 128], P(None, 'head'), may hold values from -0.5 to 0.5
- step_bias: float32 [32], P('head'), may hold values from -4.5 to -3
- decay_log: float32 [32], P('head'), may hold values from -10 to 1
- skip_gain: float32 [32], P('head'), may hold values from 0.5 to 1.5
- gated_gain: float32 [2048], P('head'), may hold values from 0.25 to 1.75
- out_proj: bfloat16 [2048, 1024], P('head'), may hold values from -0.125 to 0.125
Outputs:
- block_out: bfloat16 [4, 2048, 1024], P('sample', 'seq')
- input_grad: float32 [4, 2048, 1024], P('sample', 'seq')
- norm_gain_grad: float32 [1024], replicated
- gate_proj_grad: float32 [1024, 2048], P(None, 'head')
- value_proj_grad: float32 [1024, 2048], P(None, 'head')
- state_proj_grad: float32 [2, 1024, 128], P(None, None, 'head')
- step_proj_grad: float32 [1024, 32], P(None, 'head')
- conv_value_grad: float32 [4, 2048], P(None, 'head')
- conv_state_grad: float32 [4, 2, 128], P(None, None, 'head')
- conv_value_bias_grad: float32 [2048], P('head')
- conv_state_bias_grad: float32 [2, 128], P(None, 'head')
- step_bias_grad: float32 [32], P('head')
- decay_log_grad: float32 [32], P('head')
- skip_gain_grad: float32 [32], P('head')
- gated_gain_grad: float32 [2048], P('head')
- out_proj_grad: float32 [2048, 1024], P('head')
All inputs are finite; a program needn't handle non-finite values.
Results may differ from a plain program's by a relative error of at most 0.0055.
The roundings to bfloat16 on the way count: a program that leaves them out, or rounds other values in their place, can miss the bound.
Values may be sent and summed in bfloat16 or wider, within the bound.
A program may use at most 192 MiB of HBM per device.

v0:
```python
import jax
import jax.numpy as jnp
from jax import lax
from jax.sharding import PartitionSpec as P

GROUP = 256


highest = lax.Precision.HIGHEST


def shifted(array, axis, by):
    size = lax.axis_size(axis)
    pairs = [(i, i + by) for i in range(size) if 0 <= i + by < size]
    return lax.ppermute(array, axis, pairs)


def entering(part, axis, combine, identity, reverse):
    count = lax.axis_size(axis)
    place = lax.axis_index(axis)
    ahead = count - 1 - place if reverse else place
    gathered = jax.tree.map(lambda a: lax.all_gather(a, axis), part)
    state = jax.tree.map(lambda a, e: jnp.zeros_like(a) + jnp.asarray(e, a.dtype), part, identity)

    def one(hop, state):
        source = count - 1 - hop if reverse else hop
        return combine(
            state, jax.tree.map(lambda a: lax.dynamic_index_in_dim(a, source, 0, False), gathered)
        )

    return lax.fori_loop(0, ahead, one, state)


def group_pass(values, input_vectors, readout, step_sizes, decay_rates, skip_gain, initial):
    total_length, local_heads, head_width = values.shape
    block_count = total_length // GROUP
    state_width = input_vectors.shape[-1]
    value_blocks = values.reshape(block_count, GROUP, local_heads, head_width)
    input_blocks = input_vectors.reshape(block_count, GROUP, state_width)
    readout_blocks = readout.reshape(block_count, GROUP, state_width)
    step_blocks = step_sizes.reshape(block_count, GROUP, local_heads)
    row_index = lax.broadcasted_iota(jnp.int32, (GROUP, GROUP), 0)
    column_index = lax.broadcasted_iota(jnp.int32, (GROUP, GROUP), 1)
    causal = (row_index >= column_index)[:, :, None]

    def advance(carried_state, block_item):
        block_values, block_inputs, block_readout, block_steps = block_item
        cumulative = jnp.cumsum(block_steps * decay_rates[None, :], axis=0)
        log_gaps = jnp.where(causal, cumulative[:, None, :] - cumulative[None, :, :], 0.0)
        decay_weights = jnp.where(causal, jnp.exp(log_gaps), 0.0)
        scores = jnp.dot(block_readout, block_inputs.T, precision=highest)
        mixing = scores[:, :, None] * decay_weights * block_steps[None, :, :]
        within = jnp.einsum("tsh,shp->thp", mixing, block_values, precision=highest)
        carried = jnp.exp(cumulative)[:, :, None] * jnp.einsum(
            "tn,hpn->thp", block_readout, carried_state, precision=highest
        )
        outputs = within + carried + skip_gain[None, :, None] * block_values
        tail_weight = jnp.exp(cumulative[-1:, :] - cumulative) * block_steps
        next_state = jnp.exp(cumulative[-1])[:, None, None] * carried_state + jnp.einsum(
            "sh,sn,shp->hpn", tail_weight, block_inputs, block_values, precision=highest
        )
        return (next_state, (outputs, cumulative))

    final_state, (outputs, cumulatives) = lax.scan(
        advance, initial, (value_blocks, input_blocks, readout_blocks, step_blocks)
    )
    return (outputs.reshape(total_length, local_heads, head_width), final_state, cumulatives)


def mixer(values, input_vectors, readout, step_raw, step_bias, decay_log, skip_gain, initial):
    step_sizes = jax.nn.softplus(step_raw + step_bias[None, :])
    decay_rates = -jnp.exp(decay_log)
    outputs, final_state, cumulatives = group_pass(
        values, input_vectors, readout, step_sizes, decay_rates, skip_gain, initial
    )
    return (outputs, final_state)


def batched_mixer(
    values, input_vectors, readout, step_raw, step_bias, decay_log, skip_gain, initial
):
    return jax.vmap(mixer, in_axes=(0, 0, 0, 0, None, None, None, 0))(
        values, input_vectors, readout, step_raw, step_bias, decay_log, skip_gain, initial
    )


def silu_slope(inputs):
    sigmoid_values = jax.nn.sigmoid(inputs)
    return sigmoid_values * (1.0 + inputs * (1.0 - sigmoid_values))


def chain(earlier, later):
    return (earlier[0] * later[0], later[0][:, :, None, None] * earlier[1] + later[1])


def per_device(
    block_in,
    out_cotangent,
    norm_gain,
    gate_proj,
    value_proj,
    state_proj,
    step_proj,
    conv_value,
    conv_state,
    conv_value_bias,
    conv_state_bias,
    step_bias,
    decay_log,
    skip_gain,
    gated_gain,
    out_proj,
):
    sequences, block_length, model_width = block_in.shape
    token_rows = sequences * block_length
    local_heads = step_proj.shape[1]
    inner_width = gate_proj.shape[1]
    head_width = inner_width // local_heads
    state_part = state_proj.shape[2]
    conv_taps = conv_value.shape[0]
    channels = inner_width + 2 * state_part
    full_inner = inner_width * lax.axis_size("head")
    flat_in = block_in.reshape(token_rows, model_width).astype(jnp.float32)
    inv_rms = lax.rsqrt(jnp.mean(flat_in * flat_in, axis=1, keepdims=True) + 1e-05)
    normed = (flat_in * inv_rms * norm_gain[None, :]).astype(jnp.bfloat16)
    gate_pre = jnp.dot(normed, gate_proj, preferred_element_type=jnp.float32).astype(jnp.bfloat16)
    value_pre = jnp.dot(normed, value_proj, preferred_element_type=jnp.float32).astype(jnp.bfloat16)
    state_pre = jnp.einsum(
        "td,kdn->tkn", normed, state_proj, preferred_element_type=jnp.float32
    ).astype(jnp.bfloat16)
    step_raw = jnp.dot(normed, step_proj, preferred_element_type=jnp.float32).reshape(
        sequences, block_length, local_heads
    )
    conv_in = jnp.concatenate(
        [value_pre, state_pre.reshape(token_rows, 2 * state_part)], axis=1
    ).reshape(sequences, block_length, channels)
    conv_weight = jnp.concatenate(
        [conv_value, conv_state.reshape(conv_taps, 2 * state_part)], axis=1
    )
    conv_bias = jnp.concatenate([conv_value_bias, conv_state_bias.reshape(2 * state_part)])
    edge_rows = shifted(conv_in[:, block_length - (conv_taps - 1) :], "seq", 1)
    padded = jnp.concatenate([edge_rows, conv_in], axis=1).astype(jnp.float32)
    pre_act = jnp.zeros((sequences, block_length, channels), jnp.float32) + conv_bias[None, None, :]
    for tap_index in range(conv_taps):
        pre_act = (
            pre_act
            + conv_weight[tap_index][None, None, :]
            * padded[:, tap_index : tap_index + block_length]
        )
    activated = jax.nn.silu(pre_act).astype(jnp.bfloat16)
    values = (
        activated[:, :, :inner_width]
        .astype(jnp.float32)
        .reshape(sequences, block_length, local_heads, head_width)
    )
    state_local = activated[:, :, inner_width:].reshape(sequences, block_length, 2, state_part)
    state_full = lax.all_gather(state_local, "head", axis=3, tiled=True)
    input_vectors = state_full[:, :, 0].astype(jnp.float32)
    readout = state_full[:, :, 1].astype(jnp.float32)
    step_sizes = jax.nn.softplus(step_raw + step_bias[None, None, :])
    decay_rates = -jnp.exp(decay_log)
    zero_state = jnp.zeros((sequences, local_heads, head_width, readout.shape[-1]), jnp.float32)
    local_out, local_final, cumulatives = jax.vmap(group_pass, in_axes=(0, 0, 0, 0, None, None, 0))(
        values, input_vectors, readout, step_sizes, decay_rates, skip_gain, zero_state
    )
    block_totals = cumulatives[:, :, -1, :]
    offsets = jnp.cumsum(block_totals, axis=1) - block_totals
    through = (cumulatives + offsets[:, :, None, :]).reshape(sequences, block_length, local_heads)
    block_decay = jnp.exp(through[:, -1, :])
    identity = (jnp.ones_like(block_decay), jnp.zeros_like(local_final))
    unused_decay, incoming = entering((block_decay, local_final), "seq", chain, identity, False)
    carried = jnp.exp(through)[:, :, :, None] * jnp.einsum(
        "stn,shpn->sthp", readout, incoming, precision=highest
    )
    mixed = (local_out + carried).reshape(token_rows, inner_width)
    gate_value = gate_pre.astype(jnp.float32)
    gate_act = jax.nn.silu(gate_value)
    gated = mixed * gate_act
    total_squares = lax.psum(jnp.sum(gated * gated, axis=1), "head")
    gated_rms = lax.rsqrt(total_squares / full_inner + 1e-05)[:, None]
    gated_norm = (gated * gated_rms * gated_gain[None, :]).astype(jnp.bfloat16)
    share_rows = token_rows // lax.axis_size("head")
    branch_share = lax.psum_scatter(
        jnp.dot(gated_norm, out_proj, preferred_element_type=jnp.float32),
        "head",
        scatter_dimension=0,
        tiled=True,
    )
    own_start = lax.axis_index("head") * share_rows
    own_input = lax.dynamic_slice_in_dim(flat_in, own_start, share_rows, 0)
    out_piece = (own_input + branch_share).astype(jnp.bfloat16)
    block_out = lax.all_gather(out_piece, "head", axis=0, tiled=True).reshape(
        sequences, block_length, model_width
    )
    cotangent = out_cotangent.reshape(token_rows, model_width)
    d_norm_out = jnp.einsum("td,cd->tc", cotangent, out_proj, preferred_element_type=jnp.float32)
    out_proj_grad = jnp.einsum(
        "tc,td->cd", gated_norm, cotangent, preferred_element_type=jnp.float32
    )
    gated_gain_grad = jnp.sum(d_norm_out * gated * gated_rms, axis=0)
    scaled = d_norm_out * gated_gain[None, :]
    total_dot = lax.psum(jnp.sum(scaled * gated, axis=1), "head")
    d_gated = gated_rms * scaled - gated * gated_rms**3 * (total_dot / full_inner)[:, None]
    d_mixed = (d_gated * gate_act).reshape(sequences, block_length, local_heads, head_width)
    d_gate = (d_gated * mixed * silu_slope(gate_value)).astype(jnp.bfloat16)
    direct = jnp.einsum("sth,sthp,stn->shpn", jnp.exp(through), d_mixed, readout, precision=highest)
    unused_back, onward = entering((block_decay, direct), "seq", chain, identity, True)
    primal, pullback = jax.vjp(
        batched_mixer,
        values,
        input_vectors,
        readout,
        step_raw,
        step_bias,
        decay_log,
        skip_gain,
        incoming,
    )
    (
        d_values,
        d_inputs,
        d_readout,
        d_step_raw,
        step_bias_grad,
        decay_grad,
        skip_grad,
        unused_state,
    ) = pullback((d_mixed, onward))
    d_state = lax.psum_scatter(
        jnp.stack([d_inputs, d_readout], axis=2), "head", scatter_dimension=3, tiled=True
    )
    d_act = jnp.concatenate(
        [
            d_values.reshape(sequences, block_length, inner_width),
            d_state.reshape(sequences, block_length, 2 * state_part),
        ],
        axis=2,
    )
    d_pre = d_act * silu_slope(pre_act)
    next_rows = shifted(d_pre[:, : conv_taps - 1], "seq", -1)
    d_extended = jnp.concatenate([d_pre, next_rows], axis=1)
    d_conv_in = jnp.zeros_like(d_pre)
    conv_terms = []
    for tap_index in range(conv_taps):
        offset = conv_taps - 1 - tap_index
        d_conv_in = (
            d_conv_in
            + conv_weight[tap_index][None, None, :] * d_extended[:, offset : offset + block_length]
        )
        conv_terms.append(
            jnp.sum(d_pre * padded[:, tap_index : tap_index + block_length], axis=(0, 1))
        )
    conv_grad = jnp.stack(conv_terms)
    conv_bias_grad = jnp.sum(d_pre, axis=(0, 1))
    d_conv_flat = d_conv_in.reshape(token_rows, channels).astype(jnp.bfloat16)
    d_value_pre = d_conv_flat[:, :inner_width]
    d_state_pre = d_conv_flat[:, inner_width:].reshape(token_rows, 2, state_part)
    d_step = d_step_raw.reshape(token_rows, local_heads).astype(jnp.bfloat16)
    gate_grad = jnp.einsum("td,tc->dc", normed, d_gate, preferred_element_type=jnp.float32)
    value_grad = jnp.einsum("td,tc->dc", normed, d_value_pre, preferred_element_type=jnp.float32)
    state_grad = jnp.einsum("td,tkn->kdn", normed, d_state_pre, preferred_element_type=jnp.float32)
    step_grad = jnp.einsum("td,th->dh", normed, d_step, preferred_element_type=jnp.float32)
    partial_normed = jnp.einsum("tc,dc->td", d_gate, gate_proj, preferred_element_type=jnp.float32)
    partial_normed = partial_normed + jnp.einsum(
        "tc,dc->td", d_value_pre, value_proj, preferred_element_type=jnp.float32
    )
    partial_normed = partial_normed + jnp.einsum(
        "tkn,kdn->td", d_state_pre, state_proj, preferred_element_type=jnp.float32
    )
    partial_normed = partial_normed + jnp.einsum(
        "th,dh->td", d_step, step_proj, preferred_element_type=jnp.float32
    )
    d_normed = lax.psum(partial_normed, "head")
    norm_grad = jnp.sum(d_normed * flat_in * inv_rms, axis=0)
    scaled_in = d_normed * norm_gain[None, :]
    input_grad = (
        cotangent.astype(jnp.float32)
        + inv_rms * scaled_in
        - flat_in * inv_rms**3 * jnp.mean(scaled_in * flat_in, axis=1, keepdims=True)
    )
    conv_value_grad = conv_grad[:, :inner_width]
    conv_state_grad = conv_grad[:, inner_width:].reshape(conv_taps, 2, state_part)
    conv_value_bias_grad = conv_bias_grad[:inner_width]
    conv_state_bias_grad = conv_bias_grad[inner_width:].reshape(2, state_part)
    summed = tuple(
        lax.psum(
            (
                norm_grad,
                gate_grad,
                value_grad,
                state_grad,
                step_grad,
                conv_value_grad,
                conv_state_grad,
                conv_value_bias_grad,
                conv_state_bias_grad,
                step_bias_grad,
                decay_grad,
                skip_grad,
                gated_gain_grad,
                out_proj_grad,
            ),
            ("seq", "sample"),
        )
    )
    return (block_out, input_grad.reshape(sequences, block_length, model_width)) + summed


def solution(mesh):
    return jax.shard_map(
        per_device,
        mesh=mesh,
        in_specs=(
            P("sample", "seq", None),
            P("sample", "seq", None),
            P(),
            P(None, "head"),
            P(None, "head"),
            P(None, None, "head"),
            P(None, "head"),
            P(None, "head"),
            P(None, None, "head"),
            P("head"),
            P(None, "head"),
            P("head"),
            P("head"),
            P("head"),
            P("head"),
            P("head", None),
        ),
        out_specs=(
            P("sample", "seq", None),
            P("sample", "seq", None),
            P(),
            P(None, "head"),
            P(None, "head"),
            P(None, None, "head"),
            P(None, "head"),
            P(None, "head"),
            P(None, None, "head"),
            P("head"),
            P(None, "head"),
            P("head"),
            P("head"),
            P("head"),
            P("head"),
            P("head", None),
        ),
        check_vma=False,
    )
```

profile of v0, /device:TPU:0, one launch (start us, length us, event | category | flops | bytes accessed | tf_op | source)
XLA Modules:
  0.0 856.4 jit_solution(13407658360489493288)
XLA Ops:
  36.5 15.3 %all_gather.24 = bf16[2,512,2,128]{1,2,0,3:T(2,128)(2,1)S(1)} all-gather(bf16[2,512,2,32]{1,2,0,3:T(2,128)(2,1)S(1)} %copy.200), channel_id=1, replica_groups=mesh['seq'=4,'sample'=2,'head'=4] {'head'}, dimensions={3}, use_global_device_ids=true | all-gather | bytes 655360 | tf_op jit(solution)/shard_map/all_gather | solution.py:157
  68.3 29.9 %while.120 = (s32[]{:T(128)}, f32[2,8,64,128]{3,2,1,0:T(8,128)}, f32[2,2,256,8,64]{2,4,3,1,0:T(8,128)}, f32[2,2,256,8]{2,3,1,0:T(8,128)S(1)}, f32[2,2,256,8]{2,3...) while((s32[]{:T(128)}, f32[2,8,64,128]{3,2,1,0:T(8,128)}, ...), condition=%wide.region_4.5_spmd.clone.clone, body=%wide.region_1.4_spmd.clone.clone.sunk | while | flops 1819623424 | bytes 16686640 | solution.py:64
  103.8 10.2 %all-gather = f32[8,1,8]{2,1,0:T(1,128)S(1)} all-gather(f32[2,1,8]{2,1,0:T(1,128)S(1)} %slice_exponential_fusion), channel_id=2, replica_groups=mesh['seq'=4,'sample'=2,'head'=4] {'seq'}, dimensions={0}, use_global_device_ids=true | all-gather | bytes 320 | tf_op jit(solution)/shard_map/all_gather | solution.py:22
  120.8 15.5 %all-gather.9.cloned.1.call-done = f32[8,8,64,128]{3,2,1,0:T(8,128)} async-done(((f32[2,8,64,128]{3,2,1,0:T(8,128)}), f32[8,8,64,128]{3,2,1,0:T(8,128)}) %all-gather.9.cloned.1.call-update) | async-done | bytes 2097168 | tf_op jit(solution)/shard_map/all_gather | solution.py:22
  147.1 11.7 %psum.119 = f32[1024]{0:T(1024)S(1)} all-reduce(f32[1024]{0:T(1024)S(1)} %get-tuple-element.2065), channel_id=1, replica_groups=mesh['seq'=4,'sample'=2,'head'=4] {'head'}, use_global_device_ids=true, to_apply=%region_9.10 | all-reduce | flops 1024 | bytes 8192 | tf_op jit(solution)/shard_map/psum | solution.py:179
  158.8 6.2 multiply_reduce_fusion.7
  165.0 8.3 psum.120
  191.7 43.1 %while.119 = (s32[]{:T(128)}, f32[2,8,64,128]{3,2,1,0:T(8,128)}, f32[2,2,256,256,8]{3,4,2,1,0:T(8,128)}, f32[2,2,128,256]{2,3,1,0:T(8,128)}, f32[2,2,256,256,8]{...) while((s32[]{:T(128)}, f32[2,8,64,128]{3,2,1,0:T(8,128)}, ...), condition=%wide.region_18.19_spmd.clone.clone, body=%wide.region_15.18_spmd.clone.clone.sunk | while | flops 1013198912 | bytes 70188120 | solution.py:64
  196.4 6.8 multiply_dynamic-update-slice_fusion.2
  218.0 6.6 multiply_dynamic-update-slice_fusion.2
  243.0 6.3 while.118
  253.5 137.9 %while.121 = (s32[]{:T(128)}, f32[8]{0:T(128)}, f32[8]{0:T(128)}, f32[2,8,64,128]{3,2,1,0:T(8,128)}, f32[2,2,256,8,64]{2,4,3,1,0:T(8,128)}, /*index=5*/f32[2,2,2...) while((s32[]{:T(128)}, f32[8]{0:T(128)}, f32[8]{0:T(128)}, ...), condition=%wide.region_31.32_spmd.clone.clone, body=%wide.region_19.31_spmd.clone.clone.sunk | while | flops 3639656448 | bytes 113358104 | solution.py:64
  253.6 6.0 constant_dynamic-slice_fusion.13
  264.6 10.5 %fusion.281 = (f32[2,256,8]{1,2,0:T(8,128)S(1)}, f32[2,256,8]{1,2,0:T(8,128)S(1)}, f32[2,256,256]{2,1,0:T(8,128)}, f32[2,256,8]{1,2,0:T(8,128)S(1)}) fusion(f32[1,2,256,256,8]{3,4,2,1,0:T(8,128)S(1)} %get-tuple-element.2591, f32[2,256,8]{1,2,0:T(8,128)S(1)} %dynamic-slice_bitcast_fusion.18, f32[2,256,256]{2,1,0:T(8,128)S(1)} %dynamic-slice_bitcast_fusion.19, ...), kind=kOutput, calls=%fused_computation.155.clone.1 | convolution fusion | flops 816697344 | bytes 15860736 | tf_op jit(solution)/shard_map/transpose(jvp(vmap()))/while/body/eval_jaxpr/tsh,shp->thp/dot_general | solution.py:53
  322.3 6.0 constant_dynamic-slice_fusion.13
  333.3 10.5 %fusion.281 = (f32[2,256,8]{1,2,0:T(8,128)S(1)}, f32[2,256,8]{1,2,0:T(8,128)S(1)}, f32[2,256,256]{2,1,0:T(8,128)}, f32[2,256,8]{1,2,0:T(8,128)S(1)}) fusion(f32[1,2,256,256,8]{3,4,2,1,0:T(8,128)S(1)} %get-tuple-element.2591, f32[2,256,8]{1,2,0:T(8,128)S(1)} %dynamic-slice_bitcast_fusion.18, f32[2,256,256]{2,1,0:T(8,128)S(1)} %dynamic-slice_bitcast_fusion.19, ...), kind=kOutput, calls=%fused_computation.155.clone.1 | convolution fusion | flops 816697344 | bytes 15860736 | tf_op jit(solution)/shard_map/transpose(jvp(vmap()))/while/body/eval_jaxpr/tsh,shp->thp/dot_general | solution.py:53
  414.9 31.8 %all-reduce.11.cloned.1.call-done = f32[2,512,2,128]{1,2,0,3:T(2,128)} async-done(((f32[2,512,2,128]{1,2,0,3:T(2,128)}), f32[2,512,2,128]{1,2,0,3:T(2,128)}) %all-reduce.11.cloned.1.call-update) | async-done | bytes 1048592
  447.8 8.2 multiply_reduce_fusion.6
  463.7 6.2 fusion.151
  481.1 44.5 %reduce-scatter.2.cloned.1.call-done = f32[256,1024]{1,0:T(8,128)} async-done(((f32[1024,1024]{1,0:T(8,128)}), f32[256,1024]{1,0:T(8,128)}) %reduce-scatter.2.cloned.1.call-update) | async-done | bytes 1048592 | tf_op jit(solution)/shard_map/reduce_scatter | solution.py:183
  542.9 140.4 %all-reduce.9.cloned.1.call-done = f32[1024,1024]{1,0:T(8,128)} async-done(((f32[1024,1024]{1,0:T(8,128)}), f32[1024,1024]{1,0:T(8,128)}) %all-reduce.9.cloned.1.call-update) | async-done | bytes 4194320 | tf_op jit(solution)/shard_map/psum | solution.py:273
  686.8 26.1 %all-reduce.3 = (f32[1024]{0:T(1024)}, f32[1024,8]{0,1:T(8,128)}, f32[4,512]{1,0:T(4,128)}, f32[4,2,32]{2,1,0:T(2,128)}, f32[512]{0:T(512)}, /*index=5*/f32[2,32...) all-reduce(f32[1024]{0:T(1024)S(1)} %get-tuple-element.1844, ...), channel_id=1, replica_groups=mesh['seq'=4,'sample'=2,'head'=4] {'seq','sample'}, use_global_device_ids=true, to_apply=%region_36.37 | all-reduce | flops 12632 | bytes 101056 | tf_op jit(solution)/shard_map/psum | solution.py:286
  717.8 11.6 %all-gather.7.cloned.1.call-done = bf16[1024,1024]{1,0:T(8,128)(2,1)} async-done(((bf16[256,1024]{1,0:T(8,128)(2,1)}), bf16[1024,1024]{1,0:T(8,128)(2,1)}) %all-gather.7.cloned.1.call-update) | async-done | bytes 2097168 | tf_op jit(solution)/shard_map/all_gather | solution.py:192
  729.4 110.5 %all-reduce.13.cloned.1.call-done = (f32[1024,512]{1,0:T(8,128)}, f32[1024,512]{1,0:T(8,128)}, f32[2,1024,32]{1,2,0:T(8,128)}, f32[512,1024]{1,0:T(8,128)}) async-done(((f32[1024,512]{1,0:T(8,128)}, f32[1024,512]{1,0:T(8,128)}, f32[2,1024,32]{1,2,0:T(8,128)}, f32[512,1024]{1,0:T(8,128)}), (f32[1024,512]{1,0:T(8,128)}, f32[1024,512]{1,0:T(8,128)}, f32[2,1024,32]{1,2,0:T(8,128)}, ...) | async-done | bytes 6553616 | tf_op jit(solution)/shard_map/psum | solution.py:286
  (590 shorter events, 346.1 us)
Async XLA Ops:
  7.2 151.6 %copy-start = (bf16[512,1024]{1,0:T(8,128)(2,1)S(1)}, bf16[512,1024]{1,0:T(8,128)(2,1)}, u32[]{:S(2)}) copy-start(bf16[512,1024]{1,0:T(8,128)(2,1)} %param.41) | copy-start | bytes 3145732
  7.2 129.1 %all-gather.9.cloned.1.call-start = ((), (), s32[]{:S(2)}) async-start(), calls=%async_computation.4 | async-start | bytes 2621440 | tf_op jit(solution)/shard_map/all_gather | solution.py:22
  15.3 9.9 %copy-start.90 = (f32[4,512]{1,0:T(4,128)S(1)}, f32[4,512]{1,0:T(4,128)}, u32[]{:S(2)}) copy-start(f32[4,512]{1,0:T(4,128)} %param.33) | copy-start | bytes 24580
  15.3 9.9 %copy-start.91 = (f32[4,2,32]{2,1,0:T(2,128)S(1)}, f32[4,2,32]{2,1,0:T(2,128)}, u32[]{:S(2)}) copy-start(f32[4,2,32]{2,1,0:T(2,128)} %param.34) | copy-start | bytes 3076
  15.3 10.1 %copy-start.100 = (f32[2,32]{1,0:T(2,128)S(1)}, f32[2,32]{1,0:T(2,128)}, u32[]{:S(2)}) copy-start(f32[2,32]{1,0:T(2,128)} %param.36) | copy-start | bytes 772
  19.7 11.4 %collective-permute-start = (bf16[2,3,576]{1,2,0:T(8,128)(2,1)}, bf16[2,3,576]{1,2,0:T(8,128)(2,1)}, u32[]{:S(2)}, u32[]{:S(2)}) collective-permute-start(bf16[2,3,576]{1,2,0:T(8,128)(2,1)} %pad_maximum_fusion.2), channel_id=1, source_target_pairs={{0,8},{8,16},{16,24},{1,9},{9,17},{17,25},{2,10},{10,18},{18,26},{... | collective-permute-start | bytes 20744 | tf_op jit(solution)/shard_map/ppermute | solution.py:15
  98.2 143.9 %all-gather.11.cloned.1.call-start = ((), (), s32[]{:S(2)}) async-start(), calls=%async_computation.5 | async-start | bytes 2621440 | tf_op jit(solution)/shard_map/all_gather | solution.py:22
  144.5 14.3 %copy-start.92 = (f32[512]{0:T(512)S(1)}, f32[512]{0:T(512)}, u32[]{:S(2)}) copy-start(f32[512]{0:T(512)} %param.40) | copy-start | bytes 6148
  158.8 14.5 %copy-start.79 = (f32[1024]{0:T(1024)}, f32[1024]{0:T(1024)S(1)}, u32[]{:S(2)}) copy-start(f32[1024]{0:T(1024)S(1)} %get-tuple-element.2058) | copy-start | bytes 12292
  186.6 260.1 %all-reduce.11.cloned.1.call-start = ((), (), s32[]{:S(2)}) async-start(), calls=%async_computation.6 | async-start | bytes 2097152
  287.2 15.4 %copy-start.87 = (f32[8]{0:T(128)S(1)}, f32[8]{0:T(128)}, u32[]{:S(2)}) copy-start(f32[8]{0:T(128)} %get-tuple-element.2809) | copy-start | bytes 100 | tf_op jit(solution)/shard_map/transpose(jvp(vmap()))/while
  302.6 9.5 %copy-start.88 = (f32[8]{0:T(128)}, f32[8]{0:T(128)S(1)}, u32[]{:S(2)}) copy-start(f32[8]{0:T(128)S(1)} %fusion.287) | copy-start | bytes 100 | tf_op jit(solution)/shard_map/transpose(jvp(vmap()))/while
  303.4 10.5 %copy-start.9 = (f32[2,256,8,64]{1,3,2,0:T(8,128)S(1)}, f32[2,256,8,64]{1,3,2,0:T(8,128)}, u32[]{:S(2)}) copy-start(f32[2,256,8,64]{1,3,2,0:T(8,128)} %get-tuple-element.2602) | copy-start | bytes 3145732 | tf_op jit(solution)/shard_map/transpose(jvp(vmap()))/while
  355.9 15.4 %copy-start.87 = (f32[8]{0:T(128)S(1)}, f32[8]{0:T(128)}, u32[]{:S(2)}) copy-start(f32[8]{0:T(128)} %get-tuple-element.2809) | copy-start | bytes 100 | tf_op jit(solution)/shard_map/transpose(jvp(vmap()))/while
  371.3 9.5 %copy-start.88 = (f32[8]{0:T(128)}, f32[8]{0:T(128)S(1)}, u32[]{:S(2)}) copy-start(f32[8]{0:T(128)S(1)} %fusion.287) | copy-start | bytes 100 | tf_op jit(solution)/shard_map/transpose(jvp(vmap()))/while
  372.1 10.5 %copy-start.9 = (f32[2,256,8,64]{1,3,2,0:T(8,128)S(1)}, f32[2,256,8,64]{1,3,2,0:T(8,128)}, u32[]{:S(2)}) copy-start(f32[2,256,8,64]{1,3,2,0:T(8,128)} %get-tuple-element.2602) | copy-start | bytes 3145732 | tf_op jit(solution)/shard_map/transpose(jvp(vmap()))/while
  396.0 129.5 %reduce-scatter.2.cloned.1.call-start = ((), (), s32[]{:S(2)}) async-start(), calls=%async_computation.1 | async-start | bytes 5242880 | tf_op jit(solution)/shard_map/reduce_scatter | solution.py:183
  401.0 282.3 %all-reduce.9.cloned.1.call-start = ((), (), s32[]{:S(2)}) async-start(), calls=%async_computation.3 | async-start | bytes 8388608 | tf_op jit(solution)/shard_map/psum | solution.py:273
  457.7 5.6 collective-permute-start.1
  476.9 252.4 %all-gather.7.cloned.1.call-start = ((), (), s32[]{:S(2)}) async-start(), calls=%async_computation.2 | async-start | bytes 2621440 | tf_op jit(solution)/shard_map/all_gather | solution.py:192
  528.0 311.9 %all-reduce.13.cloned.1.call-start = ((), (), s32[]{:S(2)}) async-start(), calls=%async_computation.7 | async-start | bytes 13107200 | tf_op jit(solution)/shard_map/psum | solution.py:286
  540.6 142.7 %copy-start.64 = (f32[1024]{0:T(1024)S(1)}, f32[1024]{0:T(1024)}, u32[]{:S(2)}) copy-start(f32[1024]{0:T(1024)} %param.28) | copy-start | bytes 12292
  542.9 143.9 %copy-start.78 = (f32[8]{0:T(128)S(1)}, f32[8]{0:T(128)}, u32[]{:S(2)}) copy-start(f32[8]{0:T(128)} %get-tuple-element.1204) | copy-start | bytes 100
  542.9 143.9 %copy-start.94 = (f32[512]{0:T(512)S(1)}, f32[512]{0:T(512)}, u32[]{:S(2)}) copy-start(f32[512]{0:T(512)} %get-tuple-element.1850) | copy-start | bytes 6148
  (130 other events, 526.5 us)
Sparse Core Ops, SparseCore 0:
  98.3 37.9 all-gather.8
  186.7 40.2 all-gather.10
  396.1 50.5 all-reduce.10
  449.5 76.0 reduce-scatter.1
  527.7 155.5 all-reduce.8
  684.7 44.6 all-gather.6
  734.2 105.6 all-reduce.12
where the time goes:
time: 865 us; the launch traced here: 856 us
  waiting for transfers between devices  360 us (42%)
  matrix products  155 us (18%)
  local copies, waits for them, and re-layouts  138 us (16%)
  other arithmetic  107 us (12%)
  blocking collectives  71.6 us (8%)
  between operations  15.9 us (2%)
    psum x1, waiting for transfers between devices, per_device(): d_normed = lax.psum(partial_normed, 'head')  140 us
    psum x1, waiting for transfers between devices, per_device(): lax.psum((norm_grad, gate_grad, value_grad, state_grad, step_grad, conv_v...  111 us
    reduce_scatter x1, waiting for transfers between devices, per_device(): lax.psum_scatter(jnp.dot(gated_norm, out_proj, preferred_element_type=jnp...  44.5 us
    dot_general x6, matrix products, advance(): within = jnp.einsum('tsh,shp->thp', mixing, block_values, precision=highest)  42.7 us
    unnamed x8, waiting for transfers between devices  31.9 us
    unnamed x139, local copies, waits for them, and re-layouts  27.6 us
    psum x1, blocking collectives, per_device(): lax.psum((norm_grad, gate_grad, value_grad, state_grad, step_grad, conv_v...  26.1 us
    dynamic_slice x10, local copies, waits for them, and re-layouts, group_pass(): lax.scan(advance, initial, (value_blocks, input_blocks, readout_blocks, s...  25.2 us
  transfers between devices with their start and end apart: 9, of which 8 were waited for; matrix products, arithmetic and copies ran while one was open for 15% of the time, Pallas kernels for 0%

commit v1 on v0

v1 whole, which is shorter than its diff:
```python
import functools

import jax
import jax.numpy as jnp
from jax import lax
from jax.experimental import pallas as pl
from jax.experimental.pallas import tpu as pltpu
from jax.sharding import PartitionSpec as P

f32, bf16 = jnp.float32, jnp.bfloat16
HI = lax.Precision.HIGHEST
MESH = pl.DeviceIdType.MESH
Q = 128
TILE = 32
HALO = 16
EPS = 1e-05
NN, NT, TN = ((1,), (0,)), ((1,), (1,)), ((0,), (0,))


def mm(a, b, dims=NN, precision=None):
    return lax.dot_general(
        a, b, (dims, ((), ())), preferred_element_type=f32, precision=precision
    )


def mm2(a, b, dims=NN):
    high = b.astype(bf16)
    return mm(a, high, dims) + mm(a, (b - high.astype(f32)).astype(bf16), dims)


def at(i, n):
    return pl.ds(pl.multiple_of(i * n, n), n)


def loop(count, body):
    def step(i, carry):
        body(i)
        return carry

    lax.fori_loop(0, count, step, 0)


def iota(shape, axis):
    return lax.broadcasted_iota(jnp.int32, shape, axis)


def lane_heads(heads, width):
    shift = (width // heads).bit_length() - 1
    return ((iota((Q, width), 1) >> shift) == iota((Q, width), 0)).astype(f32)


def triangle(keep):
    return jnp.where(keep(iota((Q, Q), 0), iota((Q, Q), 1)), 1.0, 0.0)


def fold8(v):
    return jnp.sum(v.reshape(v.shape[0] // 8, 8, v.shape[1]), axis=0)


def row_of(v, e):
    return mm(jnp.broadcast_to(v, (8, Q)), e, precision=HI)[0:1]


def normalize(v, gain):
    inv = lax.rsqrt(jnp.mean(v * v, axis=1, keepdims=True) + EPS)
    return (v * inv * gain).astype(bf16), inv


def remote(src, dst, send, recv, **place):
    return pltpu.make_async_remote_copy(
        src_ref=src, dst_ref=dst, send_sem=send, recv_sem=recv, device_id=place, device_id_type=MESH
    )


class Fold:
    def __init__(self, part, near, far, sems, tiles):
        self.part, self.near, self.far, self.tiles = part, near, far, tiles
        self.a, self.b, self.c, self.d = sems
        self.rows = part.shape[0] // tiles
        place = lax.axis_index("head")
        self.inner = (place == 1) | (place == 2)
        self.beside = jnp.where(place < 2, 1 - place, 5 - place)
        self.across = 3 - place

    def outward(self, i, src):
        r = at(i, self.rows)
        return remote(src.at[r], self.near.at[r], self.a.at[i], self.b.at[i], head=self.beside)

    def middle(self, i):
        r = at(i, self.rows)
        return remote(self.part.at[r], self.far.at[r], self.c.at[i], self.d.at[i], head=self.across)

    def begin(self, first, count):
        @pl.when(jnp.logical_not(self.inner))
        def _():
            loop(count, lambda i: self.outward(first + i, self.part).start())

    def add(self, dst, u, v, i):
        def tile(j):
            r = at(i * (self.rows // TILE) + j, TILE)
            dst[r, :] = (u[r, :].astype(f32) + v[r, :].astype(f32)).astype(bf16)

        loop(self.rows // TILE, tile)

    def one(self, i):
        @pl.when(self.inner)
        def _():
            self.outward(i, self.near).wait_recv()
            self.add(self.part, self.part, self.near, i)
            self.middle(i).start()

    def two(self, i):
        @pl.when(self.inner)
        def _():
            self.middle(i).wait_recv()
            self.add(self.near, self.part, self.far, i)
            self.outward(i, self.near).start()

    def end(self):
        @pl.when(self.inner)
        def _():
            def done(i):
                self.middle(i).wait_send()
                self.outward(i, self.near).wait_send()

            loop(self.tiles, done)

        @pl.when(jnp.logical_not(self.inner))
        def _():
            def done(i):
                self.outward(i, self.part).wait_send()
                self.outward(i, self.near).wait_recv()

            loop(self.tiles, done)


class Relay:
    def __init__(self, blocks, slots, send, recv, count, way):
        self.blocks, self.slots, self.send, self.recv = blocks, slots, send, recv
        self.count, self.way = count, way
        self.place = lax.axis_index("seq")

    def copies(self, d, source):
        to = self.place + self.way * d
        return [
            remote(b, s.at[source], self.send.at[j, d - 1], self.recv.at[j, d - 1], seq=to)
            for j, (b, s) in enumerate(zip(self.blocks, self.slots))
        ]

    def reaches(self, d):
        return self.place + d < self.count if self.way > 0 else self.place >= d

    def hears(self, d):
        return self.place >= d if self.way > 0 else self.place + d < self.count

    def start(self):
        for d in range(1, self.count):

            @pl.when(self.reaches(d))
            def _():
                for c in self.copies(d, self.place):
                    c.start()

    def gather(self, state, e):
        state[...] = jnp.zeros_like(state)
        for d in range(self.count - 1, 0, -1):

            @pl.when(self.hears(d))
            def _():
                source = self.place - self.way * d
                for c in self.copies(d, source):
                    c.wait_recv()
                for s in range(state.shape[0]):
                    decay = mm(jnp.exp(self.slots[1][source, s]), e[...], precision=HI)[0:1]
                    state[s] = state[s] * decay + self.slots[0][source, s].astype(f32)

    def finish(self):
        for d in range(1, self.count):

            @pl.when(self.reaches(d))
            def _():
                for c in self.copies(d, self.place):
                    c.wait_send()


def block(
    dims,
    x_in, cot_in, gain, wg_in, wv_in, spt, stp, wo_in, cst, cwv, hp, sk, gg,
    outs, dnorm, grads, state_out, small_out,
    xb, cot, wg, wv, wst, wo, cwt, cw, xh,
    nt, inv, gate, pad, slope, act, dt, sg, cum, cum_t, dt_t, entry, ys, dy, gn, dg, later,
    dcs, e, st, work, off, tt, stats, stats_t, stats_in,
    fin, tot, slots, slots_t, chained,
    part1, far1, part2, far2,
    gr, gr_in, gr_pieces, gr_sum, sg_in, sg_pieces, sg_line, sg_sum,
    acc, hsums, sums, nsums, smallz, smallz_in, small, small_two, small_in, nx, edge8,
    load, halo_sem, wt_s, wt_r, f_s, f_r, b_s, b_r, st_s, st_r, nx_s, nx_r,
    z1, z2, ga_s, ga_r, gb_s, gb_r, gc_s, gc_r, gd_s, gd_r,
    sa_s, sa_r, sb_s, sb_r, sz_s, sz_r, sc_s, sc_r, sd_s, sd_r, m1_s, m1_r, m2_s, m2_r,
):
    S, L, seqs, lines, tiles = dims
    T, D = xb.shape
    C = wg.shape[1]
    W = C + 2 * Q
    NC = L // Q
    own = spt.shape[0] // 2
    full = C * lines
    ps, pc, ph = lax.axis_index("seq"), lax.axis_index("sample"), lax.axis_index("head")
    other = 1 - pc
    group = 2 * seqs
    DC = D // C
    mine = ps * 2 + pc
    near1, near2 = outs, dnorm
    nb = part1

    def peer(i):
        p = lax.rem(mine + i, group)
        return {"seq": p // 2, "sample": lax.rem(p, 2)}

    def line(i):
        return lax.rem(ph + i, lines)

    def ring(i):
        return lax.rem(ps + i, seqs)

    moves = [
        pltpu.make_async_copy(x_in, xb, load.at[0]),
        pltpu.make_async_copy(wg_in, wg, load.at[1]),
        pltpu.make_async_copy(wv_in, wv, load.at[2]),
        pltpu.make_async_copy(stp, wst.at[pl.ds(2 * Q, Q)], load.at[3]),
        pltpu.make_async_copy(spt.at[pl.ds(0, own)], wst.at[at(ph, own)], load.at[4]),
        pltpu.make_async_copy(
            spt.at[pl.ds(own, own)], wst.at[pl.ds(pl.multiple_of(Q + ph * own, own), own)], load.at[5]
        ),
        pltpu.make_async_copy(cst.at[pl.ds(0, own)], cwt.at[at(ph, own)], load.at[6]),
        pltpu.make_async_copy(
            cst.at[pl.ds(own, own)], cwt.at[pl.ds(pl.multiple_of(Q + ph * own, own), own)], load.at[7]
        ),
        pltpu.make_async_copy(cot_in, cot, load.at[8]),
        pltpu.make_async_copy(wo_in, wo, load.at[9]),
    ]
    for m in moves:
        m.start()
    barrier = pltpu.get_barrier_semaphore()
    for i in range(1, group):
        pl.semaphore_signal(barrier, inc=1, device_id=peer(i), device_id_type=MESH)
    for i in range(1, lines):
        pl.semaphore_signal(barrier, inc=1, device_id={"head": line(i)}, device_id_type=MESH)
    pl.semaphore_wait(barrier, group - 1 + lines - 1)

    def halo(s):
        return remote(
            x_in.at[pl.ds(s * L + L - HALO, HALO)], xh.at[pl.ds(s * HALO, HALO)],
            halo_sem.at[0, s], halo_sem.at[1, s], seq=ps + 1,
        )

    @pl.when(ps < seqs - 1)
    def _():
        for s in range(S):
            halo(s).start()

    @pl.when(ps == 0)
    def _():
        xh[...] = jnp.zeros_like(xh)

    def weights(i):
        to = line(i)
        low = at(ph, own)
        high = pl.ds(pl.multiple_of(Q + ph * own, own), own)
        parts = [
            (spt.at[pl.ds(0, own)], wst.at[low]),
            (spt.at[pl.ds(own, own)], wst.at[high]),
            (cst.at[pl.ds(0, own)], cwt.at[low]),
            (cst.at[pl.ds(own, own)], cwt.at[high]),
        ]
        return [
            remote(a, b, wt_s.at[j, i - 1], wt_r.at[j, i - 1], head=to)
            for j, (a, b) in enumerate(parts)
        ]

    for i in range(1, lines):
        for c in weights(i):
            c.start()

    e[...] = lane_heads(C // 64, C)
    moves[0].wait()

    def norm_rows(r):
        n, i = normalize(xb[at(r, TILE), :].astype(f32), gain[...])
        nb[at(r, TILE), :] = n
        inv[at(r, TILE), :] = jnp.broadcast_to(i, (TILE, Q))

    loop(T // TILE, norm_rows)
    moves[1].wait()
    moves[2].wait()

    def project(s):
        n = nb[at(s, L), :]
        gate[at(s, L), :] = mm(n, wg[...]).astype(bf16)
        pad[s, HALO:, 0:C] = mm(n, wv[...]).astype(bf16)

    loop(S, project)

    def turn(i):
        nt[:, at(i, 256)] = nb[at(i, 256), :].T

    loop(T // 256, turn)
    for m in moves[3:8]:
        m.wait()
    for i in range(1, lines):
        for c in weights(i):
            c.wait_recv()

    @pl.when(ps > 0)
    def _():
        for s in range(S):
            halo(s).wait_recv()

    def project_state(s):
        both = mm(nb[at(s, L), :], wst[...], NT)
        pad[s, HALO:, C:] = both[:, 0 : 2 * Q].astype(bf16)
        sg[at(s, L), :] = both[:, 2 * Q :]
        edge, unused = normalize(xh[at(s, HALO), :].astype(f32), gain[...])
        pad[s, 0:HALO, 0:C] = mm(edge, wv[...]).astype(bf16)
        pad[s, 0:HALO, C:] = mm(edge, wst[0 : 2 * Q, :], NT).astype(bf16)

    loop(S, project_state)
    cw[:, 0:C] = cwv[...]
    cw[:, C : C + Q] = cwt[0:Q, :].T[0:8]
    cw[:, C + Q :] = cwt[Q:, :].T[0:8]

    for s in range(S):

        def conv_rows(r):
            for lo in range(0, W, 256):
                lanes = slice(lo, lo + 256)
                w = pad[s, pl.ds(pl.multiple_of(r * TILE, TILE), TILE + HALO), lanes].astype(f32)
                v = cw[4:5, lanes] + cw[0:1, lanes] * w[13 : 13 + TILE]
                for k in range(1, 4):
                    v = v + cw[k : k + 1, lanes] * w[13 + k : 13 + k + TILE]
                g = jax.nn.sigmoid(v)
                rows = at(r + s * (L // TILE), TILE)
                act[rows, lanes] = (v * g).astype(bf16)
                slope[rows, lanes] = g * (1.0 + v * (1.0 - g))

        loop(L // TILE, conv_rows)

    def steps(c):
        z = sg[at(c, Q), :] + hp[0:1, :]
        d = jax.nn.softplus(z)
        dt[at(c, Q), :] = d
        sg[at(c, Q), :] = jax.nn.sigmoid(z)
        run = mm(triangle(lambda i, j: i >= j), d * hp[1:2, :], precision=HI)
        cum[at(c, Q), :] = run
        cum_t[:, at(c, Q)] = run.T[0:8]
        dt_t[:, at(c, Q)] = d.T[0:8]

    loop(T // Q, steps)
    for s in range(S):
        st[...] = jnp.zeros_like(st)
        tot[s] = jnp.zeros((8, Q), f32)

        def chunk(k):
            c = s * NC + k
            run = cum[at(c, Q), :]
            last = run[Q - 1 : Q, :]
            tail = mm(jnp.exp(last - run) * dt[at(c, Q), :], e[...], precision=HI)
            xt = act[at(c, Q), 0:C].astype(f32) * tail
            entry[c] = st[...]
            st[...] = st[...] * row_of(jnp.exp(last), e[...]) + mm2(
                act[at(c, Q), C : C + Q], xt, TN
            )
            tot[s] += jnp.broadcast_to(last, (8, Q))

        loop(NC, chunk)
        fin[s] = st[...].astype(bf16)
    relay = Relay((fin, tot), (slots, slots_t), f_s, f_r, seqs, 1)
    relay.start()

    def weights_of(h, here, causal):
        gap = cum[here, h : h + 1] - cum_t[h : h + 1, here]
        return jnp.exp(jnp.where(causal, gap, -1e30)) * dt_t[h : h + 1, here]

    def within(c):
        here = at(c, Q)
        scores = mm(act[here, C + Q :], act[here, C : C + Q], NT)
        causal = iota((Q, Q), 0) >= iota((Q, Q), 1)
        upper = iota((Q, Q), 1) >= 64
        for p in range(C // Q):
            xp = act[here, p * Q : (p + 1) * Q]
            y = jnp.zeros((Q, Q), f32)
            for o in range(2):
                m = (scores * weights_of(2 * p + o, here, causal)).astype(bf16)
                y = y + mm(m, jnp.where(upper == bool(o), xp, jnp.zeros_like(xp)))
            ys[here, p * Q : (p + 1) * Q] = y

    loop(T // Q, within)
    moves[8].wait()
    moves[9].wait()

    def cotangent(i):
        dy[at(i, 512), :] = mm(cot[at(i, 512), :], wo[...], NT)

    loop(T // 512, cotangent)
    relay.gather(chained, e)

    for s in range(S):
        off[...] = jnp.zeros_like(off)

        def across(k):
            c = s * NC + k
            here = at(c, Q)
            si = entry[c] + row_of(jnp.exp(off[0:1, :]), e[...]) * chained[s]
            entry[c] = si
            run = cum[here, :]
            work[0] = mm(jnp.exp(run), e[...], precision=HI) * mm2(
                act[here, C + Q :], si
            )
            off[...] += jnp.broadcast_to(run[Q - 1 : Q, :], (8, Q))

            def tile(r):
                rows = at(c * (Q // TILE) + r, TILE)
                y = ys[rows, :] + work[0, at(r, TILE), :]
                ys[rows, :] = y
                m = y + sk[...] * act[rows, 0:C].astype(f32)
                g = gate[rows, :].astype(f32)
                gated = m * (g * jax.nn.sigmoid(g))
                a = jnp.sum(gated * gated, axis=1, keepdims=True)
                b = jnp.sum(dy[rows, :] * gg[...] * gated, axis=1, keepdims=True)
                lane = iota((TILE, Q), 1)
                stats[at(r, TILE), :] = jnp.where(lane == 0, a, jnp.where(lane == 1, b, 0.0))

            loop(Q // TILE, tile)
            stats_t[:, here] = stats[...].T[0:8]

        loop(NC, across)

    def stat(i):
        return remote(stats_t, stats_in.at[i - 1], st_s.at[i - 1], st_r.at[i - 1], head=line(i))

    for i in range(1, lines):
        stat(i).start()
    relay.finish()
    sums[...] = jnp.zeros_like(sums)
    for i in range(1, lines):
        stat(i).wait_recv()

    fold1 = Fold(part1, near1, far1, [z1.at[j] for j in range(4)], tiles)
    for s in range(S):

        def gate_back(k):
            c = s * NC + k
            here = at(c, Q)
            t = stats_t[:, here]
            for i in range(1, lines):
                t = t + stats_in[i - 1, :, here]
            t = t.T
            rms = lax.rsqrt(t[:, 0:1] / full + EPS)
            tt[:, 0:1] = rms
            tt[:, 1:2] = rms * rms * rms * (t[:, 1:2] / full)

            def tile(r):
                rows = at(c * (Q // TILE) + r, TILE)
                near = at(r, TILE)
                rm, co = tt[near, 0:1], tt[near, 1:2]
                x = act[rows, 0:C].astype(f32)
                m = ys[rows, :] + sk[...] * x
                g = gate[rows, :].astype(f32)
                sig = jax.nn.sigmoid(g)
                ga = g * sig
                gated = m * ga
                scaled_rows = gated * rm
                gn[rows, :] = (scaled_rows * gg[...]).astype(bf16)
                d = dy[rows, :]
                dgd = rm * (d * gg[...]) - gated * co
                dmix = dgd * ga
                dg[rows, :] = (dgd * m * (sig * (1.0 + g * (1.0 - sig)))).astype(bf16)
                dy[rows, :] = dmix
                sums[0:8, :] += fold8(d * scaled_rows)
                sums[8:16, :] += fold8(dmix * x)

            loop(Q // TILE, tile)

        loop(NC, gate_back)
        part1[s * L : (s + 1) * L, :] = mm(gn[s * L : (s + 1) * L, :], wo[...]).astype(bf16)
        fold1.begin(s * (tiles // S), tiles // S)

    def spread_dy(c):
        return mm(jnp.exp(cum[at(c, Q), :]), e[...], precision=HI) * dy[at(c, Q), :]

    for s in range(S):
        st[...] = jnp.zeros_like(st)

        def back(k):
            c = s * NC + NC - 1 - k
            last = cum[pl.ds(pl.multiple_of(c * Q + Q - 8, 8), 8), :][7:8]
            later[c] = st[...]
            st[...] = st[...] * row_of(jnp.exp(last), e[...]) + mm2(
                act[at(c, Q), C + Q :], spread_dy(c), TN
            )

        loop(NC, back)
        fin[s] = st[...].astype(bf16)
    relay2 = Relay((fin, tot), (slots, slots_t), b_s, b_r, seqs, -1)
    relay2.start()

    def outer(i):
        half = mm(gn[...], cot[:, at(i, 512)], TN)
        gr[0, at(i, 512), :] = half.astype(bf16)

    loop(D // 512, outer)

    def outer2(i):
        gr[1, at(i, 512), :] = mm(nt[at(i, 512), :], dg[...]).astype(bf16)

    loop(D // 512, outer2)
    HG = D // 2
    PR = HG // seqs

    def pair(k):
        return remote(gr.at[k, at(other, HG)], gr_in.at[k], ga_s.at[k], ga_r.at[k], sample=other)

    pair(0).start()
    pair(1).start()
    relay2.gather(chained, e)
    half = tiles // S

    hsums[...] = jnp.zeros_like(hsums)
    for s in range(S):
        off[...] = jnp.zeros_like(off)

        def state_back(k):
            kk = NC - 1 - k
            c = s * NC + kk
            here = at(c, Q)
            run = cum[here, :]
            last = run[Q - 1 : Q, :]
            ds = later[c] + row_of(jnp.exp(off[0:1, :]), e[...]) * chained[s]
            off[...] += jnp.broadcast_to(last, (8, Q))
            upper = iota((Q, Q), 1) >= 64
            causal = iota((Q, Q), 0) >= iota((Q, Q), 1)
            b, r = act[here, C : C + Q], act[here, C + Q :]
            scores = mm(r, b, NT)
            dsc = jnp.zeros((Q, Q), f32)
            for p in range(C // Q):
                lanes = slice(p * Q, (p + 1) * Q)
                xp = act[here, lanes]
                dyp = dy[here, lanes].astype(bf16)
                dyl = (dy[here, lanes] - dyp.astype(f32)).astype(bf16)
                dx = jnp.zeros((Q, Q), f32)
                for o in range(2):
                    keep = upper == bool(o)
                    dym = jnp.where(keep, dyp, jnp.zeros_like(dyp))
                    dyn = jnp.where(keep, dyl, jnp.zeros_like(dyl))
                    w = weights_of(2 * p + o, here, causal)
                    dsc = dsc + (mm(dym, xp, NT) + mm(dyn, xp, NT)) * w
                    dx = dx + mm((scores * w).astype(bf16), dym, TN)
                work[0, :, lanes] = dx
            d = dt[here, :]
            work[2] = mm(jnp.exp(last - run) * d, e[...], precision=HI)
            work[1] = work[2] * mm2(b, ds)
            bf, rf = b.astype(f32), r.astype(f32)
            d_read = mm(dsc, bf, precision=HI) + mm(spread_dy(c), entry[c], NT, HI)
            d_in = mm(dsc, rf, TN, HI) + mm(act[here, 0:C].astype(f32) * work[2], ds, NT, HI)
            slope[here, C : C + Q] = d_in * slope[here, C : C + Q]
            slope[here, C + Q :] = d_read * slope[here, C + Q :]

            def tile(i):
                rows = at(c * (Q // TILE) + i, TILE)
                near = at(i, TILE)
                x = act[rows, 0:C].astype(f32)
                g = dy[rows, :]
                a, o = work[0, near, :], work[1, near, :]
                work[3, near, :] = g.astype(bf16).astype(f32) * ys[rows, :] - x * a
                work[4, near, :] = x * o
                both = a + o
                work[5, near, :] = x * both
                slope[rows, 0:C] = (both + sk[...] * g) * slope[rows, 0:C]

            loop(Q // TILE, tile)
            ha = mm(work[3], e[...], NT, HI)
            hb = mm(work[4], e[...], NT, HI)
            hc = mm(work[5], e[...], NT, HI)
            crossing = mm(fold8(entry[c] * ds), e[...], NT, HI)
            crossing = jnp.sum(crossing, axis=0, keepdims=True) * jnp.exp(last)
            dlog = (
                mm(triangle(lambda i, j: i <= j), ha, precision=HI)
                + mm(triangle(lambda i, j: i > j), hb, precision=HI)
                + crossing
            )
            g = sg[here, :]
            ratio = jnp.where(d > 1e-30, g / jnp.maximum(d, 1e-30), 1.0)
            rate = hp[1:2, :]
            draw = rate * dlog * g + hc * ratio
            dcs[here, 2 * Q :] = draw.astype(bf16)
            hsums[0:8, :] += fold8(draw)
            hsums[8:16, :] += fold8(rate * dlog * d)
            if s == 0:
                for j in range(half // NC):
                    fold1.one(k * (half // NC) + j)
            else:
                for j in range(half // NC):
                    fold1.one(half + k * (half // NC) + j)
                    fold1.two(k * (half // NC) + j)

        loop(NC, state_back)
        edge8[s] = slope[s * L : s * L + 8, :]

        def next_rows(s):
            return remote(edge8.at[s], nx.at[s], nx_s.at[s], nx_r.at[s], seq=ps - 1)

        @pl.when(ps > 0)
        def _():
            next_rows(s).start()

    def settle(k):
        pair(k).wait_recv()

        def tile(i):
            r = pl.ds(pl.multiple_of(pc * HG + i * TILE, TILE), TILE)
            v = gr[k, r, :].astype(f32) + gr_in[k, at(i, TILE), :].astype(f32)
            gr[k, r, :] = v.astype(bf16)

        loop(HG // TILE, tile)

    def piece(k, i):
        r = pl.ds(pl.multiple_of(pc * HG + ring(i) * PR, PR), PR)
        return remote(gr.at[k, r], gr_pieces.at[k, i - 1], gb_s.at[k, i - 1], gb_r.at[k, i - 1], seq=ring(i))

    for k in range(2):
        settle(k)
        for i in range(1, seqs):
            piece(k, i).start()

    @pl.when(ps == seqs - 1)
    def _():
        nx[...] = jnp.zeros_like(nx)

    @pl.when(ps < seqs - 1)
    def _():
        for s in range(S):
            next_rows(s).wait_recv()

    acc[...] = jnp.zeros_like(acc)
    LT = L // TILE
    for s in range(S):

        def conv_back(r, last):
            for lo in range(0, W, 256):
                lanes = slice(lo, lo + 256)
                if last:
                    w = jnp.concatenate([slope[(s + 1) * L - TILE : (s + 1) * L, lanes], nx[s, :, lanes]], axis=0)
                else:
                    w = slope[pl.ds(pl.multiple_of(s * L + r * TILE, TILE), TILE + 8), lanes]
                u = pad[s, pl.ds(pl.multiple_of(r * TILE, TILE), TILE + HALO), lanes].astype(f32)
                d = w[0:TILE]
                v = cw[3:4, lanes] * d
                for k in range(3):
                    v = v + cw[k : k + 1, lanes] * w[3 - k : 3 - k + TILE]
                rows = at(r + s * LT, TILE)
                if lo < C:
                    gate[rows, lanes] = v.astype(bf16)
                else:
                    dcs[rows, lo - C : lo - C + 256] = v.astype(bf16)
                for k in range(4):
                    acc[8 * k : 8 * k + 8, lanes] += fold8(d * u[13 + k : 13 + k + TILE])
                acc[32:40, lanes] += fold8(d)

        loop(LT - 1, lambda r: conv_back(r, False))
        conv_back(LT - 1, True)
        for j in range(half // 2):
            fold1.two(half + s * (half // 2) + j)

    nsums[...] = jnp.zeros_like(nsums)
    fold2 = Fold(part2, near2, far2, [z2.at[j] for j in range(4)], tiles)

    def into(s):
        rows = at(s, 256)
        v = (
            mm(dg[rows, :], wg[...], NT)
            + mm(gate[rows, :], wv[...], NT)
            + mm(dcs[rows, :], wst[...])
        )
        part2[rows, :] = v.astype(bf16)
        nsums[...] += fold8(v * xb[rows, :].astype(f32) * inv[rows, 0:1])
        per = tiles * 256 // T
        fold2.begin(s * per, per)

    loop(T // 256, into)

    def outer3(i):
        gr[2, at(i, 512), :] = mm(nt[at(i, 512), :], gate[...]).astype(bf16)

    loop(D // 512, outer3)
    pair(2).start()
    for k in range(D // Q):
        t = mm(nt[k * Q : (k + 1) * Q, :], dcs[...])
        for j in range(2):
            later[j * DC + k * Q // C, :, k * Q % C : k * Q % C + Q] = t[:, j * Q : (j + 1) * Q].T
        row = 8 + 8 * (k * Q // C)
        small[row : row + 8, k * Q % C : k * Q % C + Q] = t[:, 2 * Q :].T[0:8]

    SR = Q // seqs
    keep_state = at(pc, DC)

    def state_pair():
        return remote(later.at[at(other, DC)], sg_in, sa_s, sa_r, sample=other)

    state_pair().start()
    for k in range(5):
        row = jnp.sum(acc[8 * k : 8 * k + 8, :], axis=0, keepdims=True)
        small[k : k + 1, :] = row[:, 0:C]
        smallz[k : k + 1, 0 : 2 * Q] = row[:, C:]
        smallz[k : k + 1, 2 * Q :] = jnp.zeros((1, C - 2 * Q), f32)
    small[5:6, :] = jnp.sum(sums[0:8, :], axis=0, keepdims=True)
    small[6:7, :] = jnp.sum(sums[8:16, :], axis=0, keepdims=True)
    small[7:8, :] = jnp.zeros((1, C), f32)
    small[7:8, 0:Q] = jnp.sum(hsums[0:8, :], axis=0, keepdims=True)
    small[7:8, Q : 2 * Q] = jnp.sum(hsums[8:16, :], axis=0, keepdims=True)
    ngrad = jnp.sum(nsums[...], axis=0, keepdims=True)
    for j in range(D // C):
        smallz[5 + j : 6 + j, :] = ngrad[:, j * C : (j + 1) * C]
    smallz[7:8, :] = jnp.zeros((1, C), f32)

    def to_line(i):
        return remote(smallz, smallz_in.at[i - 1], m1_s.at[i - 1], m1_r.at[i - 1], head=line(i))

    for i in range(1, lines):
        to_line(i).start()
    loop(4, lambda i: fold2.one(i))
    settle(2)
    for i in range(1, seqs):
        piece(2, i).start()
    state_pair().wait_recv()
    later[keep_state] = later[keep_state] + sg_in[...]

    def state_piece(i):
        return remote(later.at[keep_state, at(ring(i), SR)], sg_pieces.at[i - 1], sb_s.at[i - 1], sb_r.at[i - 1], seq=ring(i))

    for i in range(1, seqs):
        state_piece(i).start()
    loop(4, lambda i: fold2.one(4 + i))
    total = smallz[...]
    for i in range(1, lines):
        to_line(i).wait_recv()
        total = total + smallz_in[i - 1]
    small[24:32, :] = total

    def to_core():
        return remote(small, small_two.at[0], m2_s.at[seqs - 1], m2_r.at[seqs - 1], sample=other)

    def to_peer(i):
        return remote(small_two.at[1], small_in.at[i - 1], m2_s.at[i - 1], m2_r.at[i - 1], seq=ring(i))

    to_core().start()
    loop(4, lambda i: fold2.two(0 + i))

    to_core().wait_recv()
    small_two[1] = small[...] + small_two[0]
    for i in range(1, seqs):
        to_peer(i).start()

    for k in range(3):
        for i in range(1, seqs):
            piece(k, i).wait_recv()

        def tile(j):
            r = at(j, TILE)
            v = gr[k, pl.ds(pl.multiple_of(pc * HG + ps * PR + j * TILE, TILE), TILE), :].astype(f32)
            for i in range(1, seqs):
                v = v + gr_pieces[k, i - 1, r, :].astype(f32)
            gr_sum[k, r, :] = v.astype(bf16)
            grads[k, pl.ds(pl.multiple_of(pc * HG + ps * PR + j * TILE, TILE), TILE), :] = v.astype(bf16)

        loop(PR // TILE, tile)

    def spread(k, i):
        r = pl.ds(pl.multiple_of(pc * HG + ps * PR, PR), PR)
        return remote(gr_sum.at[k], grads.at[k, r], gc_s.at[k, i - 1], gc_r.at[k, i - 1], seq=ring(i))

    def hand(k, i):
        q = lax.rem(ps + seqs - i, seqs)
        r = pl.ds(pl.multiple_of(pc * HG + q * PR, PR), PR)
        src = gr_sum.at[k] if i == 0 else grads.at[k, r]
        return remote(src, grads.at[k, r], gd_s.at[k, i], gd_r.at[k, i], sample=other)

    for k in range(3):
        for i in range(1, seqs):
            spread(k, i).start()
        hand(k, 0).start()
    loop(4, lambda i: fold2.one(8 + i))
    loop(4, lambda i: fold2.two(4 + i))

    for i in range(1, seqs):
        state_piece(i).wait_recv()
    v = later[keep_state, at(ps, SR), :]
    for i in range(1, seqs):
        v = v + sg_pieces[i - 1]
    sg_sum[0] = v
    owner = (ps * SR) // own

    def to_owner(i):
        return remote(sg_sum.at[0], sg_line.at[i - 1], sz_s.at[i - 1], sz_r.at[i - 1], head=line(i))

    for i in range(1, lines):

        @pl.when(line(i) == owner)
        def _():
            to_owner(i).start()

    loop(4, lambda i: fold2.one(12 + i))
    loop(4, lambda i: fold2.two(8 + i))
    span = max(own // SR, 1)

    def place_row(q, core):
        return pl.ds(pl.multiple_of(core * own + lax.rem(q * SR, own), SR), SR)

    def state_out_to(i):
        return remote(sg_sum.at[1], state_out.at[:, place_row(ps, pc)], sc_s.at[i - 1], sc_r.at[i - 1], seq=ring(i))

    def state_hand(j, src):
        q = ph * span + j
        return remote(src, state_out.at[:, place_row(q, pc)], sd_s.at[j], sd_r.at[j], sample=other)

    @pl.when(ph == owner)
    def _():
        t = sg_sum[0]
        for i in range(1, lines):
            to_owner(i).wait_recv()
            t = t + sg_line[i - 1]
        sg_sum[1] = t
        state_out[:, place_row(ps, pc), :] = t
        for i in range(1, seqs):
            state_out_to(i).start()

    for j in range(span):
        q = ph * span + j

        @pl.when(q == ps)
        def _():
            state_hand(j, sg_sum.at[1]).start()

        for i in range(1, seqs):

            @pl.when(ring(seqs - i) == q)
            def _():
                remote(
                    sg_sum.at[1], state_out.at[:, place_row(q, pc)], sc_s.at[i - 1], sc_r.at[i - 1], seq=ring(i)
                ).wait_recv()
                state_hand(j, state_out.at[:, place_row(q, pc)]).start()

    for k in range(3):
        for i in range(1, seqs):
            q = lax.rem(ps + seqs - i, seqs)
            r = pl.ds(pl.multiple_of(pc * HG + q * PR, PR), PR)
            remote(gr_sum.at[k], grads.at[k, r], gc_s.at[k, i - 1], gc_r.at[k, i - 1], seq=ring(i)).wait_recv()
            hand(k, i).start()
    loop(4, lambda i: fold2.two(12 + i))
    total = small_two[1]
    for i in range(1, seqs):
        to_peer(i).wait_recv()
        total = total + small_in[i - 1]
    small_out[...] = total

    fold1.end()
    fold2.end()
    relay2.finish()
    for i in range(1, lines):
        for c in weights(i):
            c.wait_send()
        stat(i).wait_send()
        to_line(i).wait_send()

        @pl.when(line(i) == owner)
        def _():
            to_owner(i).wait_send()

    @pl.when(ps < seqs - 1)
    def _():
        for s in range(S):
            halo(s).wait_send()

    @pl.when(ps > 0)
    def _():
        for s in range(S):
            next_rows(s).wait_send()

    for k in range(3):
        pair(k).wait_send()
        for i in range(1, seqs):
            piece(k, i).wait_send()
            spread(k, i).wait_send()
        for i in range(seqs):
            q = lax.rem(ps + seqs - i, seqs)
            r = pl.ds(pl.multiple_of(other * HG + q * PR, PR), PR)
            remote(gr_sum.at[k], grads.at[k, r], gd_s.at[k, i], gd_r.at[k, i], sample=other).wait()
    state_pair().wait_send()
    for i in range(1, seqs):
        state_piece(i).wait_send()

        @pl.when(ph == owner)
        def _():
            state_out_to(i).wait_send()

    for j in range(span):
        q = ph * span + j
        remote(sg_sum.at[1], state_out.at[:, place_row(q, other)], sd_s.at[j], sd_r.at[j], sample=other).wait()
    to_core().wait_send()
    for i in range(1, seqs):
        to_peer(i).wait_send()


def finish(x, cot, gain, dn, outs, gr, block_out, input_grad, gate_grad, value_grad, out_grad):
    def tile(i):
        r = at(i, TILE)
        v = x[r, :].astype(f32)
        block_out[r, :] = (v + outs[r, :].astype(f32)).astype(bf16)
        s = dn[r, :].astype(f32) * gain[...]
        i1 = lax.rsqrt(jnp.mean(v * v, axis=1, keepdims=True) + EPS)
        m = jnp.mean(s * v, axis=1, keepdims=True)
        input_grad[r, :] = cot[r, :].astype(f32) + i1 * s - v * (i1 * i1 * i1 * m)

    loop(x.shape[0] // TILE, tile)
    half = gr.shape[1] // 2
    out_grad[:, 0:half] = gr[0, 0:half, :].astype(f32)
    out_grad[:, half:] = gr[0, half:, :].astype(f32)
    gate_grad[...] = gr[1].astype(f32)
    value_grad[...] = gr[2].astype(f32)


def per_device(
    block_in, out_cotangent, norm_gain, gate_proj, value_proj, state_proj, step_proj,
    conv_value, conv_state, conv_value_bias, conv_state_bias, step_bias, decay_log,
    skip_gain, gated_gain, out_proj,
):
    S, L, D = block_in.shape
    T = S * L
    heads = step_proj.shape[1]
    C = gate_proj.shape[1]
    own = state_proj.shape[2]
    W = C + 2 * Q
    NCH = T // Q
    seqs, lines = lax.axis_size("seq"), lax.axis_size("head")
    tiles = 16
    H = D // 2
    PR = H // seqs
    SR = Q // seqs
    x = block_in.reshape(T, D)
    cot = out_cotangent.reshape(T, D)
    spt = state_proj.transpose(0, 2, 1).reshape(2 * own, D)
    stp = jnp.pad(step_proj.T, ((0, Q - heads), (0, 0)))
    taps = jnp.concatenate([conv_state, conv_state_bias[None]], axis=0)
    cst = jnp.pad(taps.transpose(1, 2, 0).reshape(2 * own, 5), ((0, 0), (0, Q - 5)))
    cwv = jnp.pad(jnp.concatenate([conv_value, conv_value_bias[None]], axis=0), ((0, 3), (0, 0)))
    hp = jnp.pad(jnp.stack([step_bias, -jnp.exp(decay_log)]), ((0, 6), (0, Q - heads)))
    sk = jnp.repeat(skip_gain, C // heads)[None]
    gg = gated_gain[None]
    gain = norm_gain[None]
    vm = pl.BlockSpec(memory_space=pltpu.VMEM)
    hbm = pl.BlockSpec(memory_space=pl.ANY)
    dma = pltpu.SemaphoreType.DMA
    n1, l1 = seqs - 1, lines - 1
    V = pltpu.VMEM
    scratch = [
        V((T, D), bf16), V((T, D), bf16), V((D, C), bf16), V((D, C), bf16), V((3 * Q, D), bf16),
        V((C, D), bf16), V((2 * Q, Q), f32), V((8, W), f32), V((S * HALO, D), bf16),
        V((D, T), bf16), V((T, Q), f32), V((T, C), bf16), V((S, HALO + L, W), bf16), V((T, W), f32),
        V((T, W), bf16), V((T, Q), f32), V((T, Q), f32), V((T, Q), f32), V((8, T), f32), V((8, T), f32),
        V((NCH, Q, C), f32), V((T, C), f32), V((T, C), f32), V((T, C), bf16), V((T, C), bf16),
        V((NCH, Q, C), f32),
        V((T, 3 * Q), bf16), V((Q, C), f32), V((Q, C), f32), V((6, Q, C), f32),
        V((8, Q), f32), V((Q, Q), f32), V((Q, Q), f32), V((8, T), f32), V((l1, 8, T), f32),
        V((S, Q, C), bf16), V((S, 8, Q), f32), V((seqs, S, Q, C), bf16), V((seqs, S, 8, Q), f32),
        V((S, Q, C), f32),
        V((T, D), bf16), V((T, D), bf16), V((T, D), bf16), V((T, D), bf16),
        V((3, D, C), bf16), V((3, H, C), bf16), V((3, n1, PR, C), bf16), V((3, PR, C), bf16),
        V((D // C, Q, C), f32), V((n1, D // C, SR, C), f32), V((l1, D // C, SR, C), f32),
        V((2, D // C, SR, C), f32),
        V((40, W), f32), V((16, Q), f32), V((16, C), f32), V((8, D), f32), V((8, C), f32),
        V((l1, 8, C), f32), V((32, C), f32), V((2, 32, C), f32), V((n1, 32, C), f32), V((S, 8, W), f32), V((S, 8, W), f32),
        dma((10,)), dma((2, S)), dma((4, l1)), dma((4, l1)), dma((2, n1)), dma((2, n1)),
        dma((2, n1)), dma((2, n1)), dma((l1,)), dma((l1,)), dma((S,)), dma((S,)),
        dma((4, tiles)), dma((4, tiles)), dma((3,)), dma((3,)), dma((3, n1)), dma((3, n1)),
        dma((3, n1)), dma((3, n1)), dma((3, seqs)), dma((3, seqs)),
        dma, dma, dma((n1,)), dma((n1,)), dma((l1,)), dma((l1,)), dma((n1,)), dma((n1,)),
        dma((max(own // SR, 1),)), dma((max(own // SR, 1),)), dma((l1,)), dma((l1,)), dma((seqs,)), dma((seqs,)),
    ]
    outs, dnorm, grads, state_out, small = pl.pallas_call(
        functools.partial(block, (S, L, seqs, lines, tiles)),
        out_shape=[
            jax.ShapeDtypeStruct((T, D), bf16), jax.ShapeDtypeStruct((T, D), bf16),
            jax.ShapeDtypeStruct((3, D, C), bf16), jax.ShapeDtypeStruct((D // C, 2 * own, C), f32),
            jax.ShapeDtypeStruct((32, C), f32),
        ],
        in_specs=[hbm, hbm, vm, hbm, hbm, hbm, hbm, hbm, hbm, vm, vm, vm, vm],
        out_specs=[vm] * 5,
        scratch_shapes=scratch,
        name="block",
        compiler_params=pltpu.CompilerParams(
            collective_id=0, has_side_effects=True, vmem_limit_bytes=67043328
        ),
    )(x, cot, gain, gate_proj, value_proj, spt, stp, out_proj, cst, cwv, hp, sk, gg)
    block_out, input_grad, gate_grad, value_grad, out_grad = pl.pallas_call(
        finish,
        out_shape=[
            jax.ShapeDtypeStruct((T, D), bf16), jax.ShapeDtypeStruct((T, D), f32),
            jax.ShapeDtypeStruct((D, C), f32), jax.ShapeDtypeStruct((D, C), f32),
            jax.ShapeDtypeStruct((C, D), f32),
        ],
        in_specs=[vm] * 6,
        out_specs=[vm] * 5,
        name="finish",
        compiler_params=pltpu.CompilerParams(vmem_limit_bytes=60 * 2**20),
    )(x, cot, gain, dnorm, outs, grads)
    ph = lax.axis_index("head")
    state_grad = state_out.reshape(D // C, 2, own, C).transpose(1, 0, 3, 2).reshape(2, D, own)
    step_grad = small[8:24].reshape(D // C, heads, C).transpose(0, 2, 1).reshape(D, heads)
    cs = lax.dynamic_slice_in_dim(small[24:29, 0 : 2 * Q].reshape(5, 2, Q), ph * own, own, 2)
    return (
        block_out.reshape(S, L, D), input_grad.reshape(S, L, D), small[29:31].reshape(D), gate_grad,
        value_grad, state_grad, step_grad, small[0:4], cs[0:4], small[4], cs[4], small[7, 0:heads],
        small[7, Q : Q + heads], jnp.sum(small[6].reshape(heads, C // heads), axis=1), small[5], out_grad,
    )


def solution(mesh):
    tokens = P("sample", "seq", None)
    params = (
        P(), P(None, "head"), P(None, "head"), P(None, None, "head"), P(None, "head"),
        P(None, "head"), P(None, None, "head"), P("head"), P(None, "head"), P("head"),
        P("head"), P("head"), P("head"), P("head", None),
    )
    return jax.shard_map(
        per_device,
        mesh=mesh,
        in_specs=(tokens, tokens) + params,
        out_specs=(tokens, tokens) + params,
        check_vma=False,
    )
```

time: 865 us -> 260 us (0.30)
  waiting for transfers between devices: 360 us -> 0 us
  Pallas kernels: 0 us -> 240 us
  matrix products: 155 us -> 0 us
  local copies, waits for them, and re-layouts: 138 us -> 13.9 us
  other arithmetic: 107 us -> 4.58 us
  blocking collectives: 71.6 us -> 0 us
  between operations: 15.9 us -> 0.67 us
    psum x2 -> x0, waiting for transfers between devices: 251 us -> none  [the longest x1 140 us: per_device(): d_normed = lax.psum(partial_normed, 'head')]
    pallas_call x0 -> x2, Pallas kernels: none -> 240 us  [the longest x1 227 us: per_device(): pl.pallas_call(functools.partial(block, (S, L, seqs, lines, tiles)), out_...]
    dot_general x46 -> x0, matrix products: 153 us -> none  [the longest x6 42.7 us: advance(): within = jnp.einsum('tsh,shp->thp', mixing, block_values, precision=highest)]
    psum x3 -> x0, blocking collectives: 46.1 us -> none  [the longest x1 26.1 us: per_device(): lax.psum((norm_grad, gate_grad, value_grad, state_grad, step_grad, conv_v...]
    reduce_scatter x1 -> x0, waiting for transfers between devices: 44.5 us -> none  [per_device(): lax.psum_scatter(jnp.dot(gated_norm, out_proj, preferred_element_type=jnp...]
    unnamed x8 -> x0, waiting for transfers between devices: 31.9 us -> none
    all_gather x3 -> x0, waiting for transfers between devices: 27.1 us -> none  [the longest x2 15.5 us: entering(): gathered = jax.tree.map(lambda a: lax.all_gather(a, axis), part)]
    unnamed x139 -> x2, local copies, waits for them, and re-layouts: 27.6 us -> 1.32 us
  transfers between devices with their start and end apart: 9 -> 0, of which waited for: 8 -> 0; matrix products, arithmetic and copies ran while one was open for 15% -> 0% of each run, Pallas kernels for 0% -> 0%
where the time goes in v1:
time: 260 us; the launch traced here: 259 us
  Pallas kernels  240 us (92%)
  local copies, waits for them, and re-layouts  13.9 us (5%)
  other arithmetic  4.58 us (2%)
    pallas_call x1, Pallas kernels, per_device(): pl.pallas_call(functools.partial(block, (S, L, seqs, lines, tiles)), out_...  227 us
    pallas_call x1, Pallas kernels, per_device(): pl.pallas_call(finish, out_shape=[jax.ShapeDtypeStruct((T, D), bf16), jax...  13.1 us

profile of v1, /device:TPU:0, one launch (start us, length us, event | category | flops | bytes accessed | tf_op | source)
XLA Modules:
  0.0 259.0 jit_solution(11922179283454281065)
XLA Ops:
  0.6 0.7 negate_bitcast_fusion
  1.3 1.3 select_maximum_fusion.1.hp
  2.6 0.7 broadcast_in_dim.18
  3.3 0.7 broadcast_in_dim_reshape.3.sk
  3.9 0.7 maximum_bitcast_fusion
  4.7 1.3 select_maximum_fusion.cwv
  6.0 0.1 copy.32
  6.1 0.6 pad.17.cst
  6.7 1.4 pad.16.stp
  8.1 226.7 %block.1 = (bf16[1024,1024]{1,0:T(8,128)(2,1)}, bf16[1024,1024]{1,0:T(8,128)(2,1)}, bf16[3,1024,512]{2,1,0:T(8,128)(2,1)}, f32[2,64,512]{2,1,0:T(8,128)}, f32[32,512]{1,0:T(8,128)}) custom-call(bf16[1024,1024]{1,0:T(8,128)(2,1)} %bitcast.39, bf16[1024,1024]{1,0:T(8,128)(2,1)} %bitcast.41, f32[1,1024]{1,0:T(1,128)} %bitcast.48, bf16[1024,512]{1,0:T(8,128)(2,1)} %wg_in.1, ...), custom_call_target="tpu_custom_call" | custom-call | tf_op jit(solution)/shard_map/block/pallas_call | solution.py:988
  234.8 1.2 slice_bitcast_fusion.1
  236.0 0.7 slice_bitcast_fusion
  236.8 0.6 copy.35
  237.4 1.4 fusion
  238.8 0.1 reshape_squeeze.3
  238.8 0.6 reduce_sum.9
  239.5 0.7 slice.36
  240.2 0.6 dynamic-slice_bitcast_fusion
  240.8 0.7 constant_dynamic-slice_fusion
  241.5 1.3 slice.35
  242.8 1.4 slice.34
  244.2 1.7 copy.34
  245.8 13.1 %finish.1 = (bf16[1024,1024]{1,0:T(8,128)(2,1)}, f32[1024,1024]{1,0:T(8,128)}, f32[1024,512]{1,0:T(8,128)}, f32[1024,512]{1,0:T(8,128)}, f32[512,1024]{1,0:T(8,128)}) custom-call(bf16[1024,1024]{1,0:T(8,128)(2,1)} %bitcast.40, bf16[1024,1024]{1,0:T(8,128)(2,1)} %bitcast.42, f32[1,1024]{1,0:T(1,128)} %bitcast.49, bf16[1024,1024]{1,0:T(8,128)(2,1)} %get-tuple-element.26.dn, ...), custom_call_target="tpu_custom_call" | custom-call | tf_op jit(solution)/shard_map/finish/pallas_call | solution.py:1003
  (1 shorter events, 0.0 us)

commit v2 on v1

--- a/solution.py
+++ b/solution.py
@@ -32,12 +32,13 @@
     return pl.ds(pl.multiple_of(i * n, n), n)
 
 
-def loop(count, body):
+def loop(count, body, each=1):
     def step(i, carry):
-        body(i)
+        for j in range(each):
+            body(i * each + j)
         return carry
 
-    lax.fori_loop(0, count, step, 0)
+    lax.fori_loop(0, count // each, step, 0)
 
 
 def iota(shape, axis):
@@ -116,6 +117,22 @@
             self.add(self.near, self.part, self.far, i)
             self.outward(i, self.near).start()
 
+    def step(self, j, lag=2):
+        if isinstance(j, int):
+            if j < self.tiles:
+                self.one(j)
+            if 0 <= j - lag < self.tiles:
+                self.two(j - lag)
+            return
+
+        @pl.when(j < self.tiles)
+        def _():
+            self.one(j)
+
+        @pl.when((j >= lag) & (j < self.tiles + lag))
+        def _():
+            self.two(j - lag)
+
     def end(self):
         @pl.when(self.inner)
         def _():
@@ -135,15 +152,18 @@
 
 
 class Relay:
-    def __init__(self, blocks, slots, send, recv, count, way):
-        self.blocks, self.slots, self.send, self.recv = blocks, slots, send, recv
+    def __init__(self, seq, blocks, slots, sems, count, way):
+        self.seq, self.blocks, self.slots, self.sems = seq, blocks, slots, sems
         self.count, self.way = count, way
         self.place = lax.axis_index("seq")
 
     def copies(self, d, source):
         to = self.place + self.way * d
         return [
-            remote(b, s.at[source], self.send.at[j, d - 1], self.recv.at[j, d - 1], seq=to)
+            remote(
+                b.at[self.seq], s.at[source, self.seq], self.sems.at[0, j, self.seq, d - 1],
+                self.sems.at[1, j, self.seq, d - 1], seq=to,
+            )
             for j, (b, s) in enumerate(zip(self.blocks, self.slots))
         ]
 
@@ -162,7 +182,8 @@
                     c.start()
 
     def gather(self, state, e):
-        state[...] = jnp.zeros_like(state)
+        q = self.seq
+        state[q] = jnp.zeros(state.shape[1:], f32)
         for d in range(self.count - 1, 0, -1):
 
             @pl.when(self.hears(d))
@@ -170,9 +191,8 @@
                 source = self.place - self.way * d
                 for c in self.copies(d, source):
                     c.wait_recv()
-                for s in range(state.shape[0]):
-                    decay = mm(jnp.exp(self.slots[1][source, s]), e[...], precision=HI)[0:1]
-                    state[s] = state[s] * decay + self.slots[0][source, s].astype(f32)
+                decay = mm(jnp.exp(self.slots[1][source, q]), e[...], precision=HI)[0:1]
+                state[q] = state[q] * decay + self.slots[0][source, q].astype(f32)
 
     def finish(self):
         for d in range(1, self.count):
@@ -185,16 +205,16 @@
 
 def block(
     dims,
-    x_in, cot_in, gain, wg_in, wv_in, spt, stp, wo_in, cst, cwv, hp, sk, gg,
+    x_in, cot_in, gain, wg_in, wv_in, spt, stp, wo_in, cs, csb, cv, cvb, sbias, dlog_in, skip, gg,
     outs, dnorm, grads, state_out, small_out,
-    xb, cot, wg, wv, wst, wo, cwt, cw, xh,
+    xb, cot, wg, wv, wst, wo, tapb, taps, cw, hp, sk, xh,
     nt, inv, gate, pad, slope, act, dt, sg, cum, cum_t, dt_t, entry, ys, dy, gn, dg, later,
     dcs, e, st, work, off, tt, stats, stats_t, stats_in,
     fin, tot, slots, slots_t, chained,
     part1, far1, part2, far2,
     gr, gr_in, gr_pieces, gr_sum, sg_in, sg_pieces, sg_line, sg_sum,
     acc, hsums, sums, nsums, smallz, smallz_in, small, small_two, small_in, nx, edge8,
-    load, halo_sem, wt_s, wt_r, f_s, f_r, b_s, b_r, st_s, st_r, nx_s, nx_r,
+    load, halo_sem, wt_s, wt_r, f_sem, b_sem, st_s, st_r, nx_s, nx_r,
     z1, z2, ga_s, ga_r, gb_s, gb_r, gc_s, gc_r, gd_s, gd_r,
     sa_s, sa_r, sb_s, sb_r, sz_s, sz_r, sc_s, sc_r, sd_s, sd_r, m1_s, m1_r, m2_s, m2_r,
 ):
@@ -223,21 +243,16 @@
     def ring(i):
         return lax.rem(ps + i, seqs)
 
-    moves = [
-        pltpu.make_async_copy(x_in, xb, load.at[0]),
-        pltpu.make_async_copy(wg_in, wg, load.at[1]),
-        pltpu.make_async_copy(wv_in, wv, load.at[2]),
-        pltpu.make_async_copy(stp, wst.at[pl.ds(2 * Q, Q)], load.at[3]),
-        pltpu.make_async_copy(spt.at[pl.ds(0, own)], wst.at[at(ph, own)], load.at[4]),
+    moves = [pltpu.make_async_copy(x_in.at[pl.ds(s * L, L)], xb.at[pl.ds(s * L, L)], load.at[s]) for s in range(S)]
+    moves += [
+        pltpu.make_async_copy(wg_in, wg, load.at[S]),
+        pltpu.make_async_copy(wv_in, wv, load.at[S + 1]),
+        pltpu.make_async_copy(spt.at[pl.ds(0, own)], wst.at[at(ph, own)], load.at[S + 2]),
         pltpu.make_async_copy(
-            spt.at[pl.ds(own, own)], wst.at[pl.ds(pl.multiple_of(Q + ph * own, own), own)], load.at[5]
+            spt.at[pl.ds(own, own)], wst.at[pl.ds(pl.multiple_of(Q + ph * own, own), own)], load.at[S + 3]
         ),
-        pltpu.make_async_copy(cst.at[pl.ds(0, own)], cwt.at[at(ph, own)], load.at[6]),
-        pltpu.make_async_copy(
-            cst.at[pl.ds(own, own)], cwt.at[pl.ds(pl.multiple_of(Q + ph * own, own), own)], load.at[7]
-        ),
-        pltpu.make_async_copy(cot_in, cot, load.at[8]),
-        pltpu.make_async_copy(wo_in, wo, load.at[9]),
+        pltpu.make_async_copy(cot_in, cot, load.at[S + 4]),
+        pltpu.make_async_copy(wo_in, wo, load.at[S + 5]),
     ]
     for m in moves:
         m.start()
@@ -246,6 +261,20 @@
         pl.semaphore_signal(barrier, inc=1, device_id=peer(i), device_id_type=MESH)
     for i in range(1, lines):
         pl.semaphore_signal(barrier, inc=1, device_id={"head": line(i)}, device_id_type=MESH)
+    heads = stp.shape[0]
+    tapb[...] = jnp.zeros_like(tapb)
+    hp[...] = jnp.zeros_like(hp)
+    for j in range(2):
+        tapb[0:4, j * own : (j + 1) * own] = cs[:, j, :]
+        tapb[4:5, j * own : (j + 1) * own] = csb[j : j + 1, :]
+    taps[ph] = tapb[...]
+    hp[0:1, 0:heads] = sbias[...]
+    hp[1:2, 0:heads] = -jnp.exp(dlog_in[...])
+    hp[2:3, 0:heads] = skip[...]
+    wst[2 * Q :, :] = jnp.zeros((Q, D), bf16)
+    wst[2 * Q : 2 * Q + heads, :] = stp[...]
+    e[...] = lane_heads(C // 64, C)
+    sk[...] = mm(hp[...], e[...], precision=HI)[2:3]
     pl.semaphore_wait(barrier, group - 1 + lines - 1)
 
     def halo(s):
@@ -263,73 +292,61 @@
     def _():
         xh[...] = jnp.zeros_like(xh)
 
-    def weights(i):
-        to = line(i)
-        low = at(ph, own)
-        high = pl.ds(pl.multiple_of(Q + ph * own, own), own)
-        parts = [
-            (spt.at[pl.ds(0, own)], wst.at[low]),
-            (spt.at[pl.ds(own, own)], wst.at[high]),
-            (cst.at[pl.ds(0, own)], cwt.at[low]),
-            (cst.at[pl.ds(own, own)], cwt.at[high]),
-        ]
+    def weights(i, source):
+        low = at(source, own)
+        high = pl.ds(pl.multiple_of(Q + source * own, own), own)
+        parts = [(spt.at[pl.ds(0, own)], wst.at[low]), (spt.at[pl.ds(own, own)], wst.at[high]), (tapb, taps.at[source])]
         return [
-            remote(a, b, wt_s.at[j, i - 1], wt_r.at[j, i - 1], head=to)
+            remote(a, b, wt_s.at[j, i - 1], wt_r.at[j, i - 1], head=line(i))
             for j, (a, b) in enumerate(parts)
         ]
 
     for i in range(1, lines):
-        for c in weights(i):
+        for c in weights(i, ph):
             c.start()
 
-    e[...] = lane_heads(C // 64, C)
-    moves[0].wait()
-
-    def norm_rows(r):
-        n, i = normalize(xb[at(r, TILE), :].astype(f32), gain[...])
-        nb[at(r, TILE), :] = n
-        inv[at(r, TILE), :] = jnp.broadcast_to(i, (TILE, Q))
-
-    loop(T // TILE, norm_rows)
-    moves[1].wait()
-    moves[2].wait()
-
-    def project(s):
-        n = nb[at(s, L), :]
-        gate[at(s, L), :] = mm(n, wg[...]).astype(bf16)
-        pad[s, HALO:, 0:C] = mm(n, wv[...]).astype(bf16)
-
-    loop(S, project)
-
-    def turn(i):
-        nt[:, at(i, 256)] = nb[at(i, 256), :].T
-
-    loop(T // 256, turn)
-    for m in moves[3:8]:
-        m.wait()
+    for s in range(S):
+        moves[s].wait()
+
+        def norm_rows(r):
+            rows = at(s * (L // 16) + r, 16)
+            v = xb[rows, :].astype(f32)
+            i = lax.rsqrt(jnp.mean(v * v, axis=1, keepdims=True) + EPS)
+            nb[rows, :] = (v * i * gain[...]).astype(bf16)
+            inv[rows, :] = jnp.broadcast_to(i, (16, Q))
+
+        loop(L // 16, norm_rows, 4)
+        if s == 0:
+            moves[S].wait()
+            moves[S + 1].wait()
+        seq_rows = slice(s * L, (s + 1) * L)
+        gate[seq_rows, :] = mm(nb[seq_rows, :], wg[...]).astype(bf16)
+        pad[s, HALO:, 0:C] = mm(nb[seq_rows, :], wv[...]).astype(bf16)
+    moves[S + 2].wait()
+    moves[S + 3].wait()
     for i in range(1, lines):
-        for c in weights(i):
+        for c in weights(i, line(lines - i)):
             c.wait_recv()
-
-    @pl.when(ps > 0)
-    def _():
-        for s in range(S):
+    cw[0:4, 0:C] = cv[...]
+    cw[4:5, 0:C] = cvb[...]
+    for h in range(lines):
+        for j in range(2):
+            cw[:, C + j * Q + h * own : C + j * Q + (h + 1) * own] = taps[h, :, j * own : (j + 1) * own]
+
+    relays, relays2 = [], []
+    for s in range(S):
+        seq_rows = slice(s * L, (s + 1) * L)
+        both = mm(nb[seq_rows, :], wst[...], NT)
+        pad[s, HALO:, C:] = both[:, 0 : 2 * Q].astype(bf16)
+        sg[seq_rows, :] = both[:, 2 * Q :]
+
+        @pl.when(ps > 0)
+        def _():
             halo(s).wait_recv()
 
-    def project_state(s):
-        both = mm(nb[at(s, L), :], wst[...], NT)
-        pad[s, HALO:, C:] = both[:, 0 : 2 * Q].astype(bf16)
-        sg[at(s, L), :] = both[:, 2 * Q :]
-        edge, unused = normalize(xh[at(s, HALO), :].astype(f32), gain[...])
+        edge, unused = normalize(xh[s * HALO : (s + 1) * HALO, :].astype(f32), gain[...])
         pad[s, 0:HALO, 0:C] = mm(edge, wv[...]).astype(bf16)
         pad[s, 0:HALO, C:] = mm(edge, wst[0 : 2 * Q, :], NT).astype(bf16)
-
-    loop(S, project_state)
-    cw[:, 0:C] = cwv[...]
-    cw[:, C : C + Q] = cwt[0:Q, :].T[0:8]
-    cw[:, C + Q :] = cwt[Q:, :].T[0:8]
-
-    for s in range(S):
 
         def conv_rows(r):
             for lo in range(0, W, 256):
@@ -345,18 +362,18 @@
 
         loop(L // TILE, conv_rows)
 
-    def steps(c):
-        z = sg[at(c, Q), :] + hp[0:1, :]
-        d = jax.nn.softplus(z)
-        dt[at(c, Q), :] = d
-        sg[at(c, Q), :] = jax.nn.sigmoid(z)
-        run = mm(triangle(lambda i, j: i >= j), d * hp[1:2, :], precision=HI)
-        cum[at(c, Q), :] = run
-        cum_t[:, at(c, Q)] = run.T[0:8]
-        dt_t[:, at(c, Q)] = d.T[0:8]
-
-    loop(T // Q, steps)
-    for s in range(S):
+        def steps(k):
+            c = s * NC + k
+            z = sg[at(c, Q), :] + hp[0:1, :]
+            d = jax.nn.softplus(z)
+            dt[at(c, Q), :] = d
+            sg[at(c, Q), :] = jax.nn.sigmoid(z)
+            run = mm(triangle(lambda i, j: i >= j), d * hp[1:2, :], precision=HI)
+            cum[at(c, Q), :] = run
+            cum_t[:, at(c, Q)] = run.T[0:8]
+            dt_t[:, at(c, Q)] = d.T[0:8]
+
+        loop(NC, steps, 2)
         st[...] = jnp.zeros_like(st)
         tot[s] = jnp.zeros((8, Q), f32)
 
@@ -367,15 +384,13 @@
             tail = mm(jnp.exp(last - run) * dt[at(c, Q), :], e[...], precision=HI)
             xt = act[at(c, Q), 0:C].astype(f32) * tail
             entry[c] = st[...]
-            st[...] = st[...] * row_of(jnp.exp(last), e[...]) + mm2(
-                act[at(c, Q), C : C + Q], xt, TN
-            )
+            st[...] = st[...] * row_of(jnp.exp(last), e[...]) + mm2(act[at(c, Q), C : C + Q], xt, TN)
             tot[s] += jnp.broadcast_to(last, (8, Q))
 
         loop(NC, chunk)
         fin[s] = st[...].astype(bf16)
-    relay = Relay((fin, tot), (slots, slots_t), f_s, f_r, seqs, 1)
-    relay.start()
+        relays.append(Relay(s, (fin, tot), (slots, slots_t), f_sem, seqs, 1))
+        relays[s].start()
 
     def weights_of(h, here, causal):
         gap = cum[here, h : h + 1] - cum_t[h : h + 1, here]
@@ -395,16 +410,21 @@
             ys[here, p * Q : (p + 1) * Q] = y
 
     loop(T // Q, within)
-    moves[8].wait()
-    moves[9].wait()
-
-    def cotangent(i):
-        dy[at(i, 512), :] = mm(cot[at(i, 512), :], wo[...], NT)
-
-    loop(T // 512, cotangent)
-    relay.gather(chained, e)
-
+    moves[S + 4].wait()
+    moves[S + 5].wait()
     for s in range(S):
+        seq_rows = slice(s * L, (s + 1) * L)
+        dy[seq_rows, :] = mm(cot[seq_rows, :], wo[...], NT)
+
+    def stat(s, i):
+        part = pl.ds(s * L, L)
+        return remote(
+            stats_t.at[:, part], stats_in.at[i - 1, :, part], st_s.at[s, i - 1], st_r.at[s, i - 1], head=line(i)
+        )
+
+    stats_t[...] = jnp.zeros_like(stats_t)
+    for s in range(S):
+        relays[s].gather(chained, e)
         off[...] = jnp.zeros_like(off)
 
         def across(k):
@@ -413,9 +433,7 @@
             si = entry[c] + row_of(jnp.exp(off[0:1, :]), e[...]) * chained[s]
             entry[c] = si
             run = cum[here, :]
-            work[0] = mm(jnp.exp(run), e[...], precision=HI) * mm2(
-                act[here, C + Q :], si
-            )
+            work[0] = mm(jnp.exp(run), e[...], precision=HI) * mm2(act[here, C + Q :], si)
             off[...] += jnp.broadcast_to(run[Q - 1 : Q, :], (8, Q))
 
             def tile(r):
@@ -425,28 +443,31 @@
                 m = y + sk[...] * act[rows, 0:C].astype(f32)
                 g = gate[rows, :].astype(f32)
                 gated = m * (g * jax.nn.sigmoid(g))
-                a = jnp.sum(gated * gated, axis=1, keepdims=True)
-                b = jnp.sum(dy[rows, :] * gg[...] * gated, axis=1, keepdims=True)
-                lane = iota((TILE, Q), 1)
-                stats[at(r, TILE), :] = jnp.where(lane == 0, a, jnp.where(lane == 1, b, 0.0))
-
-            loop(Q // TILE, tile)
-            stats_t[:, here] = stats[...].T[0:8]
+                a = gated * gated
+                b = dy[rows, :] * gg[...] * gated
+                stats[0, at(r, TILE), :] = sum(a[:, p * Q : (p + 1) * Q] for p in range(C // Q))
+                stats[1, at(r, TILE), :] = sum(b[:, p * Q : (p + 1) * Q] for p in range(C // Q))
+
+            loop(Q // TILE, tile, 2)
+            for j in range(2):
+                stats_t[j : j + 1, here] = jnp.sum(stats[j].T, axis=0, keepdims=True)
 
         loop(NC, across)
-
-    def stat(i):
-        return remote(stats_t, stats_in.at[i - 1], st_s.at[i - 1], st_r.at[i - 1], head=line(i))
-
-    for i in range(1, lines):
-        stat(i).start()
-    relay.finish()
+        for i in range(1, lines):
+            stat(s, i).start()
+
+    for r in relays:
+        r.finish()
     sums[...] = jnp.zeros_like(sums)
-    for i in range(1, lines):
-        stat(i).wait_recv()
-
     fold1 = Fold(part1, near1, far1, [z1.at[j] for j in range(4)], tiles)
+    fold2 = Fold(part2, near2, far2, [z2.at[j] for j in range(4)], tiles)
+
+    def spread_dy(c):
+        return mm(jnp.exp(cum[at(c, Q), :]), e[...], precision=HI) * dy[at(c, Q), :]
+
     for s in range(S):
+        for i in range(1, lines):
+            stat(s, i).wait_recv()
 
         def gate_back(k):
             c = s * NC + k
@@ -479,14 +500,16 @@
                 sums[0:8, :] += fold8(d * scaled_rows)
                 sums[8:16, :] += fold8(dmix * x)
 
-            loop(Q // TILE, tile)
+            loop(Q // TILE, tile, 2)
+            if s > 0:
+
+                @pl.when(lax.rem(k, 2) == 1)
+                def _():
+                    fold1.step(lax.div(k, 2))
 
         loop(NC, gate_back)
         part1[s * L : (s + 1) * L, :] = mm(gn[s * L : (s + 1) * L, :], wo[...]).astype(bf16)
         fold1.begin(s * (tiles // S), tiles // S)
-
-    def spread_dy(c):
-        return mm(jnp.exp(cum[at(c, Q), :]), e[...], precision=HI) * dy[at(c, Q), :]
 
     for s in range(S):
         st[...] = jnp.zeros_like(st)
@@ -495,38 +518,67 @@
             c = s * NC + NC - 1 - k
             last = cum[pl.ds(pl.multiple_of(c * Q + Q - 8, 8), 8), :][7:8]
             later[c] = st[...]
-            st[...] = st[...] * row_of(jnp.exp(last), e[...]) + mm2(
-                act[at(c, Q), C + Q :], spread_dy(c), TN
-            )
+            st[...] = st[...] * row_of(jnp.exp(last), e[...]) + mm2(act[at(c, Q), C + Q :], spread_dy(c), TN)
 
         loop(NC, back)
         fin[s] = st[...].astype(bf16)
-    relay2 = Relay((fin, tot), (slots, slots_t), b_s, b_r, seqs, -1)
-    relay2.start()
-
-    def outer(i):
-        half = mm(gn[...], cot[:, at(i, 512)], TN)
-        gr[0, at(i, 512), :] = half.astype(bf16)
-
-    loop(D // 512, outer)
+        relays2.append(Relay(s, (fin, tot), (slots, slots_t), b_sem, seqs, -1))
+        relays2[s].start()
+        fold1.step(2 + s)
+
+    HG = D // 2
+    PR = HG // seqs
+
+    def pair(k):
+        return remote(gr.at[k, at(other, HG)], gr_in.at[k], ga_s.at[k], ga_r.at[k], sample=other)
+
+    for i in range(D // C):
+        gr[0, i * C : (i + 1) * C, :] = mm(gn[...], cot[:, i * C : (i + 1) * C], TN).astype(bf16)
+    pair(0).start()
+    fold1.step(4)
+
+    def turn(i):
+        rows = at(i, 256)
+        nt[:, rows] = (xb[rows, :].astype(f32) * inv[rows, 0:1] * gain[...]).astype(bf16).T
+
+    loop(T // 256, turn)
+    fold1.step(5)
 
     def outer2(i):
         gr[1, at(i, 512), :] = mm(nt[at(i, 512), :], dg[...]).astype(bf16)
 
     loop(D // 512, outer2)
-    HG = D // 2
-    PR = HG // seqs
-
-    def pair(k):
-        return remote(gr.at[k, at(other, HG)], gr_in.at[k], ga_s.at[k], ga_r.at[k], sample=other)
-
-    pair(0).start()
     pair(1).start()
-    relay2.gather(chained, e)
-    half = tiles // S
+    fold1.step(6)
 
     hsums[...] = jnp.zeros_like(hsums)
+    acc[...] = jnp.zeros_like(acc)
+    nsums[...] = jnp.zeros_like(nsums)
+    LT = L // TILE
+
+    def next_rows(s):
+        return remote(edge8.at[s], nx.at[s], nx_s.at[s], nx_r.at[s], seq=ps - 1)
+
+    @pl.when(ps == seqs - 1)
+    def _():
+        nx[...] = jnp.zeros_like(nx)
+
+    def settle(k):
+        pair(k).wait_recv()
+
+        def tile(i):
+            r = pl.ds(pl.multiple_of(pc * HG + i * TILE, TILE), TILE)
+            v = gr[k, r, :].astype(f32) + gr_in[k, at(i, TILE), :].astype(f32)
+            gr[k, r, :] = v.astype(bf16)
+
+        loop(HG // TILE, tile)
+
+    def piece(k, i):
+        r = pl.ds(pl.multiple_of(pc * HG + ring(i) * PR, PR), PR)
+        return remote(gr.at[k, r], gr_pieces.at[k, i - 1], gb_s.at[k, i - 1], gb_r.at[k, i - 1], seq=ring(i))
+
     for s in range(S):
+        relays2[s].gather(chained, e)
         off[...] = jnp.zeros_like(off)
 
         def state_back(k):
@@ -577,7 +629,7 @@
                 work[5, near, :] = x * both
                 slope[rows, 0:C] = (both + sk[...] * g) * slope[rows, 0:C]
 
-            loop(Q // TILE, tile)
+            loop(Q // TILE, tile, 2)
             ha = mm(work[3], e[...], NT, HI)
             hb = mm(work[4], e[...], NT, HI)
             hc = mm(work[5], e[...], NT, HI)
@@ -595,55 +647,22 @@
             dcs[here, 2 * Q :] = draw.astype(bf16)
             hsums[0:8, :] += fold8(draw)
             hsums[8:16, :] += fold8(rate * dlog * d)
-            if s == 0:
-                for j in range(half // NC):
-                    fold1.one(k * (half // NC) + j)
-            else:
-                for j in range(half // NC):
-                    fold1.one(half + k * (half // NC) + j)
-                    fold1.two(k * (half // NC) + j)
+            fold1.step((7 if s == 0 else 13) + k)
 
         loop(NC, state_back)
         edge8[s] = slope[s * L : s * L + 8, :]
 
-        def next_rows(s):
-            return remote(edge8.at[s], nx.at[s], nx_s.at[s], nx_r.at[s], seq=ps - 1)
-
         @pl.when(ps > 0)
         def _():
             next_rows(s).start()
 
-    def settle(k):
-        pair(k).wait_recv()
-
-        def tile(i):
-            r = pl.ds(pl.multiple_of(pc * HG + i * TILE, TILE), TILE)
-            v = gr[k, r, :].astype(f32) + gr_in[k, at(i, TILE), :].astype(f32)
-            gr[k, r, :] = v.astype(bf16)
-
-        loop(HG // TILE, tile)
-
-    def piece(k, i):
-        r = pl.ds(pl.multiple_of(pc * HG + ring(i) * PR, PR), PR)
-        return remote(gr.at[k, r], gr_pieces.at[k, i - 1], gb_s.at[k, i - 1], gb_r.at[k, i - 1], seq=ring(i))
-
-    for k in range(2):
-        settle(k)
+        settle(s)
         for i in range(1, seqs):
-            piece(k, i).start()
-
-    @pl.when(ps == seqs - 1)
-    def _():
-        nx[...] = jnp.zeros_like(nx)
-
-    @pl.when(ps < seqs - 1)
-    def _():
-        for s in range(S):
+            piece(s, i).start()
+
+        @pl.when(ps < seqs - 1)
+        def _():
             next_rows(s).wait_recv()
-
-    acc[...] = jnp.zeros_like(acc)
-    LT = L // TILE
-    for s in range(S):
 
         def conv_back(r, last):
             for lo in range(0, W, 256):
@@ -668,31 +687,32 @@
 
         loop(LT - 1, lambda r: conv_back(r, False))
         conv_back(LT - 1, True)
-        for j in range(half // 2):
-            fold1.two(half + s * (half // 2) + j)
-
-    nsums[...] = jnp.zeros_like(nsums)
-    fold2 = Fold(part2, near2, far2, [z2.at[j] for j in range(4)], tiles)
-
-    def into(s):
-        rows = at(s, 256)
-        v = (
-            mm(dg[rows, :], wg[...], NT)
-            + mm(gate[rows, :], wv[...], NT)
-            + mm(dcs[rows, :], wst[...])
-        )
-        part2[rows, :] = v.astype(bf16)
-        nsums[...] += fold8(v * xb[rows, :].astype(f32) * inv[rows, 0:1])
-        per = tiles * 256 // T
-        fold2.begin(s * per, per)
-
-    loop(T // 256, into)
+        if s == 0:
+            fold1.step(11)
+        else:
+            fold1.step(17)
+
+        def into(k):
+            i = s * (L // 256) + k
+            rows = at(i, 256)
+            v = mm(dg[rows, :], wg[...], NT) + mm(gate[rows, :], wv[...], NT) + mm(dcs[rows, :], wst[...])
+            part2[rows, :] = v.astype(bf16)
+            nsums[...] += fold8(v * xb[rows, :].astype(f32) * inv[rows, 0:1])
+            per = tiles * 256 // T
+            fold2.begin(i * per, per)
+
+        loop(L // 256, into)
+        if s == 0:
+            fold1.step(12)
+        else:
+            fold2.step(0)
 
     def outer3(i):
         gr[2, at(i, 512), :] = mm(nt[at(i, 512), :], gate[...]).astype(bf16)
 
     loop(D // 512, outer3)
     pair(2).start()
+    fold2.step(1)
     for k in range(D // Q):
         t = mm(nt[k * Q : (k + 1) * Q, :], dcs[...])
         for j in range(2):
@@ -707,6 +727,7 @@
         return remote(later.at[at(other, DC)], sg_in, sa_s, sa_r, sample=other)
 
     state_pair().start()
+    fold2.step(2)
     for k in range(5):
         row = jnp.sum(acc[8 * k : 8 * k + 8, :], axis=0, keepdims=True)
         small[k : k + 1, :] = row[:, 0:C]
@@ -727,40 +748,12 @@
 
     for i in range(1, lines):
         to_line(i).start()
-    loop(4, lambda i: fold2.one(i))
     settle(2)
     for i in range(1, seqs):
         piece(2, i).start()
-    state_pair().wait_recv()
-    later[keep_state] = later[keep_state] + sg_in[...]
-
-    def state_piece(i):
-        return remote(later.at[keep_state, at(ring(i), SR)], sg_pieces.at[i - 1], sb_s.at[i - 1], sb_r.at[i - 1], seq=ring(i))
-
-    for i in range(1, seqs):
-        state_piece(i).start()
-    loop(4, lambda i: fold2.one(4 + i))
-    total = smallz[...]
-    for i in range(1, lines):
-        to_line(i).wait_recv()
-        total = total + smallz_in[i - 1]
-    small[24:32, :] = total
-
-    def to_core():
-        return remote(small, small_two.at[0], m2_s.at[seqs - 1], m2_r.at[seqs - 1], sample=other)
-
-    def to_peer(i):
-        return remote(small_two.at[1], small_in.at[i - 1], m2_s.at[i - 1], m2_r.at[i - 1], seq=ring(i))
-
-    to_core().start()
-    loop(4, lambda i: fold2.two(0 + i))
-
-    to_core().wait_recv()
-    small_two[1] = small[...] + small_two[0]
-    for i in range(1, seqs):
-        to_peer(i).start()
-
-    for k in range(3):
+    fold2.step(3)
+
+    def gather_pieces(k):
         for i in range(1, seqs):
             piece(k, i).wait_recv()
 
@@ -784,12 +777,54 @@
         src = gr_sum.at[k] if i == 0 else grads.at[k, r]
         return remote(src, grads.at[k, r], gd_s.at[k, i], gd_r.at[k, i], sample=other)
 
-    for k in range(3):
+    def send_out(k):
+        gather_pieces(k)
         for i in range(1, seqs):
             spread(k, i).start()
         hand(k, 0).start()
-    loop(4, lambda i: fold2.one(8 + i))
-    loop(4, lambda i: fold2.two(4 + i))
+
+    def hand_on(k):
+        for i in range(1, seqs):
+            q = lax.rem(ps + seqs - i, seqs)
+            r = pl.ds(pl.multiple_of(pc * HG + q * PR, PR), PR)
+            remote(gr_sum.at[k], grads.at[k, r], gc_s.at[k, i - 1], gc_r.at[k, i - 1], seq=ring(i)).wait_recv()
+            hand(k, i).start()
+
+    send_out(0)
+    fold2.step(4)
+    send_out(1)
+    fold2.step(5)
+    state_pair().wait_recv()
+    later[keep_state] = later[keep_state] + sg_in[...]
+
+    def state_piece(i):
+        return remote(later.at[keep_state, at(ring(i), SR)], sg_pieces.at[i - 1], sb_s.at[i - 1], sb_r.at[i - 1], seq=ring(i))
+
+    for i in range(1, seqs):
+        state_piece(i).start()
+    fold2.step(6)
+    total = smallz[...]
+    for i in range(1, lines):
+        to_line(i).wait_recv()
+        total = total + smallz_in[i - 1]
+    small[24:32, :] = total
+
+    def to_core():
+        return remote(small, small_two.at[0], m2_s.at[seqs - 1], m2_r.at[seqs - 1], sample=other)
+
+    def to_peer(i):
+        return remote(small_two.at[1], small_in.at[i - 1], m2_s.at[i - 1], m2_r.at[i - 1], seq=ring(i))
+
+    to_core().start()
+    fold2.step(7)
+    to_core().wait_recv()
+    small_two[1] = small[...] + small_two[0]
+    for i in range(1, seqs):
+        to_peer(i).start()
+    hand_on(0)
+    fold2.step(8)
+    send_out(2)
+    fold2.step(9)
 
     for i in range(1, seqs):
         state_piece(i).wait_recv()
@@ -808,8 +843,10 @@
         def _():
             to_owner(i).start()
 
-    loop(4, lambda i: fold2.one(12 + i))
-    loop(4, lambda i: fold2.two(8 + i))
+    fold2.step(10)
+    hand_on(1)
+    fold2.step(11)
+    fold2.step(12)
     span = max(own // SR, 1)
 
     def place_row(q, core):
@@ -833,6 +870,10 @@
         for i in range(1, seqs):
             state_out_to(i).start()
 
+    fold2.step(13)
+    hand_on(2)
+    fold2.step(14)
+    fold2.step(15)
     for j in range(span):
         q = ph * span + j
 
@@ -849,26 +890,23 @@
                 ).wait_recv()
                 state_hand(j, state_out.at[:, place_row(q, pc)]).start()
 
-    for k in range(3):
-        for i in range(1, seqs):
-            q = lax.rem(ps + seqs - i, seqs)
-            r = pl.ds(pl.multiple_of(pc * HG + q * PR, PR), PR)
-            remote(gr_sum.at[k], grads.at[k, r], gc_s.at[k, i - 1], gc_r.at[k, i - 1], seq=ring(i)).wait_recv()
-            hand(k, i).start()
-    loop(4, lambda i: fold2.two(12 + i))
+    fold2.step(16)
     total = small_two[1]
     for i in range(1, seqs):
         to_peer(i).wait_recv()
         total = total + small_in[i - 1]
     small_out[...] = total
+    fold2.step(17)
 
     fold1.end()
     fold2.end()
-    relay2.finish()
+    for r in relays2:
+        r.finish()
     for i in range(1, lines):
-        for c in weights(i):
+        for c in weights(i, ph):
             c.wait_send()
-        stat(i).wait_send()
+        for s in range(S):
+            stat(s, i).wait_send()
         to_line(i).wait_send()
 
         @pl.when(line(i) == owner)
@@ -910,22 +948,49 @@
         to_peer(i).wait_send()
 
 
-def finish(x, cot, gain, dn, outs, gr, block_out, input_grad, gate_grad, value_grad, out_grad):
-    def tile(i):
-        r = at(i, TILE)
+def finish(
+    lines, x, cot, gain, dn, outs, g_out, g_gate, g_value, state, small,
+    block_out, input_grad, gate_grad, value_grad, out_grad,
+    state_grad, norm_grad, step_grad, cv, cs, cvb, csb, sbias, dlog, skip, gated_gain,
+):
+    rows, width = x.shape
+    for j in range(rows // 16):
+        r = slice(j * 16, (j + 1) * 16)
         v = x[r, :].astype(f32)
         block_out[r, :] = (v + outs[r, :].astype(f32)).astype(bf16)
         s = dn[r, :].astype(f32) * gain[...]
         i1 = lax.rsqrt(jnp.mean(v * v, axis=1, keepdims=True) + EPS)
         m = jnp.mean(s * v, axis=1, keepdims=True)
         input_grad[r, :] = cot[r, :].astype(f32) + i1 * s - v * (i1 * i1 * i1 * m)
-
-    loop(x.shape[0] // TILE, tile)
-    half = gr.shape[1] // 2
-    out_grad[:, 0:half] = gr[0, 0:half, :].astype(f32)
-    out_grad[:, half:] = gr[0, half:, :].astype(f32)
-    gate_grad[...] = gr[1].astype(f32)
-    value_grad[...] = gr[2].astype(f32)
+    half = g_gate.shape[1]
+    for j in range(width // half):
+        out_grad[:, j * half : (j + 1) * half] = g_out[j].astype(f32)
+    gate_grad[...] = g_gate[...].astype(f32)
+    value_grad[...] = g_value[...].astype(f32)
+
+    @pl.when(pl.program_id(0) == 0)
+    def _():
+        heads, own = sbias.shape[1], csb.shape[1]
+        for j in range(width // half):
+            lanes = slice(j * half, (j + 1) * half)
+            state_grad[:, lanes] = state[j]
+            norm_grad[:, lanes] = small[29 + j : 30 + j, :]
+            step_grad[:, lanes] = small[8 + 8 * j : 16 + 8 * j, :]
+        cv[...] = small[0:4, :]
+        cvb[...] = small[4:5, :]
+        gated_gain[...] = small[5:6, :]
+        e = lane_heads(half // 64, half)
+        skip[...] = mm(jnp.broadcast_to(small[6:7, :], (8, half)), e, NT, HI)[0:1, 0:heads]
+        sbias[...] = small[7:8, 0:heads]
+        dlog[...] = small[7:8, Q : Q + heads]
+        for h in range(lines):
+
+            @pl.when(lax.axis_index("head") == h)
+            def _():
+                for j in range(2):
+                    lanes = slice(j * Q + h * own, j * Q + (h + 1) * own)
+                    cs[:, j, :] = small[24:28, lanes]
+                    csb[j : j + 1, :] = small[28:29, lanes]
 
 
 def per_device(
@@ -948,13 +1013,6 @@
     x = block_in.reshape(T, D)
     cot = out_cotangent.reshape(T, D)
     spt = state_proj.transpose(0, 2, 1).reshape(2 * own, D)
-    stp = jnp.pad(step_proj.T, ((0, Q - heads), (0, 0)))
-    taps = jnp.concatenate([conv_state, conv_state_bias[None]], axis=0)
-    cst = jnp.pad(taps.transpose(1, 2, 0).reshape(2 * own, 5), ((0, 0), (0, Q - 5)))
-    cwv = jnp.pad(jnp.concatenate([conv_value, conv_value_bias[None]], axis=0), ((0, 3), (0, 0)))
-    hp = jnp.pad(jnp.stack([step_bias, -jnp.exp(decay_log)]), ((0, 6), (0, Q - heads)))
-    sk = jnp.repeat(skip_gain, C // heads)[None]
-    gg = gated_gain[None]
     gain = norm_gain[None]
     vm = pl.BlockSpec(memory_space=pltpu.VMEM)
     hbm = pl.BlockSpec(memory_space=pl.ANY)
@@ -963,13 +1021,14 @@
     V = pltpu.VMEM
     scratch = [
         V((T, D), bf16), V((T, D), bf16), V((D, C), bf16), V((D, C), bf16), V((3 * Q, D), bf16),
-        V((C, D), bf16), V((2 * Q, Q), f32), V((8, W), f32), V((S * HALO, D), bf16),
+        V((C, D), bf16), V((8, Q), f32), V((lines, 8, Q), f32), V((8, W), f32), V((8, Q), f32), V((1, C), f32),
+        V((S * HALO, D), bf16),
         V((D, T), bf16), V((T, Q), f32), V((T, C), bf16), V((S, HALO + L, W), bf16), V((T, W), f32),
         V((T, W), bf16), V((T, Q), f32), V((T, Q), f32), V((T, Q), f32), V((8, T), f32), V((8, T), f32),
         V((NCH, Q, C), f32), V((T, C), f32), V((T, C), f32), V((T, C), bf16), V((T, C), bf16),
         V((NCH, Q, C), f32),
         V((T, 3 * Q), bf16), V((Q, C), f32), V((Q, C), f32), V((6, Q, C), f32),
-        V((8, Q), f32), V((Q, Q), f32), V((Q, Q), f32), V((8, T), f32), V((l1, 8, T), f32),
+        V((8, Q), f32), V((Q, Q), f32), V((2, Q, Q), f32), V((8, T), f32), V((l1, 8, T), f32),
         V((S, Q, C), bf16), V((S, 8, Q), f32), V((seqs, S, Q, C), bf16), V((seqs, S, 8, Q), f32),
         V((S, Q, C), f32),
         V((T, D), bf16), V((T, D), bf16), V((T, D), bf16), V((T, D), bf16),
@@ -978,8 +1037,8 @@
         V((2, D // C, SR, C), f32),
         V((40, W), f32), V((16, Q), f32), V((16, C), f32), V((8, D), f32), V((8, C), f32),
         V((l1, 8, C), f32), V((32, C), f32), V((2, 32, C), f32), V((n1, 32, C), f32), V((S, 8, W), f32), V((S, 8, W), f32),
-        dma((10,)), dma((2, S)), dma((4, l1)), dma((4, l1)), dma((2, n1)), dma((2, n1)),
-        dma((2, n1)), dma((2, n1)), dma((l1,)), dma((l1,)), dma((S,)), dma((S,)),
+        dma((S + 6,)), dma((2, S)), dma((3, l1)), dma((3, l1)), dma((2, 2, S, n1)), dma((2, 2, S, n1)),
+        dma((S, l1)), dma((S, l1)), dma((S,)), dma((S,)),
         dma((4, tiles)), dma((4, tiles)), dma((3,)), dma((3,)), dma((3, n1)), dma((3, n1)),
         dma((3, n1)), dma((3, n1)), dma((3, seqs)), dma((3, seqs)),
         dma, dma, dma((n1,)), dma((n1,)), dma((l1,)), dma((l1,)), dma((n1,)), dma((n1,)),
@@ -992,34 +1051,54 @@
             jax.ShapeDtypeStruct((3, D, C), bf16), jax.ShapeDtypeStruct((D // C, 2 * own, C), f32),
             jax.ShapeDtypeStruct((32, C), f32),
         ],
-        in_specs=[hbm, hbm, vm, hbm, hbm, hbm, hbm, hbm, hbm, vm, vm, vm, vm],
+        in_specs=[hbm, hbm, vm, hbm, hbm, hbm, vm, hbm] + [vm] * 8,
         out_specs=[vm] * 5,
         scratch_shapes=scratch,
         name="block",
         compiler_params=pltpu.CompilerParams(
             collective_id=0, has_side_effects=True, vmem_limit_bytes=67043328
         ),
-    )(x, cot, gain, gate_proj, value_proj, spt, stp, out_proj, cst, cwv, hp, sk, gg)
-    block_out, input_grad, gate_grad, value_grad, out_grad = pl.pallas_call(
-        finish,
+    )(
+        x, cot, gain, gate_proj, value_proj, spt, step_proj.T, out_proj, conv_state, conv_state_bias,
+        conv_value, conv_value_bias[None], step_bias[None], decay_log[None], skip_gain[None], gated_gain[None],
+    )
+    steps = 8
+
+    def whole(*shape):
+        return pl.BlockSpec(shape, lambda i: (0,) * len(shape))
+
+    by_rows = pl.BlockSpec((T // steps, D), lambda i: (i, 0))
+    by_grad = pl.BlockSpec((D // steps, C), lambda i: (i, 0))
+    shape = jax.ShapeDtypeStruct
+    (block_out, input_grad, gate_grad, value_grad, out_grad, state_grad, norm_grad, step_grad, cv, cs, cvb, csb,
+     sbias, dlog, skip, gated) = pl.pallas_call(
+        functools.partial(finish, lines),
+        grid=(steps,),
         out_shape=[
-            jax.ShapeDtypeStruct((T, D), bf16), jax.ShapeDtypeStruct((T, D), f32),
-            jax.ShapeDtypeStruct((D, C), f32), jax.ShapeDtypeStruct((D, C), f32),
-            jax.ShapeDtypeStruct((C, D), f32),
+            shape((T, D), bf16), shape((T, D), f32), shape((D, C), f32), shape((D, C), f32), shape((C, D), f32),
+            shape((2 * own, D), f32), shape((1, D), f32), shape((heads, D), f32), shape((4, C), f32),
+            shape((4, 2, own), f32), shape((1, C), f32), shape((2, own), f32), shape((1, heads), f32),
+            shape((1, heads), f32), shape((1, heads), f32), shape((1, C), f32),
         ],
-        in_specs=[vm] * 6,
-        out_specs=[vm] * 5,
+        in_specs=[
+            by_rows, by_rows, whole(1, D), by_rows, by_rows,
+            pl.BlockSpec((None, D // C, C // steps, C), lambda i: (0, 0, i, 0)),
+            pl.BlockSpec((None, D // steps, C), lambda i: (1, i, 0)),
+            pl.BlockSpec((None, D // steps, C), lambda i: (2, i, 0)),
+            whole(D // C, 2 * own, C), whole(32, C),
+        ],
+        out_specs=[
+            by_rows, by_rows, by_grad, by_grad, pl.BlockSpec((C // steps, D), lambda i: (i, 0)),
+            whole(2 * own, D), whole(1, D), whole(heads, D), whole(4, C), whole(4, 2, own), whole(1, C),
+            whole(2, own), whole(1, heads), whole(1, heads), whole(1, heads), whole(1, C),
+        ],
         name="finish",
         compiler_params=pltpu.CompilerParams(vmem_limit_bytes=60 * 2**20),
-    )(x, cot, gain, dnorm, outs, grads)
-    ph = lax.axis_index("head")
-    state_grad = state_out.reshape(D // C, 2, own, C).transpose(1, 0, 3, 2).reshape(2, D, own)
-    step_grad = small[8:24].reshape(D // C, heads, C).transpose(0, 2, 1).reshape(D, heads)
-    cs = lax.dynamic_slice_in_dim(small[24:29, 0 : 2 * Q].reshape(5, 2, Q), ph * own, own, 2)
+    )(x, cot, gain, dnorm, outs, grads.reshape(3, D // C, C, C), grads, grads, state_out, small)
     return (
-        block_out.reshape(S, L, D), input_grad.reshape(S, L, D), small[29:31].reshape(D), gate_grad,
-        value_grad, state_grad, step_grad, small[0:4], cs[0:4], small[4], cs[4], small[7, 0:heads],
-        small[7, Q : Q + heads], jnp.sum(small[6].reshape(heads, C // heads), axis=1), small[5], out_grad,
+        block_out.reshape(S, L, D), input_grad.reshape(S, L, D), norm_grad[0], gate_grad, value_grad,
+        state_grad.reshape(2, own, D).transpose(0, 2, 1), step_grad.T, cv, cs, cvb[0], csb, sbias[0], dlog[0],
+        skip[0], gated[0], out_grad,
     )
 
 

time: 260 us -> 199 us (0.77)
  Pallas kernels: 240 us -> 198 us
  local copies, waits for them, and re-layouts: 13.9 us -> 0 us
  other arithmetic: 4.58 us -> 0 us
    pallas_call x1, Pallas kernels: 227 us -> 185 us  [per_device(): pl.pallas_call(functools.partial(block, (S, L, seqs, lines, tiles)), out_...]
    slice x5 -> x0, local copies, waits for them, and re-layouts: 5.47 us -> none  [the longest x1 1.42 us: per_device(): small[5]]
where the time goes in v2:
time: 199 us; the launch traced here: 198 us
  Pallas kernels  198 us (99%)
    pallas_call x1, Pallas kernels, per_device(): pl.pallas_call(functools.partial(block, (S, L, seqs, lines, tiles)), out_...  185 us
    pallas_call x1, Pallas kernels, per_device(): pl.pallas_call(functools.partial(finish, lines), grid=(steps,), out_shape...  12.1 us

profile of v2, /device:TPU:0, one launch (start us, length us, event | category | flops | bytes accessed | tf_op | source)
XLA Modules:
  0.0 198.4 jit_solution(14208026537027758622)
XLA Ops:
  0.7 185.4 %block.1 = (bf16[1024,1024]{1,0:T(8,128)(2,1)}, bf16[1024,1024]{1,0:T(8,128)(2,1)}, bf16[3,1024,512]{2,1,0:T(8,128)(2,1)}, f32[2,64,512]{2,1,0:T(8,128)}, f32[32,512]{1,0:T(8,128)}) custom-call(bf16[1024,1024]{1,0:T(8,128)(2,1)} %bitcast.26, bf16[1024,1024]{1,0:T(8,128)(2,1)} %bitcast.28, f32[1,1024]{1,0:T(1,128)} %bitcast.32, bf16[1024,512]{1,0:T(8,128)(2,1)} %wg_in.1, ...), custom_call_target="tpu_custom_call" | custom-call | tf_op jit(solution)/shard_map/block/pallas_call | solution.py:1047
  186.1 12.1 %finish.1 = (bf16[1024,1024]{1,0:T(8,128)(2,1)}, f32[1024,1024]{1,0:T(8,128)}, f32[1024,512]{1,0:T(8,128)}, f32[1024,512]{1,0:T(8,128)}, f32[512,1024]{1,0:T(8,1...) custom-call(bf16[1024,1024]{1,0:T(8,128)(2,1)} %bitcast.27, ...), custom_call_target="tpu_custom_call" | custom-call | tf_op jit(solution)/shard_map/finish/pallas_call | solution.py:1074

commit v3 on v2

--- a/solution.py
+++ b/solution.py
@@ -23,9 +23,23 @@
     )
 
 
+def halves(v):
+    high = v.astype(bf16)
+    return high, (v - high.astype(f32)).astype(bf16)
+
+
 def mm2(a, b, dims=NN):
-    high = b.astype(bf16)
-    return mm(a, high, dims) + mm(a, (b - high.astype(f32)).astype(bf16), dims)
+    if a.dtype == bf16:
+        high, low = halves(b)
+        return mm(a, high, dims) + mm(a, low, dims)
+    high, low = halves(a)
+    return mm(high, b, dims) + mm(low, b, dims)
+
+
+def mm3(a, b, dims=NN):
+    ah, al = halves(a)
+    bh, bl = halves(b)
+    return mm(ah, bh, dims) + (mm(ah, bl, dims) + mm(al, bh, dims))
 
 
 def at(i, n):
@@ -47,7 +61,7 @@
 
 def lane_heads(heads, width):
     shift = (width // heads).bit_length() - 1
-    return ((iota((Q, width), 1) >> shift) == iota((Q, width), 0)).astype(f32)
+    return ((iota((Q, width), 1) >> shift) == iota((Q, width), 0)).astype(f32).astype(bf16)
 
 
 def triangle(keep):
@@ -59,7 +73,11 @@
 
 
 def row_of(v, e):
-    return mm(jnp.broadcast_to(v, (8, Q)), e, precision=HI)[0:1]
+    return mm2(jnp.broadcast_to(v, (8, Q)), e)[0:1]
+
+
+def sigmoid(v):
+    return 0.5 * jnp.tanh(0.5 * v) + 0.5
 
 
 def normalize(v, gain):
@@ -74,9 +92,9 @@
 
 
 class Fold:
-    def __init__(self, part, near, far, sems, tiles):
-        self.part, self.near, self.far, self.tiles = part, near, far, tiles
-        self.a, self.b, self.c, self.d = sems
+    def __init__(self, part, near, far, result, sems, tiles):
+        self.part, self.near, self.far, self.result, self.tiles = part, near, far, result, tiles
+        (self.b, self.d), (self.a, self.c, self.e) = sems
         self.rows = part.shape[0] // tiles
         place = lax.axis_index("head")
         self.inner = (place == 1) | (place == 2)
@@ -85,11 +103,21 @@
 
     def outward(self, i, src):
         r = at(i, self.rows)
-        return remote(src.at[r], self.near.at[r], self.a.at[i], self.b.at[i], head=self.beside)
+        return remote(src.at[r], self.near.at[r], self.a, self.b.at[i], head=self.beside)
 
     def middle(self, i):
         r = at(i, self.rows)
-        return remote(self.part.at[r], self.far.at[r], self.c.at[i], self.d.at[i], head=self.across)
+        return remote(self.part.at[r], self.far.at[r], self.c, self.d.at[i], head=self.across)
+
+    def store(self, i):
+        r = at(i, self.rows)
+        return pltpu.make_async_copy(self.near.at[r], self.result.at[r], self.e)
+
+    def take(self, i):
+        @pl.when(jnp.logical_not(self.inner))
+        def _():
+            self.outward(i, self.near).wait_recv()
+            self.store(i).start()
 
     def begin(self, first, count):
         @pl.when(jnp.logical_not(self.inner))
@@ -116,39 +144,48 @@
             self.middle(i).wait_recv()
             self.add(self.near, self.part, self.far, i)
             self.outward(i, self.near).start()
-
-    def step(self, j, lag=2):
-        if isinstance(j, int):
-            if j < self.tiles:
-                self.one(j)
-            if 0 <= j - lag < self.tiles:
-                self.two(j - lag)
-            return
-
-        @pl.when(j < self.tiles)
-        def _():
-            self.one(j)
-
-        @pl.when((j >= lag) & (j < self.tiles + lag))
-        def _():
-            self.two(j - lag)
+            self.store(i).start()
+
+    def step(self, j):
+        for ago, move in ((0, self.one), (2, self.two), (4, self.take)):
+            if isinstance(j, int):
+                if 0 <= 2 * (j - ago) < self.tiles:
+                    loop(2, lambda q: move(2 * (j - ago) + q))
+            else:
+
+                @pl.when((j >= ago) & (2 * j < self.tiles + 2 * ago))
+                def _():
+                    loop(2, lambda q: move(2 * (j - ago) + q))
+
+    def last(self, j, parts):
+        o, t, k = 2 * j + 2, 2 * j - 2, 2 * j - 6
+        moves = []
+        while k < self.tiles:
+            if o < self.tiles:
+                moves.append((self.one, o))
+                o += 1
+            for unused in range(2):
+                if t < self.tiles and (t < o - 2 or o == self.tiles):
+                    moves.append((self.two, t))
+                    t += 1
+            for unused in range(2):
+                if k < self.tiles and (k < t - 3 or t == self.tiles):
+                    moves.append((self.take, k))
+                    k += 1
+        size = -(-len(moves) // parts)
+        return [moves[i : i + size] for i in range(0, len(moves), size)]
 
     def end(self):
+        pltpu.make_async_copy(self.near, self.result, self.e).wait()
+        remote(self.part, self.near, self.a, self.b.at[0], head=self.beside).wait_send()
+
         @pl.when(self.inner)
         def _():
-            def done(i):
-                self.middle(i).wait_send()
-                self.outward(i, self.near).wait_send()
-
-            loop(self.tiles, done)
-
-        @pl.when(jnp.logical_not(self.inner))
-        def _():
-            def done(i):
-                self.outward(i, self.part).wait_send()
-                self.outward(i, self.near).wait_recv()
-
-            loop(self.tiles, done)
+            remote(self.part, self.far, self.c, self.d.at[0], head=self.across).wait_send()
+
+
+def fold_sems(tiles, streams):
+    return [tiles.at[j] for j in range(2)], [streams.at[j] for j in range(3)]
 
 
 class Relay:
@@ -191,7 +228,7 @@
                 source = self.place - self.way * d
                 for c in self.copies(d, source):
                     c.wait_recv()
-                decay = mm(jnp.exp(self.slots[1][source, q]), e[...], precision=HI)[0:1]
+                decay = mm2(jnp.exp(self.slots[1][source, q]), e[...])[0:1]
                 state[q] = state[q] * decay + self.slots[0][source, q].astype(f32)
 
     def finish(self):
@@ -206,17 +243,17 @@
 def block(
     dims,
     x_in, cot_in, gain, wg_in, wv_in, spt, stp, wo_in, cs, csb, cv, cvb, sbias, dlog_in, skip, gg,
-    outs, dnorm, grads, state_out, small_out,
+    outs, dnorm, grads_out, state_out, small_out,
     xb, cot, wg, wv, wst, wo, tapb, taps, cw, hp, sk, xh,
     nt, inv, gate, pad, slope, act, dt, sg, cum, cum_t, dt_t, entry, ys, dy, gn, dg, later,
     dcs, e, st, work, off, tt, stats, stats_t, stats_in,
     fin, tot, slots, slots_t, chained,
-    part1, far1, part2, far2,
-    gr, gr_in, gr_pieces, gr_sum, sg_in, sg_pieces, sg_line, sg_sum,
+    part1, near1, far1, part2, near2, far2, grads,
+    gr, gr_in, gr_pieces, gr_sum, sg_in, sg_pieces, sg_line, sg_wire, sg_sum,
     acc, hsums, sums, nsums, smallz, smallz_in, small, small_two, small_in, nx, edge8,
     load, halo_sem, wt_s, wt_r, f_sem, b_sem, st_s, st_r, nx_s, nx_r,
-    z1, z2, ga_s, ga_r, gb_s, gb_r, gc_s, gc_r, gd_s, gd_r,
-    sa_s, sa_r, sb_s, sb_r, sz_s, sz_r, sc_s, sc_r, sd_s, sd_r, m1_s, m1_r, m2_s, m2_r,
+    z1, y1, z2, y2, ga_s, ga_r, gb_s, gb_r, gc_s, gc_r, gd_s, gd_r,
+    out_sem, sa_s, sa_r, sb_s, sb_r, sz_s, sz_r, sc_s, sc_r, sd_s, sd_r, m1_s, m1_r, m2_s, m2_r,
 ):
     S, L, seqs, lines, tiles = dims
     T, D = xb.shape
@@ -230,7 +267,6 @@
     group = 2 * seqs
     DC = D // C
     mine = ps * 2 + pc
-    near1, near2 = outs, dnorm
     nb = part1
 
     def peer(i):
@@ -247,12 +283,11 @@
     moves += [
         pltpu.make_async_copy(wg_in, wg, load.at[S]),
         pltpu.make_async_copy(wv_in, wv, load.at[S + 1]),
-        pltpu.make_async_copy(spt.at[pl.ds(0, own)], wst.at[at(ph, own)], load.at[S + 2]),
         pltpu.make_async_copy(
-            spt.at[pl.ds(own, own)], wst.at[pl.ds(pl.multiple_of(Q + ph * own, own), own)], load.at[S + 3]
+            spt.at[at(pc, own)], wst.at[pl.ds(pl.multiple_of(pc * Q + ph * own, own), own)], load.at[S + 2]
         ),
+        pltpu.make_async_copy(wo_in, wo, load.at[S + 3]),
         pltpu.make_async_copy(cot_in, cot, load.at[S + 4]),
-        pltpu.make_async_copy(wo_in, wo, load.at[S + 5]),
     ]
     for m in moves:
         m.start()
@@ -274,38 +309,9 @@
     wst[2 * Q :, :] = jnp.zeros((Q, D), bf16)
     wst[2 * Q : 2 * Q + heads, :] = stp[...]
     e[...] = lane_heads(C // 64, C)
-    sk[...] = mm(hp[...], e[...], precision=HI)[2:3]
-    pl.semaphore_wait(barrier, group - 1 + lines - 1)
-
-    def halo(s):
-        return remote(
-            x_in.at[pl.ds(s * L + L - HALO, HALO)], xh.at[pl.ds(s * HALO, HALO)],
-            halo_sem.at[0, s], halo_sem.at[1, s], seq=ps + 1,
-        )
-
-    @pl.when(ps < seqs - 1)
-    def _():
-        for s in range(S):
-            halo(s).start()
-
-    @pl.when(ps == 0)
-    def _():
-        xh[...] = jnp.zeros_like(xh)
-
-    def weights(i, source):
-        low = at(source, own)
-        high = pl.ds(pl.multiple_of(Q + source * own, own), own)
-        parts = [(spt.at[pl.ds(0, own)], wst.at[low]), (spt.at[pl.ds(own, own)], wst.at[high]), (tapb, taps.at[source])]
-        return [
-            remote(a, b, wt_s.at[j, i - 1], wt_r.at[j, i - 1], head=line(i))
-            for j, (a, b) in enumerate(parts)
-        ]
-
-    for i in range(1, lines):
-        for c in weights(i, ph):
-            c.start()
-
-    for s in range(S):
+    sk[...] = mm(hp[...], e[...].astype(f32), precision=HI)[2:3]
+
+    def norm(s):
         moves[s].wait()
 
         def norm_rows(r):
@@ -316,22 +322,94 @@
             inv[rows, :] = jnp.broadcast_to(i, (16, Q))
 
         loop(L // 16, norm_rows, 4)
-        if s == 0:
+
+    norm(0)
+    pl.semaphore_wait(barrier, group - 1 + lines - 1)
+
+    def halo(s):
+        return remote(
+            x_in.at[pl.ds(s * L + L - HALO, HALO)], xh.at[pl.ds(s * HALO, HALO)],
+            halo_sem.at[0, s], halo_sem.at[1, s], seq=ps + 1,
+        )
+
+    @pl.when(ps < seqs - 1)
+    def _():
+        for s in range(S):
+            halo(s).start()
+
+    @pl.when(ps == 0)
+    def _():
+        xh[...] = jnp.zeros_like(xh)
+
+    def weights(i, source):
+        r = pl.ds(pl.multiple_of(pc * Q + source * own, own), own)
+        parts = [(spt.at[at(pc, own)], wst.at[r]), (tapb, taps.at[source])]
+        return [
+            remote(a, b, wt_s.at[j, i - 1], wt_r.at[j, i - 1], head=line(i))
+            for j, (a, b) in enumerate(parts)
+        ]
+
+    for i in range(1, lines):
+        for c in weights(i, ph):
+            c.start()
+
+    for s in range(S):
+        if s > 0:
+            norm(s)
+        else:
             moves[S].wait()
             moves[S + 1].wait()
         seq_rows = slice(s * L, (s + 1) * L)
         gate[seq_rows, :] = mm(nb[seq_rows, :], wg[...]).astype(bf16)
         pad[s, HALO:, 0:C] = mm(nb[seq_rows, :], wv[...]).astype(bf16)
+
+    def conv(s, first, end):
+        def conv_rows(r):
+            for lo in range(first, end, 256):
+                lanes = slice(lo, lo + 256)
+                w = pad[s, pl.ds(pl.multiple_of(r * TILE, TILE), TILE + HALO), lanes].astype(f32)
+                v = cw[4:5, lanes] + cw[0:1, lanes] * w[13 : 13 + TILE]
+                for k in range(1, 4):
+                    v = v + cw[k : k + 1, lanes] * w[13 + k : 13 + k + TILE]
+                g = sigmoid(v)
+                rows = at(r + s * (L // TILE), TILE)
+                act[rows, lanes] = (v * g).astype(bf16)
+                slope[rows, lanes] = g * (1.0 + v * (1.0 - g))
+
+        loop(L // TILE, conv_rows, 2)
+
+    cw[0:4, 0:C] = cv[...]
+    cw[4:5, 0:C] = cvb[...]
+    edges = []
+    for s in range(S):
+
+        @pl.when(ps > 0)
+        def _():
+            halo(s).wait_recv()
+
+        edges.append(normalize(xh[s * HALO : (s + 1) * HALO, :].astype(f32), gain[...])[0])
+        pad[s, 0:HALO, 0:C] = mm(edges[s], wv[...]).astype(bf16)
+        conv(s, 0, C)
+    moves[S + 3].wait()
+    moves[S + 4].wait()
+    for s in range(S):
+        seq_rows = slice(s * L, (s + 1) * L)
+        dy[seq_rows, :] = mm(cot[seq_rows, :], wo[...], NT)
+
+    def share():
+        r = at(pc, Q)
+        return remote(wst.at[r], wst.at[r], wt_s.at[0, lines - 1], wt_r.at[0, lines - 1], sample=other)
+
     moves[S + 2].wait()
-    moves[S + 3].wait()
     for i in range(1, lines):
         for c in weights(i, line(lines - i)):
             c.wait_recv()
-    cw[0:4, 0:C] = cv[...]
-    cw[4:5, 0:C] = cvb[...]
+    share().start()
     for h in range(lines):
         for j in range(2):
             cw[:, C + j * Q + h * own : C + j * Q + (h + 1) * own] = taps[h, :, j * own : (j + 1) * own]
+    r = at(other, Q)
+    remote(wst.at[r], wst.at[r], wt_s.at[0, lines - 1], wt_r.at[0, lines - 1], sample=other).wait_recv()
 
     relays, relays2 = [], []
     for s in range(S):
@@ -339,28 +417,8 @@
         both = mm(nb[seq_rows, :], wst[...], NT)
         pad[s, HALO:, C:] = both[:, 0 : 2 * Q].astype(bf16)
         sg[seq_rows, :] = both[:, 2 * Q :]
-
-        @pl.when(ps > 0)
-        def _():
-            halo(s).wait_recv()
-
-        edge, unused = normalize(xh[s * HALO : (s + 1) * HALO, :].astype(f32), gain[...])
-        pad[s, 0:HALO, 0:C] = mm(edge, wv[...]).astype(bf16)
-        pad[s, 0:HALO, C:] = mm(edge, wst[0 : 2 * Q, :], NT).astype(bf16)
-
-        def conv_rows(r):
-            for lo in range(0, W, 256):
-                lanes = slice(lo, lo + 256)
-                w = pad[s, pl.ds(pl.multiple_of(r * TILE, TILE), TILE + HALO), lanes].astype(f32)
-                v = cw[4:5, lanes] + cw[0:1, lanes] * w[13 : 13 + TILE]
-                for k in range(1, 4):
-                    v = v + cw[k : k + 1, lanes] * w[13 + k : 13 + k + TILE]
-                g = jax.nn.sigmoid(v)
-                rows = at(r + s * (L // TILE), TILE)
-                act[rows, lanes] = (v * g).astype(bf16)
-                slope[rows, lanes] = g * (1.0 + v * (1.0 - g))
-
-        loop(L // TILE, conv_rows)
+        pad[s, 0:HALO, C:] = mm(edges[s], wst[0 : 2 * Q, :], NT).astype(bf16)
+        conv(s, C, W)
 
         def steps(k):
             c = s * NC + k
@@ -381,13 +439,13 @@
             c = s * NC + k
             run = cum[at(c, Q), :]
             last = run[Q - 1 : Q, :]
-            tail = mm(jnp.exp(last - run) * dt[at(c, Q), :], e[...], precision=HI)
+            tail = mm2(jnp.exp(last - run) * dt[at(c, Q), :], e[...])
             xt = act[at(c, Q), 0:C].astype(f32) * tail
             entry[c] = st[...]
             st[...] = st[...] * row_of(jnp.exp(last), e[...]) + mm2(act[at(c, Q), C : C + Q], xt, TN)
             tot[s] += jnp.broadcast_to(last, (8, Q))
 
-        loop(NC, chunk)
+        loop(NC, chunk, NC)
         fin[s] = st[...].astype(bf16)
         relays.append(Relay(s, (fin, tot), (slots, slots_t), f_sem, seqs, 1))
         relays[s].start()
@@ -409,12 +467,7 @@
                 y = y + mm(m, jnp.where(upper == bool(o), xp, jnp.zeros_like(xp)))
             ys[here, p * Q : (p + 1) * Q] = y
 
-    loop(T // Q, within)
-    moves[S + 4].wait()
-    moves[S + 5].wait()
-    for s in range(S):
-        seq_rows = slice(s * L, (s + 1) * L)
-        dy[seq_rows, :] = mm(cot[seq_rows, :], wo[...], NT)
+    loop(NC, within)
 
     def stat(s, i):
         part = pl.ds(s * L, L)
@@ -423,7 +476,8 @@
         )
 
     stats_t[...] = jnp.zeros_like(stats_t)
-    for s in range(S):
+
+    def cross(s):
         relays[s].gather(chained, e)
         off[...] = jnp.zeros_like(off)
 
@@ -433,7 +487,7 @@
             si = entry[c] + row_of(jnp.exp(off[0:1, :]), e[...]) * chained[s]
             entry[c] = si
             run = cum[here, :]
-            work[0] = mm(jnp.exp(run), e[...], precision=HI) * mm2(act[here, C + Q :], si)
+            work[0] = mm2(jnp.exp(run), e[...]) * mm2(act[here, C + Q :], si)
             off[...] += jnp.broadcast_to(run[Q - 1 : Q, :], (8, Q))
 
             def tile(r):
@@ -442,13 +496,13 @@
                 ys[rows, :] = y
                 m = y + sk[...] * act[rows, 0:C].astype(f32)
                 g = gate[rows, :].astype(f32)
-                gated = m * (g * jax.nn.sigmoid(g))
+                gated = m * (g * sigmoid(g))
                 a = gated * gated
                 b = dy[rows, :] * gg[...] * gated
                 stats[0, at(r, TILE), :] = sum(a[:, p * Q : (p + 1) * Q] for p in range(C // Q))
                 stats[1, at(r, TILE), :] = sum(b[:, p * Q : (p + 1) * Q] for p in range(C // Q))
 
-            loop(Q // TILE, tile, 2)
+            loop(Q // TILE, tile, 4)
             for j in range(2):
                 stats_t[j : j + 1, here] = jnp.sum(stats[j].T, axis=0, keepdims=True)
 
@@ -456,16 +510,16 @@
         for i in range(1, lines):
             stat(s, i).start()
 
-    for r in relays:
-        r.finish()
+    cross(0)
+    loop(NC, lambda k: within(NC + k))
     sums[...] = jnp.zeros_like(sums)
-    fold1 = Fold(part1, near1, far1, [z1.at[j] for j in range(4)], tiles)
-    fold2 = Fold(part2, near2, far2, [z2.at[j] for j in range(4)], tiles)
+    fold1 = Fold(part1, near1, far1, outs, fold_sems(z1, y1), tiles)
+    fold2 = Fold(part2, near2, far2, dnorm, fold_sems(z2, y2), tiles)
 
     def spread_dy(c):
-        return mm(jnp.exp(cum[at(c, Q), :]), e[...], precision=HI) * dy[at(c, Q), :]
-
-    for s in range(S):
+        return mm2(jnp.exp(cum[at(c, Q), :]), e[...]) * dy[at(c, Q), :]
+
+    def gating(s):
         for i in range(1, lines):
             stat(s, i).wait_recv()
 
@@ -487,7 +541,7 @@
                 x = act[rows, 0:C].astype(f32)
                 m = ys[rows, :] + sk[...] * x
                 g = gate[rows, :].astype(f32)
-                sig = jax.nn.sigmoid(g)
+                sig = sigmoid(g)
                 ga = g * sig
                 gated = m * ga
                 scaled_rows = gated * rm
@@ -500,18 +554,12 @@
                 sums[0:8, :] += fold8(d * scaled_rows)
                 sums[8:16, :] += fold8(dmix * x)
 
-            loop(Q // TILE, tile, 2)
-            if s > 0:
-
-                @pl.when(lax.rem(k, 2) == 1)
-                def _():
-                    fold1.step(lax.div(k, 2))
-
+            loop(Q // TILE, tile, 4)
         loop(NC, gate_back)
         part1[s * L : (s + 1) * L, :] = mm(gn[s * L : (s + 1) * L, :], wo[...]).astype(bf16)
         fold1.begin(s * (tiles // S), tiles // S)
 
-    for s in range(S):
+    def rewind(s):
         st[...] = jnp.zeros_like(st)
 
         def back(k):
@@ -520,11 +568,20 @@
             later[c] = st[...]
             st[...] = st[...] * row_of(jnp.exp(last), e[...]) + mm2(act[at(c, Q), C + Q :], spread_dy(c), TN)
 
-        loop(NC, back)
+        loop(NC, back, NC)
         fin[s] = st[...].astype(bf16)
         relays2.append(Relay(s, (fin, tot), (slots, slots_t), b_sem, seqs, -1))
         relays2[s].start()
-        fold1.step(2 + s)
+
+    cross(1)
+    gating(0)
+    for r in relays:
+        r.finish()
+    gating(1)
+    rewind(0)
+    fold1.step(0)
+    rewind(1)
+    fold1.step(1)
 
     HG = D // 2
     PR = HG // seqs
@@ -535,21 +592,21 @@
     for i in range(D // C):
         gr[0, i * C : (i + 1) * C, :] = mm(gn[...], cot[:, i * C : (i + 1) * C], TN).astype(bf16)
     pair(0).start()
-    fold1.step(4)
+    fold1.step(2)
 
     def turn(i):
         rows = at(i, 256)
         nt[:, rows] = (xb[rows, :].astype(f32) * inv[rows, 0:1] * gain[...]).astype(bf16).T
 
     loop(T // 256, turn)
-    fold1.step(5)
+    fold1.step(3)
 
     def outer2(i):
         gr[1, at(i, 512), :] = mm(nt[at(i, 512), :], dg[...]).astype(bf16)
 
     loop(D // 512, outer2)
     pair(1).start()
-    fold1.step(6)
+    fold1.step(4)
 
     hsums[...] = jnp.zeros_like(hsums)
     acc[...] = jnp.zeros_like(acc)
@@ -577,6 +634,61 @@
         r = pl.ds(pl.multiple_of(pc * HG + ring(i) * PR, PR), PR)
         return remote(gr.at[k, r], gr_pieces.at[k, i - 1], gb_s.at[k, i - 1], gb_r.at[k, i - 1], seq=ring(i))
 
+    def gather_pieces(k):
+        for i in range(1, seqs):
+            piece(k, i).wait_recv()
+
+        def tile(j):
+            r = at(j, TILE)
+            v = gr[k, pl.ds(pl.multiple_of(pc * HG + ps * PR + j * TILE, TILE), TILE), :].astype(f32)
+            for i in range(1, seqs):
+                v = v + gr_pieces[k, i - 1, r, :].astype(f32)
+            gr_sum[k, r, :] = v.astype(bf16)
+            grads[k, pl.ds(pl.multiple_of(pc * HG + ps * PR + j * TILE, TILE), TILE), :] = v.astype(bf16)
+
+        loop(PR // TILE, tile)
+
+    def spread(k, i):
+        r = pl.ds(pl.multiple_of(pc * HG + ps * PR, PR), PR)
+        return remote(gr_sum.at[k], grads.at[k, r], gc_s.at[k, i - 1], gc_r.at[k, i - 1], seq=ring(i))
+
+    def hand(k, i):
+        q = lax.rem(ps + seqs - i, seqs)
+        r = pl.ds(pl.multiple_of(pc * HG + q * PR, PR), PR)
+        src = gr_sum.at[k] if i == 0 else grads.at[k, r]
+        return remote(src, grads.at[k, r], gd_s.at[k, i], gd_r.at[k, i], sample=other)
+
+    def send_out(k):
+        gather_pieces(k)
+        for i in range(1, seqs):
+            spread(k, i).start()
+        hand(k, 0).start()
+
+    def hand_on(k):
+        for i in range(1, seqs):
+            q = lax.rem(ps + seqs - i, seqs)
+            r = pl.ds(pl.multiple_of(pc * HG + q * PR, PR), PR)
+            remote(gr_sum.at[k], grads.at[k, r], gc_s.at[k, i - 1], gc_r.at[k, i - 1], seq=ring(i)).wait_recv()
+            hand(k, i).start()
+
+    def result(k):
+        return pltpu.make_async_copy(grads.at[k], grads_out.at[k], out_sem.at[k])
+
+    def complete(k):
+        for i in range(seqs):
+            q = lax.rem(ps + seqs - i, seqs)
+            r = pl.ds(pl.multiple_of(other * HG + q * PR, PR), PR)
+            remote(gr_sum.at[k], grads.at[k, r], gd_s.at[k, i], gd_r.at[k, i], sample=other).wait()
+        result(k).start()
+
+    def send_pieces(k):
+        settle(k)
+        for i in range(1, seqs):
+            piece(k, i).start()
+
+    send_pieces(0)
+    send_pieces(1)
+    fold1.step(5)
     for s in range(S):
         relays2[s].gather(chained, e)
         off[...] = jnp.zeros_like(off)
@@ -609,11 +721,10 @@
                     dx = dx + mm((scores * w).astype(bf16), dym, TN)
                 work[0, :, lanes] = dx
             d = dt[here, :]
-            work[2] = mm(jnp.exp(last - run) * d, e[...], precision=HI)
+            work[2] = mm2(jnp.exp(last - run) * d, e[...])
             work[1] = work[2] * mm2(b, ds)
-            bf, rf = b.astype(f32), r.astype(f32)
-            d_read = mm(dsc, bf, precision=HI) + mm(spread_dy(c), entry[c], NT, HI)
-            d_in = mm(dsc, rf, TN, HI) + mm(act[here, 0:C].astype(f32) * work[2], ds, NT, HI)
+            d_read = mm2(dsc, b) + mm3(spread_dy(c), entry[c], NT)
+            d_in = mm2(dsc, r, TN) + mm3(act[here, 0:C].astype(f32) * work[2], ds, NT)
             slope[here, C : C + Q] = d_in * slope[here, C : C + Q]
             slope[here, C + Q :] = d_read * slope[here, C + Q :]
 
@@ -629,15 +740,15 @@
                 work[5, near, :] = x * both
                 slope[rows, 0:C] = (both + sk[...] * g) * slope[rows, 0:C]
 
-            loop(Q // TILE, tile, 2)
-            ha = mm(work[3], e[...], NT, HI)
-            hb = mm(work[4], e[...], NT, HI)
-            hc = mm(work[5], e[...], NT, HI)
-            crossing = mm(fold8(entry[c] * ds), e[...], NT, HI)
+            loop(Q // TILE, tile, 4)
+            ha = mm2(work[3], e[...], NT)
+            hb = mm2(work[4], e[...], NT)
+            hc = mm2(work[5], e[...], NT)
+            crossing = mm2(fold8(entry[c] * ds), e[...], NT)
             crossing = jnp.sum(crossing, axis=0, keepdims=True) * jnp.exp(last)
             dlog = (
-                mm(triangle(lambda i, j: i <= j), ha, precision=HI)
-                + mm(triangle(lambda i, j: i > j), hb, precision=HI)
+                mm2(triangle(lambda i, j: i <= j).astype(bf16), ha)
+                + mm2(triangle(lambda i, j: i > j).astype(bf16), hb)
                 + crossing
             )
             g = sg[here, :]
@@ -647,7 +758,7 @@
             dcs[here, 2 * Q :] = draw.astype(bf16)
             hsums[0:8, :] += fold8(draw)
             hsums[8:16, :] += fold8(rate * dlog * d)
-            fold1.step((7 if s == 0 else 13) + k)
+            fold1.step((6 if s == 0 else 12) + k)
 
         loop(NC, state_back)
         edge8[s] = slope[s * L : s * L + 8, :]
@@ -655,14 +766,6 @@
         @pl.when(ps > 0)
         def _():
             next_rows(s).start()
-
-        settle(s)
-        for i in range(1, seqs):
-            piece(s, i).start()
-
-        @pl.when(ps < seqs - 1)
-        def _():
-            next_rows(s).wait_recv()
 
         def conv_back(r, last):
             for lo in range(0, W, 256):
@@ -686,11 +789,20 @@
                 acc[32:40, lanes] += fold8(d)
 
         loop(LT - 1, lambda r: conv_back(r, False))
+        if s == 0:
+            fold1.step(10)
+        else:
+            fold1.step(16)
+            fold1.step(17)
+            fold2.step(0)
+
+        @pl.when(ps < seqs - 1)
+        def _():
+            next_rows(s).wait_recv()
+
         conv_back(LT - 1, True)
-        if s == 0:
-            fold1.step(11)
-        else:
-            fold1.step(17)
+        if s > 0:
+            fold2.step(1)
 
         def into(k):
             i = s * (L // 256) + k
@@ -698,21 +810,35 @@
             v = mm(dg[rows, :], wg[...], NT) + mm(gate[rows, :], wv[...], NT) + mm(dcs[rows, :], wst[...])
             part2[rows, :] = v.astype(bf16)
             nsums[...] += fold8(v * xb[rows, :].astype(f32) * inv[rows, 0:1])
-            per = tiles * 256 // T
-            fold2.begin(i * per, per)
 
         loop(L // 256, into)
         if s == 0:
-            fold1.step(12)
-        else:
-            fold2.step(0)
-
-    def outer3(i):
-        gr[2, at(i, 512), :] = mm(nt[at(i, 512), :], gate[...]).astype(bf16)
-
-    loop(D // 512, outer3)
-    pair(2).start()
-    fold2.step(1)
+            fold2.begin(0, tiles // S)
+            fold1.step(11)
+            send_out(0)
+
+    for k in range(5):
+        row = jnp.sum(acc[8 * k : 8 * k + 8, :], axis=0, keepdims=True)
+        small[k : k + 1, :] = row[:, 0:C]
+        smallz[k : k + 1, 0 : 2 * Q] = row[:, C:]
+        smallz[k : k + 1, 2 * Q :] = jnp.zeros((1, C - 2 * Q), f32)
+    ngrad = jnp.sum(nsums[...], axis=0, keepdims=True)
+    for j in range(D // C):
+        smallz[5 + j : 6 + j, :] = ngrad[:, j * C : (j + 1) * C]
+    smallz[7:8, :] = jnp.zeros((1, C), f32)
+
+    def to_line(i):
+        return remote(smallz, smallz_in.at[i - 1], m1_s.at[i - 1], m1_r.at[i - 1], head=line(i))
+
+    for i in range(1, lines):
+        to_line(i).start()
+    held = 6
+    fold2.begin(tiles // S, tiles - tiles // S - held)
+    fold1.step(18)
+    fold1.step(19)
+    fold2.step(2)
+
+    rest = fold2.last(13, 6)
     for k in range(D // Q):
         t = mm(nt[k * Q : (k + 1) * Q, :], dcs[...])
         for j in range(2):
@@ -727,73 +853,18 @@
         return remote(later.at[at(other, DC)], sg_in, sa_s, sa_r, sample=other)
 
     state_pair().start()
-    fold2.step(2)
-    for k in range(5):
-        row = jnp.sum(acc[8 * k : 8 * k + 8, :], axis=0, keepdims=True)
-        small[k : k + 1, :] = row[:, 0:C]
-        smallz[k : k + 1, 0 : 2 * Q] = row[:, C:]
-        smallz[k : k + 1, 2 * Q :] = jnp.zeros((1, C - 2 * Q), f32)
     small[5:6, :] = jnp.sum(sums[0:8, :], axis=0, keepdims=True)
     small[6:7, :] = jnp.sum(sums[8:16, :], axis=0, keepdims=True)
     small[7:8, :] = jnp.zeros((1, C), f32)
     small[7:8, 0:Q] = jnp.sum(hsums[0:8, :], axis=0, keepdims=True)
     small[7:8, Q : 2 * Q] = jnp.sum(hsums[8:16, :], axis=0, keepdims=True)
-    ngrad = jnp.sum(nsums[...], axis=0, keepdims=True)
-    for j in range(D // C):
-        smallz[5 + j : 6 + j, :] = ngrad[:, j * C : (j + 1) * C]
-    smallz[7:8, :] = jnp.zeros((1, C), f32)
-
-    def to_line(i):
-        return remote(smallz, smallz_in.at[i - 1], m1_s.at[i - 1], m1_r.at[i - 1], head=line(i))
-
-    for i in range(1, lines):
-        to_line(i).start()
-    settle(2)
-    for i in range(1, seqs):
-        piece(2, i).start()
     fold2.step(3)
-
-    def gather_pieces(k):
-        for i in range(1, seqs):
-            piece(k, i).wait_recv()
-
-        def tile(j):
-            r = at(j, TILE)
-            v = gr[k, pl.ds(pl.multiple_of(pc * HG + ps * PR + j * TILE, TILE), TILE), :].astype(f32)
-            for i in range(1, seqs):
-                v = v + gr_pieces[k, i - 1, r, :].astype(f32)
-            gr_sum[k, r, :] = v.astype(bf16)
-            grads[k, pl.ds(pl.multiple_of(pc * HG + ps * PR + j * TILE, TILE), TILE), :] = v.astype(bf16)
-
-        loop(PR // TILE, tile)
-
-    def spread(k, i):
-        r = pl.ds(pl.multiple_of(pc * HG + ps * PR, PR), PR)
-        return remote(gr_sum.at[k], grads.at[k, r], gc_s.at[k, i - 1], gc_r.at[k, i - 1], seq=ring(i))
-
-    def hand(k, i):
-        q = lax.rem(ps + seqs - i, seqs)
-        r = pl.ds(pl.multiple_of(pc * HG + q * PR, PR), PR)
-        src = gr_sum.at[k] if i == 0 else grads.at[k, r]
-        return remote(src, grads.at[k, r], gd_s.at[k, i], gd_r.at[k, i], sample=other)
-
-    def send_out(k):
-        gather_pieces(k)
-        for i in range(1, seqs):
-            spread(k, i).start()
-        hand(k, 0).start()
-
-    def hand_on(k):
-        for i in range(1, seqs):
-            q = lax.rem(ps + seqs - i, seqs)
-            r = pl.ds(pl.multiple_of(pc * HG + q * PR, PR), PR)
-            remote(gr_sum.at[k], grads.at[k, r], gc_s.at[k, i - 1], gc_r.at[k, i - 1], seq=ring(i)).wait_recv()
-            hand(k, i).start()
-
-    send_out(0)
+    def outer3(i):
+        gr[2, at(i, 512), :] = mm(nt[at(i, 512), :], gate[...]).astype(bf16)
+
+    loop(D // 512, outer3)
+    pair(2).start()
     fold2.step(4)
-    send_out(1)
-    fold2.step(5)
     state_pair().wait_recv()
     later[keep_state] = later[keep_state] + sg_in[...]
 
@@ -802,7 +873,34 @@
 
     for i in range(1, seqs):
         state_piece(i).start()
+    fold2.step(5)
+    send_pieces(2)
     fold2.step(6)
+    hand_on(0)
+    fold2.step(7)
+    fold2.step(8)
+    for i in range(1, seqs):
+        state_piece(i).wait_recv()
+    v = later[keep_state, at(ps, SR), :]
+    for i in range(1, seqs):
+        v = v + sg_pieces[i - 1]
+    sg_wire[...] = v.astype(bf16)
+    sg_sum[...] = v
+    owner = (ps * SR) // own
+
+    def to_owner(i):
+        return remote(sg_wire, sg_line.at[i - 1], sz_s.at[i - 1], sz_r.at[i - 1], head=line(i))
+
+    for i in range(1, lines):
+
+        @pl.when(line(i) == owner)
+        def _():
+            to_owner(i).start()
+
+    fold2.begin(tiles - held, held)
+    fold2.step(9)
+    send_out(1)
+    fold2.step(10)
     total = smallz[...]
     for i in range(1, lines):
         to_line(i).wait_recv()
@@ -816,44 +914,21 @@
         return remote(small_two.at[1], small_in.at[i - 1], m2_s.at[i - 1], m2_r.at[i - 1], seq=ring(i))
 
     to_core().start()
-    fold2.step(7)
+    fold2.step(11)
+    send_out(2)
+    fold2.step(12)
     to_core().wait_recv()
     small_two[1] = small[...] + small_two[0]
     for i in range(1, seqs):
         to_peer(i).start()
-    hand_on(0)
-    fold2.step(8)
-    send_out(2)
-    fold2.step(9)
-
-    for i in range(1, seqs):
-        state_piece(i).wait_recv()
-    v = later[keep_state, at(ps, SR), :]
-    for i in range(1, seqs):
-        v = v + sg_pieces[i - 1]
-    sg_sum[0] = v
-    owner = (ps * SR) // own
-
-    def to_owner(i):
-        return remote(sg_sum.at[0], sg_line.at[i - 1], sz_s.at[i - 1], sz_r.at[i - 1], head=line(i))
-
-    for i in range(1, lines):
-
-        @pl.when(line(i) == owner)
-        def _():
-            to_owner(i).start()
-
-    fold2.step(10)
-    hand_on(1)
-    fold2.step(11)
-    fold2.step(12)
+    fold2.step(13)
     span = max(own // SR, 1)
 
     def place_row(q, core):
         return pl.ds(pl.multiple_of(core * own + lax.rem(q * SR, own), SR), SR)
 
     def state_out_to(i):
-        return remote(sg_sum.at[1], state_out.at[:, place_row(ps, pc)], sc_s.at[i - 1], sc_r.at[i - 1], seq=ring(i))
+        return remote(sg_sum, state_out.at[:, place_row(ps, pc)], sc_s.at[i - 1], sc_r.at[i - 1], seq=ring(i))
 
     def state_hand(j, src):
         q = ph * span + j
@@ -861,43 +936,54 @@
 
     @pl.when(ph == owner)
     def _():
-        t = sg_sum[0]
+        t = sg_sum[...]
         for i in range(1, lines):
             to_owner(i).wait_recv()
-            t = t + sg_line[i - 1]
-        sg_sum[1] = t
+            t = t + sg_line[i - 1].astype(f32)
+        sg_sum[...] = t
         state_out[:, place_row(ps, pc), :] = t
         for i in range(1, seqs):
             state_out_to(i).start()
 
-    fold2.step(13)
+    for move, i in rest[0]:
+        move(i)
+    hand_on(1)
+    complete(0)
+    for move, i in rest[1]:
+        move(i)
+    for move, i in rest[2]:
+        move(i)
     hand_on(2)
-    fold2.step(14)
-    fold2.step(15)
-    for j in range(span):
-        q = ph * span + j
-
-        @pl.when(q == ps)
-        def _():
-            state_hand(j, sg_sum.at[1]).start()
-
-        for i in range(1, seqs):
-
-            @pl.when(ring(seqs - i) == q)
-            def _():
-                remote(
-                    sg_sum.at[1], state_out.at[:, place_row(q, pc)], sc_s.at[i - 1], sc_r.at[i - 1], seq=ring(i)
-                ).wait_recv()
-                state_hand(j, state_out.at[:, place_row(q, pc)]).start()
-
-    fold2.step(16)
+    complete(1)
+    for move, i in rest[3]:
+        move(i)
     total = small_two[1]
     for i in range(1, seqs):
         to_peer(i).wait_recv()
         total = total + small_in[i - 1]
     small_out[...] = total
-    fold2.step(17)
-
+    for move, i in rest[4]:
+        move(i)
+    for move, i in rest[5]:
+        move(i)
+    for j in range(span):
+        q = ph * span + j
+
+        @pl.when(q == ps)
+        def _():
+            state_hand(j, sg_sum).start()
+
+        for i in range(1, seqs):
+
+            @pl.when(ring(seqs - i) == q)
+            def _():
+                remote(
+                    sg_sum, state_out.at[:, place_row(q, pc)], sc_s.at[i - 1], sc_r.at[i - 1], seq=ring(i)
+                ).wait_recv()
+                state_hand(j, state_out.at[:, place_row(q, pc)]).start()
+
+
+    complete(2)
     fold1.end()
     fold2.end()
     for r in relays2:
@@ -928,11 +1014,9 @@
         for i in range(1, seqs):
             piece(k, i).wait_send()
             spread(k, i).wait_send()
-        for i in range(seqs):
-            q = lax.rem(ps + seqs - i, seqs)
-            r = pl.ds(pl.multiple_of(other * HG + q * PR, PR), PR)
-            remote(gr_sum.at[k], grads.at[k, r], gd_s.at[k, i], gd_r.at[k, i], sample=other).wait()
+        result(k).wait()
     state_pair().wait_send()
+    share().wait_send()
     for i in range(1, seqs):
         state_piece(i).wait_send()
 
@@ -942,7 +1026,7 @@
 
     for j in range(span):
         q = ph * span + j
-        remote(sg_sum.at[1], state_out.at[:, place_row(q, other)], sd_s.at[j], sd_r.at[j], sample=other).wait()
+        remote(sg_sum, state_out.at[:, place_row(q, other)], sd_s.at[j], sd_r.at[j], sample=other).wait()
     to_core().wait_send()
     for i in range(1, seqs):
         to_peer(i).wait_send()
@@ -980,7 +1064,7 @@
         cvb[...] = small[4:5, :]
         gated_gain[...] = small[5:6, :]
         e = lane_heads(half // 64, half)
-        skip[...] = mm(jnp.broadcast_to(small[6:7, :], (8, half)), e, NT, HI)[0:1, 0:heads]
+        skip[...] = mm(jnp.broadcast_to(small[6:7, :], (8, half)), e.astype(f32), NT, HI)[0:1, 0:heads]
         sbias[...] = small[7:8, 0:heads]
         dlog[...] = small[7:8, Q : Q + heads]
         for h in range(lines):
@@ -1006,7 +1090,7 @@
     W = C + 2 * Q
     NCH = T // Q
     seqs, lines = lax.axis_size("seq"), lax.axis_size("head")
-    tiles = 16
+    tiles = 32
     H = D // 2
     PR = H // seqs
     SR = Q // seqs
@@ -1027,21 +1111,21 @@
         V((T, W), bf16), V((T, Q), f32), V((T, Q), f32), V((T, Q), f32), V((8, T), f32), V((8, T), f32),
         V((NCH, Q, C), f32), V((T, C), f32), V((T, C), f32), V((T, C), bf16), V((T, C), bf16),
         V((NCH, Q, C), f32),
-        V((T, 3 * Q), bf16), V((Q, C), f32), V((Q, C), f32), V((6, Q, C), f32),
+        V((T, 3 * Q), bf16), V((Q, C), bf16), V((Q, C), f32), V((6, Q, C), f32),
         V((8, Q), f32), V((Q, Q), f32), V((2, Q, Q), f32), V((8, T), f32), V((l1, 8, T), f32),
         V((S, Q, C), bf16), V((S, 8, Q), f32), V((seqs, S, Q, C), bf16), V((seqs, S, 8, Q), f32),
         V((S, Q, C), f32),
-        V((T, D), bf16), V((T, D), bf16), V((T, D), bf16), V((T, D), bf16),
-        V((3, D, C), bf16), V((3, H, C), bf16), V((3, n1, PR, C), bf16), V((3, PR, C), bf16),
-        V((D // C, Q, C), f32), V((n1, D // C, SR, C), f32), V((l1, D // C, SR, C), f32),
-        V((2, D // C, SR, C), f32),
+        V((T, D), bf16), V((T, D), bf16), V((T, D), bf16), V((T, D), bf16), V((T, D), bf16), V((T, D), bf16),
+        V((3, D, C), bf16), V((3, D, C), bf16), V((3, H, C), bf16), V((3, n1, PR, C), bf16), V((3, PR, C), bf16),
+        V((D // C, Q, C), f32), V((n1, D // C, SR, C), f32), V((l1, D // C, SR, C), bf16),
+        V((D // C, SR, C), bf16), V((D // C, SR, C), f32),
         V((40, W), f32), V((16, Q), f32), V((16, C), f32), V((8, D), f32), V((8, C), f32),
         V((l1, 8, C), f32), V((32, C), f32), V((2, 32, C), f32), V((n1, 32, C), f32), V((S, 8, W), f32), V((S, 8, W), f32),
-        dma((S + 6,)), dma((2, S)), dma((3, l1)), dma((3, l1)), dma((2, 2, S, n1)), dma((2, 2, S, n1)),
+        dma((S + 5,)), dma((2, S)), dma((2, lines)), dma((2, lines)), dma((2, 2, S, n1)), dma((2, 2, S, n1)),
         dma((S, l1)), dma((S, l1)), dma((S,)), dma((S,)),
-        dma((4, tiles)), dma((4, tiles)), dma((3,)), dma((3,)), dma((3, n1)), dma((3, n1)),
+        dma((2, tiles)), dma((3,)), dma((2, tiles)), dma((3,)), dma((3,)), dma((3,)), dma((3, n1)), dma((3, n1)),
         dma((3, n1)), dma((3, n1)), dma((3, seqs)), dma((3, seqs)),
-        dma, dma, dma((n1,)), dma((n1,)), dma((l1,)), dma((l1,)), dma((n1,)), dma((n1,)),
+        dma((3,)), dma, dma, dma((n1,)), dma((n1,)), dma((l1,)), dma((l1,)), dma((n1,)), dma((n1,)),
         dma((max(own // SR, 1),)), dma((max(own // SR, 1),)), dma((l1,)), dma((l1,)), dma((seqs,)), dma((seqs,)),
     ]
     outs, dnorm, grads, state_out, small = pl.pallas_call(
@@ -1052,7 +1136,7 @@
             jax.ShapeDtypeStruct((32, C), f32),
         ],
         in_specs=[hbm, hbm, vm, hbm, hbm, hbm, vm, hbm] + [vm] * 8,
-        out_specs=[vm] * 5,
+        out_specs=[hbm, hbm, hbm, vm, vm],
         scratch_shapes=scratch,
         name="block",
         compiler_params=pltpu.CompilerParams(
@@ -1062,7 +1146,7 @@
         x, cot, gain, gate_proj, value_proj, spt, step_proj.T, out_proj, conv_state, conv_state_bias,
         conv_value, conv_value_bias[None], step_bias[None], decay_log[None], skip_gain[None], gated_gain[None],
     )
-    steps = 8
+    steps = 4
 
     def whole(*shape):
         return pl.BlockSpec(shape, lambda i: (0,) * len(shape))

time: 199 us -> 159 us (0.80)
  Pallas kernels: 198 us -> 157 us
    pallas_call x1, Pallas kernels: 185 us -> 147 us  [per_device(): pl.pallas_call(functools.partial(block, (S, L, seqs, lines, tiles)), out_...]
    pallas_call x1, Pallas kernels: 12.1 us -> 10.1 us  [per_device(): pl.pallas_call(functools.partial(finish, lines), grid=(steps,), out_shape...]
where the time goes in v3:
time: 159 us; the launch traced here: 157 us
  Pallas kernels  157 us (99%)
    pallas_call x1, Pallas kernels, per_device(): pl.pallas_call(functools.partial(block, (S, L, seqs, lines, tiles)), out_...  147 us
    pallas_call x1, Pallas kernels, per_device(): pl.pallas_call(functools.partial(finish, lines), grid=(steps,), out_shape...  10.1 us

profile of v3, /device:TPU:0, one launch (start us, length us, event | category | flops | bytes accessed | tf_op | source)
XLA Modules:
  0.0 157.5 jit_solution(5372517101073987677)
XLA Ops:
  0.7 146.5 %block.1 = (bf16[1024,1024]{1,0:T(8,128)(2,1)}, bf16[1024,1024]{1,0:T(8,128)(2,1)}, bf16[3,1024,512]{2,1,0:T(8,128)(2,1)}, f32[2,64,512]{2,1,0:T(8,128)}, f32[32,512]{1,0:T(8,128)}) custom-call(bf16[1024,1024]{1,0:T(8,128)(2,1)} %bitcast.26, bf16[1024,1024]{1,0:T(8,128)(2,1)} %bitcast.28, f32[1,1024]{1,0:T(1,128)} %bitcast.32, bf16[1024,512]{1,0:T(8,128)(2,1)} %wg_in.1, ...), custom_call_target="tpu_custom_call" | custom-call | tf_op jit(solution)/shard_map/block/pallas_call | solution.py:1131
  147.2 10.1 %finish.1 = (bf16[1024,1024]{1,0:T(8,128)(2,1)}, f32[1024,1024]{1,0:T(8,128)}, f32[1024,512]{1,0:T(8,128)}, f32[1024,512]{1,0:T(8,128)}, f32[512,1024]{1,0:T(8,1...) custom-call(bf16[1024,1024]{1,0:T(8,128)(2,1)} %bitcast.27, ...), custom_call_target="tpu_custom_call" | custom-call | tf_op jit(solution)/shard_map/finish/pallas_call | solution.py:1158

commit v4 on v3

--- a/solution.py
+++ b/solution.py
@@ -43,7 +43,7 @@
 
 
 def at(i, n):
-    return pl.ds(pl.multiple_of(i * n, n), n)
+    return pl.ds(i * n if isinstance(i, int) else pl.multiple_of(i * n, n), n)
 
 
 def loop(count, body, each=1):
@@ -52,7 +52,11 @@
             body(i * each + j)
         return carry
 
-    lax.fori_loop(0, count // each, step, 0)
+    if count == each:
+        for i in range(count):
+            body(i)
+    else:
+        lax.fori_loop(0, count // each, step, 0)
 
 
 def iota(shape, axis):
@@ -147,18 +151,30 @@
             self.store(i).start()
 
     def step(self, j):
-        for ago, move in ((0, self.one), (2, self.two), (4, self.take)):
+        for ago, move in ((0, self.one), (4, self.two), (8, self.take)):
             if isinstance(j, int):
-                if 0 <= 2 * (j - ago) < self.tiles:
-                    loop(2, lambda q: move(2 * (j - ago) + q))
+                first, end = max(2 * j - ago, 0), min(2 * j - ago + 2, self.tiles)
+                if first < end:
+                    loop(end - first, lambda q: move(first + q))
             else:
-
-                @pl.when((j >= ago) & (2 * j < self.tiles + 2 * ago))
-                def _():
-                    loop(2, lambda q: move(2 * (j - ago) + q))
+                for q in range(2):
+                    i = 2 * j - ago + q
+
+                    @pl.when((i >= 0) & (i < self.tiles))
+                    def _():
+                        move(i)
+
+    def closely(self, j):
+        def tile(q):
+            self.one(2 * j + q)
+            self.two(2 * j - 3 + q)
+            if 2 * j >= 7:
+                self.take(2 * j - 7 + q)
+
+        loop(2, tile)
 
     def last(self, j, parts):
-        o, t, k = 2 * j + 2, 2 * j - 2, 2 * j - 6
+        o, t, k = 2 * j + 2, 2 * j - 1, 2 * j - 5
         moves = []
         while k < self.tiles:
             if o < self.tiles:
@@ -243,13 +259,13 @@
 def block(
     dims,
     x_in, cot_in, gain, wg_in, wv_in, spt, stp, wo_in, cs, csb, cv, cvb, sbias, dlog_in, skip, gg,
-    outs, dnorm, grads_out, state_out, small_out,
+    outs, dnorm, grads_out, state_result, small_result,
     xb, cot, wg, wv, wst, wo, tapb, taps, cw, hp, sk, xh,
     nt, inv, gate, pad, slope, act, dt, sg, cum, cum_t, dt_t, entry, ys, dy, gn, dg, later,
     dcs, e, st, work, off, tt, stats, stats_t, stats_in,
     fin, tot, slots, slots_t, chained,
-    part1, near1, far1, part2, near2, far2, grads,
-    gr, gr_in, gr_pieces, gr_sum, sg_in, sg_pieces, sg_line, sg_wire, sg_sum,
+    part1, near1, far1, part2, near2, far2, grads, state_out, small_out,
+    gr, gr_in, gr_pieces, gr_sum, sg_in, sg_pieces, sg_line, sg_wire, sg_sum, sg_done,
     acc, hsums, sums, nsums, smallz, smallz_in, small, small_two, small_in, nx, edge8,
     load, halo_sem, wt_s, wt_r, f_sem, b_sem, st_s, st_r, nx_s, nx_r,
     z1, y1, z2, y2, ga_s, ga_r, gb_s, gb_r, gc_s, gc_r, gd_s, gd_r,
@@ -425,8 +441,12 @@
             z = sg[at(c, Q), :] + hp[0:1, :]
             d = jax.nn.softplus(z)
             dt[at(c, Q), :] = d
-            sg[at(c, Q), :] = jax.nn.sigmoid(z)
-            run = mm(triangle(lambda i, j: i >= j), d * hp[1:2, :], precision=HI)
+            sg[at(c, Q), :] = sigmoid(z)
+            step = d * hp[1:2, :]
+            high, rest = halves(step)
+            middle, low = halves(step - high.astype(f32))
+            tri = triangle(lambda i, j: i >= j).astype(bf16)
+            run = mm(tri, high) + (mm(tri, middle) + mm(tri, low))
             cum[at(c, Q), :] = run
             cum_t[:, at(c, Q)] = run.T[0:8]
             dt_t[:, at(c, Q)] = d.T[0:8]
@@ -448,7 +468,8 @@
         loop(NC, chunk, NC)
         fin[s] = st[...].astype(bf16)
         relays.append(Relay(s, (fin, tot), (slots, slots_t), f_sem, seqs, 1))
-        relays[s].start()
+        if s == 0:
+            relays[s].start()
 
     def weights_of(h, here, causal):
         gap = cum[here, h : h + 1] - cum_t[h : h + 1, here]
@@ -468,6 +489,7 @@
             ys[here, p * Q : (p + 1) * Q] = y
 
     loop(NC, within)
+    relays[1].start()
 
     def stat(s, i):
         part = pl.ds(s * L, L)
@@ -481,32 +503,36 @@
         relays[s].gather(chained, e)
         off[...] = jnp.zeros_like(off)
 
-        def across(k):
+        def across(k, lane=0):
             c = s * NC + k
             here = at(c, Q)
             si = entry[c] + row_of(jnp.exp(off[0:1, :]), e[...]) * chained[s]
             entry[c] = si
             run = cum[here, :]
-            work[0] = mm2(jnp.exp(run), e[...]) * mm2(act[here, C + Q :], si)
+            work[lane] = mm2(jnp.exp(run), e[...]) * mm2(act[here, C + Q :], si)
             off[...] += jnp.broadcast_to(run[Q - 1 : Q, :], (8, Q))
 
             def tile(r):
                 rows = at(c * (Q // TILE) + r, TILE)
-                y = ys[rows, :] + work[0, at(r, TILE), :]
+                y = ys[rows, :] + work[lane, at(r, TILE), :]
                 ys[rows, :] = y
                 m = y + sk[...] * act[rows, 0:C].astype(f32)
                 g = gate[rows, :].astype(f32)
                 gated = m * (g * sigmoid(g))
                 a = gated * gated
                 b = dy[rows, :] * gg[...] * gated
-                stats[0, at(r, TILE), :] = sum(a[:, p * Q : (p + 1) * Q] for p in range(C // Q))
-                stats[1, at(r, TILE), :] = sum(b[:, p * Q : (p + 1) * Q] for p in range(C // Q))
+                stats[2 * lane, at(r, TILE), :] = sum(a[:, p * Q : (p + 1) * Q] for p in range(C // Q))
+                stats[2 * lane + 1, at(r, TILE), :] = sum(b[:, p * Q : (p + 1) * Q] for p in range(C // Q))
 
             loop(Q // TILE, tile, 4)
             for j in range(2):
-                stats_t[j : j + 1, here] = jnp.sum(stats[j].T, axis=0, keepdims=True)
-
-        loop(NC, across)
+                stats_t[j : j + 1, here] = jnp.sum(stats[2 * lane + j].T, axis=0, keepdims=True)
+
+        def pair_of(k):
+            across(2 * k, 0)
+            across(2 * k + 1, 1)
+
+        loop(NC // 2, pair_of)
         for i in range(1, lines):
             stat(s, i).start()
 
@@ -555,9 +581,9 @@
                 sums[8:16, :] += fold8(dmix * x)
 
             loop(Q // TILE, tile, 4)
+            part1[here, :] = mm(gn[here, :], wo[...]).astype(bf16)
+            fold1.begin(c * (tiles * Q // T), tiles * Q // T)
         loop(NC, gate_back)
-        part1[s * L : (s + 1) * L, :] = mm(gn[s * L : (s + 1) * L, :], wo[...]).astype(bf16)
-        fold1.begin(s * (tiles // S), tiles // S)
 
     def rewind(s):
         st[...] = jnp.zeros_like(st)
@@ -577,9 +603,9 @@
     gating(0)
     for r in relays:
         r.finish()
-    gating(1)
     rewind(0)
     fold1.step(0)
+    gating(1)
     rewind(1)
     fold1.step(1)
 
@@ -592,21 +618,20 @@
     for i in range(D // C):
         gr[0, i * C : (i + 1) * C, :] = mm(gn[...], cot[:, i * C : (i + 1) * C], TN).astype(bf16)
     pair(0).start()
-    fold1.step(2)
 
     def turn(i):
         rows = at(i, 256)
         nt[:, rows] = (xb[rows, :].astype(f32) * inv[rows, 0:1] * gain[...]).astype(bf16).T
 
     loop(T // 256, turn)
-    fold1.step(3)
+    fold1.step(2)
 
     def outer2(i):
         gr[1, at(i, 512), :] = mm(nt[at(i, 512), :], dg[...]).astype(bf16)
 
     loop(D // 512, outer2)
     pair(1).start()
-    fold1.step(4)
+    fold1.step(3)
 
     hsums[...] = jnp.zeros_like(hsums)
     acc[...] = jnp.zeros_like(acc)
@@ -688,7 +713,7 @@
 
     send_pieces(0)
     send_pieces(1)
-    fold1.step(5)
+    fold1.step(4)
     for s in range(S):
         relays2[s].gather(chained, e)
         off[...] = jnp.zeros_like(off)
@@ -758,7 +783,7 @@
             dcs[here, 2 * Q :] = draw.astype(bf16)
             hsums[0:8, :] += fold8(draw)
             hsums[8:16, :] += fold8(rate * dlog * d)
-            fold1.step((6 if s == 0 else 12) + k)
+            fold1.step((5 if s == 0 else 11) + k)
 
         loop(NC, state_back)
         edge8[s] = slope[s * L : s * L + 8, :]
@@ -789,11 +814,9 @@
                 acc[32:40, lanes] += fold8(d)
 
         loop(LT - 1, lambda r: conv_back(r, False))
-        if s == 0:
-            fold1.step(10)
-        else:
+        fold1.step(9 if s == 0 else 15)
+        if s > 0:
             fold1.step(16)
-            fold1.step(17)
             fold2.step(0)
 
         @pl.when(ps < seqs - 1)
@@ -802,6 +825,7 @@
 
         conv_back(LT - 1, True)
         if s > 0:
+            fold1.step(17)
             fold2.step(1)
 
         def into(k):
@@ -814,7 +838,7 @@
         loop(L // 256, into)
         if s == 0:
             fold2.begin(0, tiles // S)
-            fold1.step(11)
+            fold1.step(10)
             send_out(0)
 
     for k in range(5):
@@ -832,17 +856,22 @@
 
     for i in range(1, lines):
         to_line(i).start()
-    held = 6
+    held = 4
     fold2.begin(tiles // S, tiles - tiles // S - held)
+    fold2.step(2)
     fold1.step(18)
     fold1.step(19)
-    fold2.step(2)
 
     rest = fold2.last(13, 6)
     for k in range(D // Q):
         t = mm(nt[k * Q : (k + 1) * Q, :], dcs[...])
         for j in range(2):
-            later[j * DC + k * Q // C, :, k * Q % C : k * Q % C + Q] = t[:, j * Q : (j + 1) * Q].T
+            turned = t[:, j * Q : (j + 1) * Q].T
+            for g in range(own // 8):
+                for h in range(lines):
+                    later[j * DC + k * Q // C, 8 * (g * lines + h) : 8 * (g * lines + h) + 8, k * Q % C : k * Q % C + Q] = (
+                        turned[h * own + 8 * g : h * own + 8 * g + 8]
+                    )
         row = 8 + 8 * (k * Q // C)
         small[row : row + 8, k * Q % C : k * Q % C + Q] = t[:, 2 * Q :].T[0:8]
 
@@ -864,7 +893,9 @@
 
     loop(D // 512, outer3)
     pair(2).start()
-    fold2.step(4)
+    fold2.two(4)
+    fold2.take(0)
+    fold2.closely(4)
     state_pair().wait_recv()
     later[keep_state] = later[keep_state] + sg_in[...]
 
@@ -873,34 +904,40 @@
 
     for i in range(1, seqs):
         state_piece(i).start()
-    fold2.step(5)
+    fold2.closely(5)
     send_pieces(2)
-    fold2.step(6)
+    fold2.closely(6)
     hand_on(0)
-    fold2.step(7)
-    fold2.step(8)
+    fold2.closely(7)
+    fold2.closely(8)
     for i in range(1, seqs):
         state_piece(i).wait_recv()
     v = later[keep_state, at(ps, SR), :]
     for i in range(1, seqs):
         v = v + sg_pieces[i - 1]
-    sg_wire[...] = v.astype(bf16)
     sg_sum[...] = v
-    owner = (ps * SR) // own
+    blocks = SR // 8
+
+    def block_of(h):
+        return lax.rem(h + lines * blocks - lax.rem(ps * blocks, lines), lines)
+
+    for k in range(blocks):
+        sg_wire[k] = v[:, 8 * k : 8 * k + 8, :].astype(bf16)
+    owns = block_of(ph) < blocks
 
     def to_owner(i):
-        return remote(sg_wire, sg_line.at[i - 1], sz_s.at[i - 1], sz_r.at[i - 1], head=line(i))
+        return remote(sg_wire.at[lax.rem(block_of(line(i)), blocks)], sg_line.at[i - 1], sz_s.at[i - 1], sz_r.at[i - 1], head=line(i))
 
     for i in range(1, lines):
 
-        @pl.when(line(i) == owner)
+        @pl.when(block_of(line(i)) < blocks)
         def _():
             to_owner(i).start()
 
     fold2.begin(tiles - held, held)
-    fold2.step(9)
+    fold2.closely(9)
     send_out(1)
-    fold2.step(10)
+    fold2.closely(10)
     total = smallz[...]
     for i in range(1, lines):
         to_line(i).wait_recv()
@@ -914,34 +951,38 @@
         return remote(small_two.at[1], small_in.at[i - 1], m2_s.at[i - 1], m2_r.at[i - 1], seq=ring(i))
 
     to_core().start()
-    fold2.step(11)
+    fold2.closely(11)
     send_out(2)
-    fold2.step(12)
+    fold2.closely(12)
     to_core().wait_recv()
     small_two[1] = small[...] + small_two[0]
     for i in range(1, seqs):
         to_peer(i).start()
-    fold2.step(13)
-    span = max(own // SR, 1)
-
-    def place_row(q, core):
-        return pl.ds(pl.multiple_of(core * own + lax.rem(q * SR, own), SR), SR)
+    fold2.closely(13)
+    span = own // 8
+
+    def place_row(g, core):
+        return pl.ds(pl.multiple_of(core * own + g * 8, 8), 8)
+
+    my_row = lax.div(ps * blocks, lines)
 
     def state_out_to(i):
-        return remote(sg_sum, state_out.at[:, place_row(ps, pc)], sc_s.at[i - 1], sc_r.at[i - 1], seq=ring(i))
-
-    def state_hand(j, src):
-        q = ph * span + j
-        return remote(src, state_out.at[:, place_row(q, pc)], sd_s.at[j], sd_r.at[j], sample=other)
-
-    @pl.when(ph == owner)
+        return remote(sg_done, state_out.at[:, place_row(my_row, pc)], sc_s.at[i - 1], sc_r.at[i - 1], seq=ring(i))
+
+    def holder(g):
+        return lax.div(g * lines + ph, blocks)
+
+    def state_hand(g, src):
+        return remote(src, state_out.at[:, place_row(g, pc)], sd_s.at[g], sd_r.at[g], sample=other)
+
+    @pl.when(owns)
     def _():
-        t = sg_sum[...]
+        t = sg_sum[:, pl.ds(pl.multiple_of(8 * block_of(ph), 8), 8), :]
         for i in range(1, lines):
             to_owner(i).wait_recv()
             t = t + sg_line[i - 1].astype(f32)
-        sg_sum[...] = t
-        state_out[:, place_row(ps, pc), :] = t
+        sg_done[...] = t
+        state_out[:, place_row(my_row, pc), :] = t
         for i in range(1, seqs):
             state_out_to(i).start()
 
@@ -962,27 +1003,31 @@
         to_peer(i).wait_recv()
         total = total + small_in[i - 1]
     small_out[...] = total
+    small_copy = pltpu.make_async_copy(small_out, small_result, out_sem.at[3])
+    small_copy.start()
     for move, i in rest[4]:
         move(i)
     for move, i in rest[5]:
         move(i)
-    for j in range(span):
-        q = ph * span + j
-
-        @pl.when(q == ps)
+    for g in range(span):
+
+        @pl.when(holder(g) == ps)
         def _():
-            state_hand(j, sg_sum).start()
+            state_hand(g, sg_done).start()
 
         for i in range(1, seqs):
 
-            @pl.when(ring(seqs - i) == q)
+            @pl.when(ring(seqs - i) == holder(g))
             def _():
                 remote(
-                    sg_sum, state_out.at[:, place_row(q, pc)], sc_s.at[i - 1], sc_r.at[i - 1], seq=ring(i)
+                    sg_done, state_out.at[:, place_row(g, pc)], sc_s.at[i - 1], sc_r.at[i - 1], seq=ring(i)
                 ).wait_recv()
-                state_hand(j, state_out.at[:, place_row(q, pc)]).start()
-
-
+                state_hand(g, state_out.at[:, place_row(g, pc)]).start()
+
+    for g in range(span):
+        remote(sg_done, state_out.at[:, place_row(g, other)], sd_s.at[g], sd_r.at[g], sample=other).wait()
+    state_copy = pltpu.make_async_copy(state_out, state_result, out_sem.at[4])
+    state_copy.start()
     complete(2)
     fold1.end()
     fold2.end()
@@ -995,7 +1040,7 @@
             stat(s, i).wait_send()
         to_line(i).wait_send()
 
-        @pl.when(line(i) == owner)
+        @pl.when(block_of(line(i)) < blocks)
         def _():
             to_owner(i).wait_send()
 
@@ -1015,18 +1060,17 @@
             piece(k, i).wait_send()
             spread(k, i).wait_send()
         result(k).wait()
+    small_copy.wait()
+    state_copy.wait()
     state_pair().wait_send()
     share().wait_send()
     for i in range(1, seqs):
         state_piece(i).wait_send()
 
-        @pl.when(ph == owner)
+        @pl.when(owns)
         def _():
             state_out_to(i).wait_send()
 
-    for j in range(span):
-        q = ph * span + j
-        remote(sg_sum, state_out.at[:, place_row(q, other)], sd_s.at[j], sd_r.at[j], sample=other).wait()
     to_core().wait_send()
     for i in range(1, seqs):
         to_peer(i).wait_send()
@@ -1112,21 +1156,21 @@
         V((NCH, Q, C), f32), V((T, C), f32), V((T, C), f32), V((T, C), bf16), V((T, C), bf16),
         V((NCH, Q, C), f32),
         V((T, 3 * Q), bf16), V((Q, C), bf16), V((Q, C), f32), V((6, Q, C), f32),
-        V((8, Q), f32), V((Q, Q), f32), V((2, Q, Q), f32), V((8, T), f32), V((l1, 8, T), f32),
+        V((8, Q), f32), V((Q, Q), f32), V((4, Q, Q), f32), V((8, T), f32), V((l1, 8, T), f32),
         V((S, Q, C), bf16), V((S, 8, Q), f32), V((seqs, S, Q, C), bf16), V((seqs, S, 8, Q), f32),
         V((S, Q, C), f32),
         V((T, D), bf16), V((T, D), bf16), V((T, D), bf16), V((T, D), bf16), V((T, D), bf16), V((T, D), bf16),
-        V((3, D, C), bf16), V((3, D, C), bf16), V((3, H, C), bf16), V((3, n1, PR, C), bf16), V((3, PR, C), bf16),
-        V((D // C, Q, C), f32), V((n1, D // C, SR, C), f32), V((l1, D // C, SR, C), bf16),
-        V((D // C, SR, C), bf16), V((D // C, SR, C), f32),
+        V((3, D, C), bf16), V((D // C, 2 * own, C), f32), V((32, C), f32), V((3, D, C), bf16), V((3, H, C), bf16), V((3, n1, PR, C), bf16), V((3, PR, C), bf16),
+        V((D // C, Q, C), f32), V((n1, D // C, SR, C), f32), V((l1, D // C, 8, C), bf16),
+        V((SR // 8, D // C, 8, C), bf16), V((D // C, SR, C), f32), V((D // C, 8, C), f32),
         V((40, W), f32), V((16, Q), f32), V((16, C), f32), V((8, D), f32), V((8, C), f32),
         V((l1, 8, C), f32), V((32, C), f32), V((2, 32, C), f32), V((n1, 32, C), f32), V((S, 8, W), f32), V((S, 8, W), f32),
         dma((S + 5,)), dma((2, S)), dma((2, lines)), dma((2, lines)), dma((2, 2, S, n1)), dma((2, 2, S, n1)),
         dma((S, l1)), dma((S, l1)), dma((S,)), dma((S,)),
         dma((2, tiles)), dma((3,)), dma((2, tiles)), dma((3,)), dma((3,)), dma((3,)), dma((3, n1)), dma((3, n1)),
         dma((3, n1)), dma((3, n1)), dma((3, seqs)), dma((3, seqs)),
-        dma((3,)), dma, dma, dma((n1,)), dma((n1,)), dma((l1,)), dma((l1,)), dma((n1,)), dma((n1,)),
-        dma((max(own // SR, 1),)), dma((max(own // SR, 1),)), dma((l1,)), dma((l1,)), dma((seqs,)), dma((seqs,)),
+        dma((5,)), dma, dma, dma((n1,)), dma((n1,)), dma((l1,)), dma((l1,)), dma((n1,)), dma((n1,)),
+        dma((own // 8,)), dma((own // 8,)), dma((l1,)), dma((l1,)), dma((seqs,)), dma((seqs,)),
     ]
     outs, dnorm, grads, state_out, small = pl.pallas_call(
         functools.partial(block, (S, L, seqs, lines, tiles)),
@@ -1136,7 +1180,7 @@
             jax.ShapeDtypeStruct((32, C), f32),
         ],
         in_specs=[hbm, hbm, vm, hbm, hbm, hbm, vm, hbm] + [vm] * 8,
-        out_specs=[hbm, hbm, hbm, vm, vm],
+        out_specs=[hbm] * 5,
         scratch_shapes=scratch,
         name="block",
         compiler_params=pltpu.CompilerParams(
@@ -1146,7 +1190,7 @@
         x, cot, gain, gate_proj, value_proj, spt, step_proj.T, out_proj, conv_state, conv_state_bias,
         conv_value, conv_value_bias[None], step_bias[None], decay_log[None], skip_gain[None], gated_gain[None],
     )
-    steps = 4
+    steps = 2
 
     def whole(*shape):
         return pl.BlockSpec(shape, lambda i: (0,) * len(shape))

time: 159 us -> 156 us (0.981)
  the two profiles are of different devices: /device:TPU:0 before, /device:TPU:5 now
where the time goes in v4:
time: 156 us
  Pallas kernels  155 us (99%)
    pallas_call x1, Pallas kernels, per_device(): pl.pallas_call(functools.partial(block, (S, L, seqs, lines, tiles)), out_...  146 us
    pallas_call x1, Pallas kernels, per_device(): pl.pallas_call(functools.partial(finish, lines), grid=(steps,), out_shape...  9.01 us

profile of v4, /device:TPU:5, one launch (start us, length us, event | category | flops | bytes accessed | tf_op | source)
XLA Modules:
  0.0 155.8 jit_solution(596056853577872026)
XLA Ops:
  0.7 146.0 %block.1 = (bf16[1024,1024]{1,0:T(8,128)(2,1)}, bf16[1024,1024]{1,0:T(8,128)(2,1)}, bf16[3,1024,512]{2,1,0:T(8,128)(2,1)}, f32[2,64,512]{2,1,0:T(8,128)}, f32[32,512]{1,0:T(8,128)}) custom-call(bf16[1024,1024]{1,0:T(8,128)(2,1)} %bitcast.26, bf16[1024,1024]{1,0:T(8,128)(2,1)} %bitcast.28, f32[1,1024]{1,0:T(1,128)} %bitcast.32, bf16[1024,512]{1,0:T(8,128)(2,1)} %wg_in.1, ...), custom_call_target="tpu_custom_call" | custom-call | tf_op jit(solution)/shard_map/block/pallas_call | solution.py:1175
  146.7 9.0 %finish.1 = (bf16[1024,1024]{1,0:T(8,128)(2,1)}, f32[1024,1024]{1,0:T(8,128)}, f32[1024,512]{1,0:T(8,128)}, f32[1024,512]{1,0:T(8,128)}, f32[512,1024]{1,0:T(8,1...) custom-call(bf16[1024,1024]{1,0:T(8,128)(2,1)} %bitcast.27, ...), custom_call_target="tpu_custom_call" | custom-call | tf_op jit(solution)/shard_map/finish/pallas_call | solution.py:1202

commit v5 on v4

--- a/solution.py
+++ b/solution.py
@@ -582,7 +582,15 @@
 
             loop(Q // TILE, tile, 4)
             part1[here, :] = mm(gn[here, :], wo[...]).astype(bf16)
-            fold1.begin(c * (tiles * Q // T), tiles * Q // T)
+            few = tiles * Q // T
+            if s == 0:
+
+                @pl.when(k == 0)
+                def _():
+                    fold1.begin(0, few)
+
+            else:
+                fold1.begin(c * few, few)
         loop(NC, gate_back)
 
     def rewind(s):
@@ -599,8 +607,9 @@
         relays2.append(Relay(s, (fin, tot), (slots, slots_t), b_sem, seqs, -1))
         relays2[s].start()
 
+    gating(0)
     cross(1)
-    gating(0)
+    fold1.begin(tiles * Q // T, tiles // S - tiles * Q // T)
     for r in relays:
         r.finish()
     rewind(0)

time: 156 us -> 159 us (1.019)
  Pallas kernels: 155 us -> 157 us
    pallas_call x1, Pallas kernels: 146 us -> 148 us  [per_device(): pl.pallas_call(functools.partial(block, (S, L, seqs, lines, tiles)), out_...]
where the time goes in v5:
time: 159 us; the launch traced here: 158 us
  Pallas kernels  157 us (99%)
    pallas_call x1, Pallas kernels, per_device(): pl.pallas_call(functools.partial(block, (S, L, seqs, lines, tiles)), out_...  148 us
    pallas_call x1, Pallas kernels, per_device(): pl.pallas_call(functools.partial(finish, lines), grid=(steps,), out_shape...  9.01 us

profile of v5, /device:TPU:5, one launch (start us, length us, event | category | flops | bytes accessed | tf_op | source)
XLA Modules:
  0.0 158.3 jit_solution(16023274776679135813)
XLA Ops:
  0.7 148.4 %block.1 = (bf16[1024,1024]{1,0:T(8,128)(2,1)}, bf16[1024,1024]{1,0:T(8,128)(2,1)}, bf16[3,1024,512]{2,1,0:T(8,128)(2,1)}, f32[2,64,512]{2,1,0:T(8,128)}, f32[32,512]{1,0:T(8,128)}) custom-call(bf16[1024,1024]{1,0:T(8,128)(2,1)} %bitcast.26, bf16[1024,1024]{1,0:T(8,128)(2,1)} %bitcast.28, f32[1,1024]{1,0:T(1,128)} %bitcast.32, bf16[1024,512]{1,0:T(8,128)(2,1)} %wg_in.1, ...), custom_call_target="tpu_custom_call" | custom-call | tf_op jit(solution)/shard_map/block/pallas_call | solution.py:1184
  149.1 9.0 %finish.1 = (bf16[1024,1024]{1,0:T(8,128)(2,1)}, f32[1024,1024]{1,0:T(8,128)}, f32[1024,512]{1,0:T(8,128)}, f32[1024,512]{1,0:T(8,128)}, f32[512,1024]{1,0:T(8,1...) custom-call(bf16[1024,1024]{1,0:T(8,128)(2,1)} %bitcast.27, ...), custom_call_target="tpu_custom_call" | custom-call | tf_op jit(solution)/shard_map/finish/pallas_call | solution.py:1211
